TPU v7x, 128 devices: a whole 4x4x4 slice. The times are simulated.
128 devices in a mesh: dom: 32 (over y, x, core), dim: 4 (over z).
Axes of the slice: x: 4, y: 4, z: 4, core: 2. Of those that a mesh axis runs over, the one named last changes fastest.
Arguments:
- particles: float32 [256, 1024], P('dom', 'dim'), may hold values from -5 to 5
- data_rows: bfloat16 [256, 16, 1024], P('dom', None, 'dim'), may hold values from -0.375 to 0.375
- labels: int32 [256, 16], P('dom'), may hold values from 0 to 1
Outputs:
- updates: float32 [2, 256, 1024], P(None, 'dom', 'dim')
All inputs are finite; a program needn't handle non-finite values.
Results may differ from a plain program's by a relative error of at most 0.0003.
Values may be sent and summed in bfloat16 or wider, within the bound.
No kernel may reach another device: no remote copies, remote signals or barrier semaphores. Data moves between devices by JAX's collectives and lax.ppermute only.
A program may use at most 64 MiB of HBM per device.

v0:
```python
from functools import partial

import jax
import jax.numpy as jnp
import numpy as np
from jax import lax
from jax.experimental import pallas as pl
from jax.experimental.pallas import tpu as pltpu
from jax.sharding import Mesh
from jax.sharding import PartitionSpec as P


AXES = ("y", "x", "c", "z")
NEWTON = 2
prior_precision = 0.05
like_weight = 4.0
move_size = 0.5

f32 = jnp.float32
bf16 = jnp.bfloat16
WIDE = 1024
MANY = 256
HALF = 128
DATA = 16
SLICE = 256
scale = 1.0 * WIDE
cross = 4.0 / (scale * scale)

MASKS = (1, 3)
ORDERS = ("xyz", "yzx", "zxy")
SPOT = {"y": 0, "x": 1, "z": 3}
THIRDS = (96, 0, 48)
FIRSTS = (6, 0, 3)
ROWS = (512, 768, 768)
STARTS = (0, 512, 1280)
CHUNK = 256


def places():
    return np.ndindex(4, 4, 2, 4)


def spot(at):
    return int(np.ravel_multi_index(at, (4, 4, 2, 4)))


def pairs(axis):
    out = []
    for at in places():
        to = list(at)
        to[SPOT[axis]] ^= MASKS[1 - at[2]]
        out.append((spot(at), spot(to)))
    return out


def cubes():
    groups = {}
    for at in places():
        mask = MASKS[at[2]]
        key = (at[2],) + tuple(min(at[d], at[d] ^ mask) for d in (0, 1, 3))
        groups.setdefault(key, []).append(spot(at))
    return list(groups.values())


def swap_cores(x):
    return lax.ppermute(x, "c", [(0, 1), (1, 0)])


def gathered(copies):
    cube = lax.all_to_all(copies, AXES, 0, 0, axis_index_groups=cubes(), tiled=True)
    parts = [cube[:, k : k + 48] for k in THIRDS]

    def sent(parts, step):
        out = []
        for part, order in zip(parts, ORDERS):
            out.append(lax.ppermute(part, AXES, pairs(order[step])))
        return out

    near = [jnp.concatenate(both, axis=0) for both in zip(parts, sent(parts, 0))]
    aside = sent(near, 1)
    far = sent(near, 2)
    last = sent(aside, 2)
    return list(zip(near, aside, far, last))


def two(v):
    high = v.astype(bf16)
    return high, (v - high.astype(f32)).astype(bf16)


def nn(a, b):
    return lax.dot_general(a, b, (((1,), (0,)), ((), ())), preferred_element_type=f32)


def tn(a, b):
    return lax.dot_general(a, b, (((0,), (0,)), ((), ())), preferred_element_type=f32)


def stacked(a, b):
    left = jnp.concatenate([a[0], a[1], a[0]], axis=1)
    right = jnp.concatenate([b[0], b[0], b[1]], axis=0)
    return nn(left, right)


def own_place():
    y, x = lax.axis_index("y"), lax.axis_index("x")
    shift = lax.axis_index("c")
    return ((y >> shift) & 1) * 4 + ((x >> shift) & 1)


def slice_at(k):
    core, z = lax.axis_index("c"), lax.axis_index("z")
    seen = (0, 3, 1, 2)
    turned = (z ^ (z >> 1)) & 1
    return jnp.where(core == 0, k ^ (z & 2), jnp.where(turned == 1, seen[k ^ 2], seen[k]))


def cols(k):
    return slice(k * SLICE, (k + 1) * SLICE)


def span(color):
    return slice(STARTS[color], STARTS[color] + ROWS[color])


def half_of(core):
    return pl.ds(pl.multiple_of(core * HALF, HALF), HALF)


def in_order(core, own, other, axis):
    pair = jnp.where(core == 0, own, other), jnp.where(core == 0, other, own)
    return jnp.concatenate(pair, axis=axis)


def prepare_kernel(x_far, rows_far, labels_far, out_ref, x_ref, rows_ref, labels_ref, done):
    copies = [
        pltpu.make_async_copy(far, near, done.at[k])
        for k, (far, near) in enumerate(
            ((x_far, x_ref), (rows_far, rows_ref), (labels_far, labels_ref))
        )
    ]
    for copy in copies:
        copy.start()
    for copy in copies:
        copy.wait()
    sign = (2 * labels_ref[...] - 1).astype(f32).T
    pieces = [rows_ref[p].astype(f32) * sign[:, p : p + 1] for p in range(8)]
    whole = jnp.concatenate([p.astype(bf16) for p in pieces] + list(two(x_ref[...])), axis=0)
    for k in range(8):
        out_ref[k] = whole


def land(color, refs, rows_ref, hot_ref, tail_ref=None):
    count = ROWS[color] // 16
    order = ORDERS[color]
    for k in range(4):
        slot = pl.ds(pl.multiple_of(slice_at(k) * SLICE, SLICE), SLICE)
        for at in range(16):
            step = {"z": k >> 1, "y": at >> 3, "x": (at >> 1) & 1}
            unit = step[order[0]] * 8 + ((at >> 2) & 1) * 4 + (at & 1) * 2 + (k & 1)
            ref = refs[step[order[2]] * 2 + step[order[1]]]
            rows_ref[at * count : (at + 1) * count, slot] = ref[unit, :count, :]
            if tail_ref is not None:
                high, low = ref[unit, 32:40, :], ref[unit, 40:48, :]
                tail_ref[at * 8 : at * 8 + 8, slot] = high.astype(f32) + low.astype(f32)
    row = lax.broadcasted_iota(jnp.int32, (ROWS[color], HALF), 0)
    place = (row * 43691) >> 21 if count == 48 else row >> 5
    owner = place * 8 + FIRSTS[color] + ((row - place * count) >> 4)
    hot = owner == lax.broadcasted_iota(jnp.int32, (ROWS[color], HALF), 1)
    hot = jnp.where(hot, 1.0, 0.0).astype(bf16)
    hot_ref[:, :HALF] = hot
    hot_ref[:, HALF:] = hot


def gradient(rows_ref, hot_ref, both, curve_ref):
    weights = []
    for at in range(0, rows_ref.shape[0], CHUNK):
        part = pl.ds(at, CHUNK)
        logit = nn(rows_ref[part, :], both)
        hot = hot_ref[part, :HALF].astype(f32)
        logit = jnp.sum((logit[:, :HALF] + logit[:, HALF:]) * hot, axis=1, keepdims=True)
        prob = 1.0 / (1.0 + jnp.exp(logit))
        curve_ref[part, :] = jnp.broadcast_to(like_weight * prob * (1.0 - prob), (CHUNK, HALF))
        weights.append(jnp.concatenate(two(like_weight * prob * hot), axis=1))
    return tn(rows_ref[...], jnp.concatenate(weights, axis=0))


def folded(total):
    return total[:, :HALF] + total[:, HALF:]


def land_kernel(a, b, c, d, rows_ref, hot_ref, x_ref, tail_ref):
    land(0, (a, b, c, d), rows_ref, hot_ref, tail_ref)
    for k in range(4):
        x_ref[cols(k), :] = tail_ref[:, cols(k)].T


def grad_kernel(rows_ref, hot_ref, x_ref, grad_ref, curve_ref):
    x = x_ref[...]
    both = jnp.concatenate(two(x), axis=1)
    grad_ref[...] = folded(gradient(rows_ref, hot_ref, both, curve_ref)) - (
        prior_precision + 2.0 / scale
    ) * x


def land_grad_kernel(color, a, b, c, d, x_ref, before_ref, rows_ref, hot_ref, grad_ref, curve_ref):
    land(color, (a, b, c, d), rows_ref, hot_ref)
    both = jnp.concatenate(two(x_ref[...]), axis=1)
    grad_ref[...] = before_ref[...] + folded(gradient(rows_ref, hot_ref, both, curve_ref))


def factors(own_ref, other_ref):
    mu0, mu1, mu2 = (own_ref[k : k + 1, :1] for k in range(3))
    mu3 = own_ref[3:4, :1] + other_ref[3:4, :1]
    alpha = mu0 / mu1
    left = mu0 - 2.0 * alpha * mu1 + alpha * alpha * mu2
    grown = 1.0 + left / mu0
    gamma = left / (grown * grown * mu1 - 2.0 * grown * alpha * mu2 + alpha * alpha * mu3)
    return alpha + gamma * grown, -gamma * alpha


def own_update(on_drift, on_image, drift_ref, image_ref, turn_ref):
    mine = half_of(lax.axis_index("c"))
    own = pl.ds(pl.multiple_of(lax.axis_index("z") * SLICE, SLICE), SLICE)
    turn_ref[...] = (on_drift * drift_ref[own, mine] + on_image * image_ref[own, mine]).T
    return turn_ref[pl.ds(pl.multiple_of(own_place() * 8, 8), 8), :]


def next_kernel(
    r0, r1, r2, h0, h1, h2, x_ref, drift_ref, image_ref, own_ref, other_ref,
    grad_ref, c0, c1, c2, new_ref, out_ref, turn_ref,
):
    on_drift, on_image = factors(own_ref, other_ref)
    out_ref[...] = own_update(on_drift, on_image, drift_ref, image_ref, turn_ref)
    update = on_drift * drift_ref[...] + on_image * image_ref[...]
    new_ref[...] = x_ref[...] + move_size * update
    x = new_ref[:, half_of(lax.axis_index("c"))]
    both = jnp.concatenate(two(x), axis=1)
    total = gradient(r0, h0, both, c0) + gradient(r1, h1, both, c1) + gradient(r2, h2, both, c2)
    grad_ref[...] = folded(total) - (prior_precision + 2.0 / scale) * x


def last_kernel(
    drift_ref, image_ref, own_ref, other_ref, before_ref, out_ref, turn_ref
):
    on_drift, on_image = factors(own_ref, other_ref)
    out_ref[0] = before_ref[...]
    out_ref[1] = own_update(on_drift, on_image, drift_ref, image_ref, turn_ref)


def similarity(x, kernel_ref):
    high, low = two(x)
    gram = tn(high, high) + (tn(high, low) + tn(low, high))
    shape = (MANY, MANY)
    same = lax.broadcasted_iota(jnp.int32, shape, 0) == lax.broadcasted_iota(jnp.int32, shape, 1)
    diag = jnp.where(same, gram, 0.0)
    squares = jnp.sum(diag, axis=1, keepdims=True) + jnp.sum(diag, axis=0, keepdims=True)
    kernel_ref[...] = jnp.exp((2.0 * gram - squares) / scale)


def start_kernel(own_ref, other_ref, kernel_ref, x_ref):
    x = in_order(lax.axis_index("c"), own_ref[...], other_ref[...], 1)
    x_ref[...] = x
    similarity(x, kernel_ref)


def again_kernel(x_ref, kernel_ref):
    similarity(x_ref[...], kernel_ref)


def first_kernel(
    r0, r1, r2, h0, h1, h2, c0, c1, c2, x_ref, kernel_ref, own_ref, other_ref,
    drift_ref, image_ref, factor_ref, weighted_ref,
):
    core = lax.axis_index("c")
    mine = half_of(core)
    x = x_ref[...]
    grad = in_order(core, own_ref[...], other_ref[...], 1)
    drift = stacked(two(grad), two(kernel_ref[...]))
    total = jnp.sum(kernel_ref[...], axis=0, keepdims=True)
    drift = (drift + (2.0 / scale) * total * x) / MANY
    drift_ref[...] = drift
    drift_two = two(drift)
    kernel_own = kernel_ref[mine, :]
    square = kernel_own * kernel_own
    square_two = jnp.concatenate(two(square), axis=0)
    thirds = (r0, r1, r2)
    for color, (rows_ref, hot_ref, curve_ref) in enumerate(zip(thirds, (h0, h1, h2), (c0, c1, c2))):
        for at in range(0, ROWS[color], CHUNK):
            part, to = pl.ds(at, CHUNK), pl.ds(STARTS[color] + at, CHUNK)
            curve = curve_ref[part, :]
            factor = nn(hot_ref[part, :], square_two) * jnp.concatenate([curve, curve], axis=1)
            factor_ref[to, :] = factor
            rows = rows_ref[part, :]
            high, low = two((nn(rows, drift_two[0]) + nn(rows, drift_two[1])) * factor)
            weighted_ref[0, to, :] = high
            weighted_ref[1, to, :] = low
    x_own = x_ref[:, mine]
    x_two = two(x_own)
    along = stacked(two(x_own.T), drift_two)
    q = square * (jnp.sum(x * drift, axis=0, keepdims=True) - along)
    pull = x * jnp.sum(q, axis=0, keepdims=True) - stacked(x_two, two(q))
    image_ref[...] = (
        sum(
            tn(rows_ref[...], weighted_ref[k, span(color), :])
            for color, rows_ref in enumerate(thirds)
            for k in range(2)
        )
        + (prior_precision * jnp.sum(square, axis=0, keepdims=True) * drift + cross * pull)
    ) / MANY


def second_kernel(
    r0, r1, r2, x_ref, kernel_ref, factor_ref, drift_ref, own_ref, other_ref,
    image_ref, sums_ref,
):
    mine = half_of(lax.axis_index("c"))
    image = own_ref[...] + other_ref[...]
    image_ref[...] = image
    drift = drift_ref[...]
    image_two = two(image)
    rounded = image_two[0]
    wide = rounded.astype(f32)
    total = jnp.zeros((1, MANY), f32)
    for color, rows_ref in enumerate((r0, r1, r2)):
        for at in range(0, ROWS[color], CHUNK):
            projected = nn(rows_ref[pl.ds(at, CHUNK), :], rounded)
            factor = factor_ref[pl.ds(STARTS[color] + at, CHUNK), :]
            total += jnp.sum(projected * projected * factor, axis=0, keepdims=True)
    fit = jnp.sum(image * wide, axis=0, keepdims=True)
    fit = fit / jnp.maximum(jnp.sum(wide * wide, axis=0, keepdims=True), 1e-30)
    total *= fit * fit
    square = kernel_ref[mine, :] * kernel_ref[mine, :]
    along = stacked(two(x_ref[:, mine].T), image_two)
    gap = jnp.sum(x_ref[...] * image, axis=0, keepdims=True) - along
    total += cross * jnp.sum(square * gap * gap, axis=0, keepdims=True)
    length = jnp.sum(image * image, axis=0, keepdims=True)
    total += prior_precision * jnp.sum(square, axis=0, keepdims=True) * length
    figures = (
        jnp.sum(drift * drift, axis=0, keepdims=True),
        jnp.sum(drift * image, axis=0, keepdims=True),
        length,
        total / MANY,
    )
    for at, value in enumerate(figures):
        sums_ref[at : at + 1, :] = jnp.broadcast_to(
            jnp.sum(value, axis=1, keepdims=True), (1, HALF)
        )
    sums_ref[4:, :] = jnp.zeros((4, HALF), f32)


def call(kernel, outs, *args, scratch=(), far=False):
    whole = pl.BlockSpec(memory_space=pltpu.VMEM)
    return pl.pallas_call(
        kernel,
        out_shape=[jax.ShapeDtypeStruct(s, t) for s, t in outs],
        in_specs=[pl.BlockSpec(memory_space=pltpu.HBM) if far else whole] * len(args),
        out_specs=[whole] * len(outs),
        scratch_shapes=scratch,
        compiler_params=pltpu.CompilerParams(vmem_limit_bytes=(60 if far else 24) * 1024 * 1024),
    )(*args)


def per_device(particles, data_rows, labels):
    (copies,) = call(
        prepare_kernel,
        [((8, 8 * DATA + 16, SLICE), bf16)],
        particles, data_rows, labels,
        scratch=[
            pltpu.VMEM((8, SLICE), f32),
            pltpu.VMEM((8, DATA, SLICE), bf16),
            pltpu.VMEM((8, DATA), jnp.int32),
            pltpu.SemaphoreType.DMA((3,)),
        ],
        far=True,
    )
    pieces = gathered(copies)
    count = HALF * DATA
    tall = ((count, MANY), f32)
    square = ((MANY, MANY), f32)
    long = ((WIDE, MANY), f32)
    half = ((WIDE, HALF), f32)
    turn = [pltpu.VMEM((HALF, SLICE), f32)]
    rows_of = [((r, WIDE), bf16) for r in ROWS]
    hot_of = [((r, MANY), bf16) for r in ROWS]
    curve_of = [((r, HALF), f32) for r in ROWS]
    rows, hot, curve = [None] * 3, [None] * 3, [None] * 3
    rows[0], hot[0], x_own = call(
        land_kernel, [rows_of[0], hot_of[0], half], *pieces[0],
        scratch=[pltpu.VMEM((HALF, WIDE), f32)],
    )
    x_other = swap_cores(x_own)
    grad, curve[0] = call(grad_kernel, [half, curve_of[0]], rows[0], hot[0], x_own)
    kernel, x = call(start_kernel, [square, long], x_own, x_other)
    for color in (1, 2):
        rows[color], hot[color], grad, curve[color] = call(
            partial(land_grad_kernel, color),
            [rows_of[color], hot_of[color], half, curve_of[color]],
            *pieces[color], x_own, grad,
        )
    for newton_step in range(NEWTON):
        if newton_step > 0:
            grad, *curve, x, update = call(
                next_kernel, [half, *curve_of, long, ((8, SLICE), f32)],
                *rows, *hot, x, drift, image, sums, sums_other, scratch=turn,
            )
        grad_other = swap_cores(grad)
        if newton_step > 0:
            (kernel,) = call(again_kernel, [square], x)
        drift, image_own, factor = call(
            first_kernel,
            [long, long, tall],
            *rows, *hot, *curve, x, kernel, grad, grad_other,
            scratch=[pltpu.VMEM((2, count, MANY), bf16)],
        )
        image, sums = call(
            second_kernel,
            [long, ((8, HALF), f32)],
            *rows, x, kernel, factor, drift, image_own, swap_cores(image_own),
        )
        sums_other = swap_cores(sums)
    (updates,) = call(
        last_kernel, [((NEWTON, 8, SLICE), f32)],
        drift, image, sums, sums_other, update, scratch=turn,
    )
    return updates


def solution(mesh):
    torus = Mesh(mesh.devices.reshape(4, 4, 2, mesh.shape["dim"]), AXES)
    groups = ("y", "x", "c")
    in_specs = (P(groups, "z"), P(groups, None, "z"), P(groups, None))
    out_specs = P(None, groups, "z")

    return jax.shard_map(
        per_device, mesh=torus, in_specs=in_specs, out_specs=out_specs, check_vma=False
    )
```

profile of v0, /device:TPU:1, one launch (start us, length us, event | category | flops | bytes accessed | tf_op | source)
XLA Modules:
  0.0 87.2 jit_solution(433181566268838121)
XLA Ops:
  0.0 1.9 %shard_map.37 = bf16[8,144,256]{2,1,0:T(8,128)(2,1)} custom-call(f32[8,256]{1,0:T(8,128)} %x_far.1, bf16[8,16,256]{2,1,0:T(8,128)(2,1)} %rows_far.1, s32[8,16]{1,0:T(8,128)} %labels_far.1), custom_call_target="tpu_custom_call" | custom-call | tf_op jit(solution)/shard_map/pallas_call | solution.py:354
  1.9 21.7 %all_to_all.5 = bf16[8,144,256]{2,1,0:T(8,128)(2,1)S(1)} all-to-all(bf16[8,144,256]{2,1,0:T(8,128)(2,1)} %shard_map.37), channel_id=1, replica_groups={{0,1,8,9,32,33,40,41},{2,3,10,11,34,35,42,43},{4,7,28,31,100,103,124,12..., dimensions={0} | all-to-all | bytes 1179648 | tf_op jit(solution)/shard_map/all_to_all | solution.py:70
  23.7 0.1 collective-permute-start
  23.7 0.1 collective-permute-start.4
  23.8 0.1 collective-permute-start.8
  23.9 4.3 %collective-permute-done = bf16[8,48,256]{2,1,0:T(8,128)(2,1)S(1)} collective-permute-done((bf16[8,48,256]{2,1,0:T(8,128)(2,1)S(1)}, bf16[8,48,256]{2,1,0:T(8,128)(2,1)S(1)}, u32[]{:S(2)}, u32[]{:S(2)}) %collective-permute-start) | collective-permute-done | bytes 196640 | tf_op jit(solution)/shard_map/ppermute | solution.py:76
  28.3 0.1 collective-permute-start.2
  28.4 0.1 collective-permute-start.1
  28.5 0.0 collective-permute-done.4
  28.5 1.4 %collective-permute-start.5 = (bf16[16,48,256]{2,1,0:T(8,128)(2,1)S(1)}, bf16[16,48,256]{2,1,0:T(8,128)(2,1)S(1)}, u32[]{:S(2)}, u32[]{:S(2)}) collective-permute-start(bf16[16,48,256]{2,1,0:T(8,128)(2,1)S(1)} %pad_maximum_fusion.1.a), channel_id=1, source_target_pairs={{0,3},{1,2},{2,1},{3,0},{4,5},{5,4},{6,7},{7,6},{8,11},{9,10},{10,... | collective-permute-start | bytes 1179656 | tf_op jit(solution)/shard_map/ppermute | solution.py:76
  30.0 0.0 collective-permute-done.8
  30.0 0.3 collective-permute-start.9
  30.3 5.1 %collective-permute-done.1.b = bf16[16,48,256]{2,1,0:T(8,128)(2,1)S(1)} collective-permute-done((bf16[16,48,256]{2,1,0:T(8,128)(2,1)S(1)}, bf16[16,48,256]{2,1,0:T(8,128)(2,1)S(1)}, u32[]{:S(2)}, u32[]{:S(2)}) %collective-permute-start.1) | collective-permute-done | bytes 393248 | tf_op jit(solution)/shard_map/ppermute | solution.py:76
  35.4 1.4 %collective-permute-start.3 = (bf16[16,48,256]{2,1,0:T(8,128)(2,1)S(1)}, bf16[16,48,256]{2,1,0:T(8,128)(2,1)S(1)}, u32[]{:S(2)}, u32[]{:S(2)}) collective-permute-start(bf16[16,48,256]{2,1,0:T(8,128)(2,1)S(1)} %collective-permute-done.1.b), channel_id=1, source_target_pairs={{0,3},{1,2},{2,1},{3,0},{4,5},{5,4},{6,7},{7,6},{8,11},{9,10},{10,... | collective-permute-start | bytes 1179656 | tf_op jit(solution)/shard_map/ppermute | solution.py:76
  36.8 0.0 collective-permute-start.6
  36.8 2.4 %collective-permute-done.5.b = bf16[16,48,256]{2,1,0:T(8,128)(2,1)S(1)} collective-permute-done((bf16[16,48,256]{2,1,0:T(8,128)(2,1)S(1)}, bf16[16,48,256]{2,1,0:T(8,128)(2,1)S(1)}, u32[]{:S(2)}, u32[]{:S(2)}) %collective-permute-start.5) | collective-permute-done | bytes 393248 | tf_op jit(solution)/shard_map/ppermute | solution.py:76
  39.2 0.3 collective-permute-start.7
  39.5 0.0 collective-permute-done.2.c
  39.5 0.4 collective-permute-start.10
  39.9 0.0 collective-permute-done.9.b
  39.9 1.1 %collective-permute-start.11 = (bf16[16,48,256]{2,1,0:T(8,128)(2,1)S(1)}, bf16[16,48,256]{2,1,0:T(8,128)(2,1)S(1)}, u32[]{:S(2)}, u32[]{:S(2)}) collective-permute-start(bf16[16,48,256]{2,1,0:T(8,128)(2,1)S(1)} %collective-permute-done.9.b), channel_id=1, source_target_pairs={{0,96},{1,97},{2,98},{3,99},{4,36},{5,37},{6,38},{7,39},{8,104},{9... | collective-permute-start | bytes 1179656 | tf_op jit(solution)/shard_map/ppermute | solution.py:76
  41.0 2.7 %collective-permute-done.3.d = bf16[16,48,256]{2,1,0:T(8,128)(2,1)S(1)} collective-permute-done((bf16[16,48,256]{2,1,0:T(8,128)(2,1)S(1)}, bf16[16,48,256]{2,1,0:T(8,128)(2,1)S(1)}, u32[]{:S(2)}, u32[]{:S(2)}) %collective-permute-start.3) | collective-permute-done | bytes 393248 | tf_op jit(solution)/shard_map/ppermute | solution.py:76
  43.7 0.5 shard_map.38
  44.2 1.2 %collective-permute-start.12 = (f32[1024,128]{1,0:T(8,128)S(1)}, f32[1024,128]{1,0:T(8,128)S(1)}, u32[]{:S(2)}, u32[]{:S(2)}) collective-permute-start(f32[1024,128]{1,0:T(8,128)S(1)} %get-tuple-element.37.x_ref.own_ref), channel_id=1, source_target_pairs={{0,4},{4,0},{1,5},{5,1},{2,6},{6,2},{3,7},{7,3},{8,12},{12,8},{9,1... | collective-permute-start | bytes 1572872 | tf_op jit(solution)/shard_map/ppermute | solution.py:66
  45.5 1.0 %shard_map.39 = (f32[1024,128]{1,0:T(8,128)S(1)}, f32[512,128]{1,0:T(8,128)S(1)}) custom-call(bf16[512,1024]{1,0:T(8,128)(2,1)S(1)} %get-tuple-element.36.rows_ref.r0, bf16[512,256]{1,0:T(8,128)(2,1)S(1)} %get-tuple-element.38.hot_ref.h0, f32[1024,128]{1,0:T(8,128)S(1)} %get-tuple-element.37.x_ref.own_ref), custom_call_target="tpu_custom_call" | custom-call | tf_op jit(solution)/shard_map/pallas_call | solution.py:354
  46.5 0.0 collective-permute-done.6.c
  46.5 1.4 %collective-permute-done.7.d = bf16[16,48,256]{2,1,0:T(8,128)(2,1)S(1)} collective-permute-done((bf16[16,48,256]{2,1,0:T(8,128)(2,1)S(1)}, bf16[16,48,256]{2,1,0:T(8,128)(2,1)S(1)}, u32[]{:S(2)}, u32[]{:S(2)}) %collective-permute-start.7) | collective-permute-done | bytes 393248 | tf_op jit(solution)/shard_map/ppermute | solution.py:76
  47.9 1.4 %shard_map.40 = (bf16[768,1024]{1,0:T(8,128)(2,1)S(1)}, bf16[768,256]{1,0:T(8,128)(2,1)S(1)}, f32[1024,128]{1,0:T(8,128)S(1)}, f32[768,128]{1,0:T(8,128)S(1)}) custom-call(bf16[16,48,256]{2,1,0:T(8,128)(2,1)S(1)} %pad_maximum_fusion.1.a, bf16[16,48,256]{2,1,0:T(8,128)(2,1)S(1)} %collective-permute-done.5.b, ...), custom_call_target="tpu_custom_call" | custom-call | tf_op jit(solution)/shard_map/pallas_call | solution.py:354
  49.3 0.0 collective-permute-done.10.c
  49.4 1.3 %collective-permute-done.11.d = bf16[16,48,256]{2,1,0:T(8,128)(2,1)S(1)} collective-permute-done((bf16[16,48,256]{2,1,0:T(8,128)(2,1)S(1)}, bf16[16,48,256]{2,1,0:T(8,128)(2,1)S(1)}, u32[]{:S(2)}, u32[]{:S(2)}) %collective-permute-start.11) | collective-permute-done | bytes 393248 | tf_op jit(solution)/shard_map/ppermute | solution.py:76
  50.7 1.4 %shard_map.41 = (bf16[768,1024]{1,0:T(8,128)(2,1)S(1)}, bf16[768,256]{1,0:T(8,128)(2,1)S(1)}, f32[1024,128]{1,0:T(8,128)S(1)}, f32[768,128]{1,0:T(8,128)S(1)}) custom-call(bf16[16,48,256]{2,1,0:T(8,128)(2,1)S(1)} %pad_maximum_fusion.2.a, bf16[16,48,256]{2,1,0:T(8,128)(2,1)S(1)} %collective-permute-done.9.b, ...), custom_call_target="tpu_custom_call" | custom-call | tf_op jit(solution)/shard_map/pallas_call | solution.py:354
  52.1 2.8 %collective-permute-start.13 = (f32[1024,128]{1,0:T(8,128)S(1)}, f32[1024,128]{1,0:T(8,128)S(1)}, u32[]{:S(2)}, u32[]{:S(2)}) collective-permute-start(f32[1024,128]{1,0:T(8,128)S(1)} %get-tuple-element.50.own_ref), channel_id=1, source_target_pairs={{0,4},{4,0},{1,5},{5,1},{2,6},{6,2},{3,7},{7,3},{8,12},{12,8},{9,1... | collective-permute-start | bytes 1572872 | tf_op jit(solution)/shard_map/ppermute | solution.py:66
  54.9 0.0 collective-permute-done.12.other_ref
  54.9 0.8 shard_map.42
  55.7 0.8 collective-permute-done.13.other_ref
  56.5 6.4 %shard_map.43 = (f32[1024,256]{1,0:T(8,128)S(1)}, f32[1024,256]{1,0:T(8,128)S(1)}, f32[2048,256]{1,0:T(8,128)S(1)}) custom-call(bf16[512,1024]{1,0:T(8,128)(2,1)S(1)} %get-tuple-element.36.rows_ref.r0, bf16[768,1024]{1,0:T(8,128)(2,1)S(1)} %get-tuple-element.40.r1, bf16[768,1024]{1,0:T(8,128)(2,1)S(1)} %get-tuple-element.42.r2, ...), custom_call_target="tpu_custom_call" | custom-call | tf_op jit(solution)/shard_map/pallas_call | solution.py:354
  62.9 0.4 collective-permute-start.14
  63.3 2.3 %collective-permute-done.14.other_ref = f32[1024,256]{1,0:T(8,128)S(1)} collective-permute-done((f32[1024,256]{1,0:T(8,128)S(1)}, f32[1024,256]{1,0:T(8,128)S(1)}, u32[]{:S(2)}, u32[]{:S(2)}) %collective-permute-start.14) | collective-permute-done | bytes 1048608 | tf_op jit(solution)/shard_map/ppermute | solution.py:66
  65.6 1.8 %shard_map.44 = (f32[1024,256]{1,0:T(8,128)S(1)}, f32[8,128]{1,0:T(8,128)S(1)}) custom-call(bf16[512,1024]{1,0:T(8,128)(2,1)S(1)} %get-tuple-element.36.rows_ref.r0, bf16[768,1024]{1,0:T(8,128)(2,1)S(1)} %get-tuple-element.40.r1, bf16[768,1024]{1,0:T(8,128)(2,1)S(1)} %get-tuple-element.42.r2, f32[1024,256]{1,0:T(8,128)S(1)} %get-tuple-element.45.x_ref, ...), custom_call_target="tpu_custom_call" | custom-call | tf_op jit(solution)/shard_map/pallas_call | solution.py:354
  67.5 0.3 collective-permute-start.15
  67.8 0.8 collective-permute-done.15.other_ref
  68.6 3.2 %shard_map.45 = (f32[1024,128]{1,0:T(8,128)S(1)}, f32[512,128]{1,0:T(8,128)S(1)}, f32[768,128]{1,0:T(8,128)S(1)}, f32[768,128]{1,0:T(8,128)S(1)}, f32[1024,256]{1,0:T(8,128)S(1)}, /*index=5*/f32[8,256]{1,0:T(8,128)S(1)}) custom-call(bf16[512,1024]{1,0:T(8,128)(2,1)S(1)} %get-tuple-element.36.rows_ref.r0, bf16[768,1024]{1,0:T(8,128)(2,1)S(1)} %get-tuple-element.40.r1, ...), custom_call_target="tpu_custom_call" | custom-call | tf_op jit(solution)/shard_map/pallas_call | solution.py:354
  71.8 0.6 collective-permute-start.16
  72.4 0.7 shard_map.46.kernel_ref
  73.1 0.9 %collective-permute-done.16.other_ref = f32[1024,128]{1,0:T(8,128)S(1)} collective-permute-done((f32[1024,128]{1,0:T(8,128)S(1)}, f32[1024,128]{1,0:T(8,128)S(1)}, u32[]{:S(2)}, u32[]{:S(2)}) %collective-permute-start.16) | collective-permute-done | bytes 524320 | tf_op jit(solution)/shard_map/ppermute | solution.py:66
  74.1 6.5 %shard_map.47 = (f32[1024,256]{1,0:T(8,128)S(1)}, f32[1024,256]{1,0:T(8,128)S(1)}, f32[2048,256]{1,0:T(8,128)S(1)}) custom-call(bf16[512,1024]{1,0:T(8,128)(2,1)S(1)} %get-tuple-element.36.rows_ref.r0, bf16[768,1024]{1,0:T(8,128)(2,1)S(1)} %get-tuple-element.40.r1, bf16[768,1024]{1,0:T(8,128)(2,1)S(1)} %get-tuple-element.42.r2, ...), custom_call_target="tpu_custom_call" | custom-call | tf_op jit(solution)/shard_map/pallas_call | solution.py:354
  80.5 0.3 collective-permute-start.17
  80.9 2.4 %collective-permute-done.17.other_ref = f32[1024,256]{1,0:T(8,128)S(1)} collective-permute-done((f32[1024,256]{1,0:T(8,128)S(1)}, f32[1024,256]{1,0:T(8,128)S(1)}, u32[]{:S(2)}, u32[]{:S(2)}) %collective-permute-start.17) | collective-permute-done | bytes 1048608 | tf_op jit(solution)/shard_map/ppermute | solution.py:66
  83.3 1.9 %shard_map.48 = (f32[1024,256]{1,0:T(8,128)S(1)}, f32[8,128]{1,0:T(8,128)S(1)}) custom-call(bf16[512,1024]{1,0:T(8,128)(2,1)S(1)} %get-tuple-element.36.rows_ref.r0, bf16[768,1024]{1,0:T(8,128)(2,1)S(1)} %get-tuple-element.40.r1, bf16[768,1024]{1,0:T(8,128)(2,1)S(1)} %get-tuple-element.42.r2, f32[1024,256]{1,0:T(8,128)S(1)} %get-tuple-element.59.x_ref, ...), custom_call_target="tpu_custom_call" | custom-call | tf_op jit(solution)/shard_map/pallas_call | solution.py:354
  85.2 0.2 collective-permute-start.18
  85.5 0.9 %collective-permute-done.18.other_ref = f32[8,128]{1,0:T(8,128)S(1)} collective-permute-done((f32[8,128]{1,0:T(8,128)S(1)}, f32[8,128]{1,0:T(8,128)S(1)}, u32[]{:S(2)}, u32[]{:S(2)}) %collective-permute-start.18) | collective-permute-done | bytes 4128 | tf_op jit(solution)/shard_map/ppermute | solution.py:66
  86.4 0.8 shard_map.49
  (4 shorter events, 0.1 us)
Async XLA Ops:
  23.7 4.6 %collective-permute-start = (bf16[8,48,256]{2,1,0:T(8,128)(2,1)S(1)}, bf16[8,48,256]{2,1,0:T(8,128)(2,1)S(1)}, u32[]{:S(2)}, u32[]{:S(2)}) collective-permute-start(bf16[8,48,256]{2,1,0:T(8,128)(2,1)S(1)} %get-tuple-element.69), channel_id=1, source_target_pairs={{0,24},{1,25},{2,26},{3,27},{4,12},{5,13},{6,14},{7,15},{8,16},{9,... | collective-permute-start | bytes 589832 | tf_op jit(solution)/shard_map/ppermute | solution.py:76
  23.7 4.7 %collective-permute-start.4 = (bf16[8,48,256]{2,1,0:T(8,128)(2,1)S(1)}, bf16[8,48,256]{2,1,0:T(8,128)(2,1)S(1)}, u32[]{:S(2)}, u32[]{:S(2)}) collective-permute-start(bf16[8,48,256]{2,1,0:T(8,128)(2,1)S(1)} %get-tuple-element.68), channel_id=1, source_target_pairs={{0,96},{1,97},{2,98},{3,99},{4,36},{5,37},{6,38},{7,39},{8,104},{9... | collective-permute-start | bytes 589832 | tf_op jit(solution)/shard_map/ppermute | solution.py:76
  23.8 6.1 %collective-permute-start.8 = (bf16[8,48,256]{2,1,0:T(8,128)(2,1)S(1)}, bf16[8,48,256]{2,1,0:T(8,128)(2,1)S(1)}, u32[]{:S(2)}, u32[]{:S(2)}) collective-permute-start(bf16[8,48,256]{2,1,0:T(8,128)(2,1)S(1)} %get-tuple-element.67), channel_id=1, source_target_pairs={{0,3},{1,2},{2,1},{3,0},{4,5},{5,4},{6,7},{7,6},{8,11},{9,10},{10,... | collective-permute-start | bytes 589832 | tf_op jit(solution)/shard_map/ppermute | solution.py:76
  28.3 11.2 %collective-permute-start.2 = (bf16[16,48,256]{2,1,0:T(8,128)(2,1)S(1)}, bf16[16,48,256]{2,1,0:T(8,128)(2,1)S(1)}, u32[]{:S(2)}, u32[]{:S(2)}) collective-permute-start(bf16[16,48,256]{2,1,0:T(8,128)(2,1)S(1)} %pad_maximum_fusion.a), channel_id=1, source_target_pairs={{0,3},{1,2},{2,1},{3,0},{4,5},{5,4},{6,7},{7,6},{8,11},{9,10},{10,... | collective-permute-start | bytes 1179656 | tf_op jit(solution)/shard_map/ppermute | solution.py:76
  28.4 7.0 %collective-permute-start.1 = (bf16[16,48,256]{2,1,0:T(8,128)(2,1)S(1)}, bf16[16,48,256]{2,1,0:T(8,128)(2,1)S(1)}, u32[]{:S(2)}, u32[]{:S(2)}) collective-permute-start(bf16[16,48,256]{2,1,0:T(8,128)(2,1)S(1)} %pad_maximum_fusion.a), channel_id=1, source_target_pairs={{0,96},{1,97},{2,98},{3,99},{4,36},{5,37},{6,38},{7,39},{8,104},{9... | collective-permute-start | bytes 1179656 | tf_op jit(solution)/shard_map/ppermute | solution.py:76
  28.5 10.7 %collective-permute-start.5 = (bf16[16,48,256]{2,1,0:T(8,128)(2,1)S(1)}, bf16[16,48,256]{2,1,0:T(8,128)(2,1)S(1)}, u32[]{:S(2)}, u32[]{:S(2)}) collective-permute-start(bf16[16,48,256]{2,1,0:T(8,128)(2,1)S(1)} %pad_maximum_fusion.1.a), channel_id=1, source_target_pairs={{0,3},{1,2},{2,1},{3,0},{4,5},{5,4},{6,7},{7,6},{8,11},{9,10},{10,... | collective-permute-start | bytes 1179656 | tf_op jit(solution)/shard_map/ppermute | solution.py:76
  30.0 9.9 %collective-permute-start.9 = (bf16[16,48,256]{2,1,0:T(8,128)(2,1)S(1)}, bf16[16,48,256]{2,1,0:T(8,128)(2,1)S(1)}, u32[]{:S(2)}, u32[]{:S(2)}) collective-permute-start(bf16[16,48,256]{2,1,0:T(8,128)(2,1)S(1)} %pad_maximum_fusion.2.a), channel_id=1, source_target_pairs={{0,24},{1,25},{2,26},{3,27},{4,12},{5,13},{6,14},{7,15},{8,16},{9,... | collective-permute-start | bytes 1179656 | tf_op jit(solution)/shard_map/ppermute | solution.py:76
  35.4 8.3 %collective-permute-start.3 = (bf16[16,48,256]{2,1,0:T(8,128)(2,1)S(1)}, bf16[16,48,256]{2,1,0:T(8,128)(2,1)S(1)}, u32[]{:S(2)}, u32[]{:S(2)}) collective-permute-start(bf16[16,48,256]{2,1,0:T(8,128)(2,1)S(1)} %collective-permute-done.1.b), channel_id=1, source_target_pairs={{0,3},{1,2},{2,1},{3,0},{4,5},{5,4},{6,7},{7,6},{8,11},{9,10},{10,... | collective-permute-start | bytes 1179656 | tf_op jit(solution)/shard_map/ppermute | solution.py:76
  36.8 9.7 %collective-permute-start.6 = (bf16[16,48,256]{2,1,0:T(8,128)(2,1)S(1)}, bf16[16,48,256]{2,1,0:T(8,128)(2,1)S(1)}, u32[]{:S(2)}, u32[]{:S(2)}) collective-permute-start(bf16[16,48,256]{2,1,0:T(8,128)(2,1)S(1)} %pad_maximum_fusion.1.a), channel_id=1, source_target_pairs={{0,24},{1,25},{2,26},{3,27},{4,12},{5,13},{6,14},{7,15},{8,16},{9,... | collective-permute-start | bytes 1179656 | tf_op jit(solution)/shard_map/ppermute | solution.py:76
  39.2 8.7 %collective-permute-start.7 = (bf16[16,48,256]{2,1,0:T(8,128)(2,1)S(1)}, bf16[16,48,256]{2,1,0:T(8,128)(2,1)S(1)}, u32[]{:S(2)}, u32[]{:S(2)}) collective-permute-start(bf16[16,48,256]{2,1,0:T(8,128)(2,1)S(1)} %collective-permute-done.5.b), channel_id=1, source_target_pairs={{0,24},{1,25},{2,26},{3,27},{4,12},{5,13},{6,14},{7,15},{8,16},{9,... | collective-permute-start | bytes 1179656 | tf_op jit(solution)/shard_map/ppermute | solution.py:76
  39.5 9.8 %collective-permute-start.10 = (bf16[16,48,256]{2,1,0:T(8,128)(2,1)S(1)}, bf16[16,48,256]{2,1,0:T(8,128)(2,1)S(1)}, u32[]{:S(2)}, u32[]{:S(2)}) collective-permute-start(bf16[16,48,256]{2,1,0:T(8,128)(2,1)S(1)} %pad_maximum_fusion.2.a), channel_id=1, source_target_pairs={{0,96},{1,97},{2,98},{3,99},{4,36},{5,37},{6,38},{7,39},{8,104},{9... | collective-permute-start | bytes 1179656 | tf_op jit(solution)/shard_map/ppermute | solution.py:76
  39.9 10.8 %collective-permute-start.11 = (bf16[16,48,256]{2,1,0:T(8,128)(2,1)S(1)}, bf16[16,48,256]{2,1,0:T(8,128)(2,1)S(1)}, u32[]{:S(2)}, u32[]{:S(2)}) collective-permute-start(bf16[16,48,256]{2,1,0:T(8,128)(2,1)S(1)} %collective-permute-done.9.b), channel_id=1, source_target_pairs={{0,96},{1,97},{2,98},{3,99},{4,36},{5,37},{6,38},{7,39},{8,104},{9... | collective-permute-start | bytes 1179656 | tf_op jit(solution)/shard_map/ppermute | solution.py:76
  44.2 10.7 %collective-permute-start.12 = (f32[1024,128]{1,0:T(8,128)S(1)}, f32[1024,128]{1,0:T(8,128)S(1)}, u32[]{:S(2)}, u32[]{:S(2)}) collective-permute-start(f32[1024,128]{1,0:T(8,128)S(1)} %get-tuple-element.37.x_ref.own_ref), channel_id=1, source_target_pairs={{0,4},{4,0},{1,5},{5,1},{2,6},{6,2},{3,7},{7,3},{8,12},{12,8},{9,1... | collective-permute-start | bytes 1572872 | tf_op jit(solution)/shard_map/ppermute | solution.py:66
  52.1 4.3 %collective-permute-start.13 = (f32[1024,128]{1,0:T(8,128)S(1)}, f32[1024,128]{1,0:T(8,128)S(1)}, u32[]{:S(2)}, u32[]{:S(2)}) collective-permute-start(f32[1024,128]{1,0:T(8,128)S(1)} %get-tuple-element.50.own_ref), channel_id=1, source_target_pairs={{0,4},{4,0},{1,5},{5,1},{2,6},{6,2},{3,7},{7,3},{8,12},{12,8},{9,1... | collective-permute-start | bytes 1572872 | tf_op jit(solution)/shard_map/ppermute | solution.py:66
  62.9 2.7 %collective-permute-start.14 = (f32[1024,256]{1,0:T(8,128)S(1)}, f32[1024,256]{1,0:T(8,128)S(1)}, u32[]{:S(2)}, u32[]{:S(2)}) collective-permute-start(f32[1024,256]{1,0:T(8,128)S(1)} %get-tuple-element.53.own_ref), channel_id=1, source_target_pairs={{0,4},{4,0},{1,5},{5,1},{2,6},{6,2},{3,7},{7,3},{8,12},{12,8},{9,1... | collective-permute-start | bytes 3145736 | tf_op jit(solution)/shard_map/ppermute | solution.py:66
  67.5 1.2 %collective-permute-start.15 = (f32[8,128]{1,0:T(8,128)S(1)}, f32[8,128]{1,0:T(8,128)S(1)}, u32[]{:S(2)}, u32[]{:S(2)}) collective-permute-start(f32[8,128]{1,0:T(8,128)S(1)} %get-tuple-element.55.own_ref), channel_id=1, source_target_pairs={{0,4},{4,0},{1,5},{5,1},{2,6},{6,2},{3,7},{7,3},{8,12},{12,8},{9,1... | collective-permute-start | bytes 12296 | tf_op jit(solution)/shard_map/ppermute | solution.py:66
  71.8 2.2 %collective-permute-start.16 = (f32[1024,128]{1,0:T(8,128)S(1)}, f32[1024,128]{1,0:T(8,128)S(1)}, u32[]{:S(2)}, u32[]{:S(2)}) collective-permute-start(f32[1024,128]{1,0:T(8,128)S(1)} %get-tuple-element.60.own_ref), channel_id=1, source_target_pairs={{0,4},{4,0},{1,5},{5,1},{2,6},{6,2},{3,7},{7,3},{8,12},{12,8},{9,1... | collective-permute-start | bytes 1572872 | tf_op jit(solution)/shard_map/ppermute | solution.py:66
  80.5 2.7 %collective-permute-start.17 = (f32[1024,256]{1,0:T(8,128)S(1)}, f32[1024,256]{1,0:T(8,128)S(1)}, u32[]{:S(2)}, u32[]{:S(2)}) collective-permute-start(f32[1024,256]{1,0:T(8,128)S(1)} %get-tuple-element.63.own_ref), channel_id=1, source_target_pairs={{0,4},{4,0},{1,5},{5,1},{2,6},{6,2},{3,7},{7,3},{8,12},{12,8},{9,1... | collective-permute-start | bytes 3145736 | tf_op jit(solution)/shard_map/ppermute | solution.py:66
  85.2 1.2 %collective-permute-start.18 = (f32[8,128]{1,0:T(8,128)S(1)}, f32[8,128]{1,0:T(8,128)S(1)}, u32[]{:S(2)}, u32[]{:S(2)}) collective-permute-start(f32[8,128]{1,0:T(8,128)S(1)} %get-tuple-element.65.own_ref), channel_id=1, source_target_pairs={{0,4},{4,0},{1,5},{5,1},{2,6},{6,2},{3,7},{7,3},{8,12},{12,8},{9,1... | collective-permute-start | bytes 12296 | tf_op jit(solution)/shard_map/ppermute | solution.py:66
where the time goes:
time: 87.4 us; the launch traced here: 87.2 us
  Pallas kernels  28.4 us (32%)
  waiting for transfers between devices  25.5 us (29%)
  blocking collectives  21.7 us (25%)
  starting transfers between devices  11.2 us (13%)
    pallas_call x13, Pallas kernels, call(): pl.pallas_call(kernel, out_shape=[jax.ShapeDtypeStruct(s, t) for s, t in...  28.4 us
    all_to_all x1, blocking collectives, gathered(): lax.all_to_all(copies, AXES, 0, 0, axis_index_groups=cubes(), tiled=True)  21.7 us
    ppermute x12, waiting for transfers between devices, sent(): out.append(lax.ppermute(part, AXES, pairs(order[step])))  17.3 us
    ppermute x7, waiting for transfers between devices, swap_cores(): return lax.ppermute(x, 'c', [(0, 1), (1, 0)])  8.22 us
    ppermute x7, starting transfers between devices, swap_cores(): return lax.ppermute(x, 'c', [(0, 1), (1, 0)])  5.9 us
    ppermute x12, starting transfers between devices, sent(): out.append(lax.ppermute(part, AXES, pairs(order[step])))  5.31 us
  transfers between devices with their start and end apart: 19, of which 12 were waited for; matrix products, arithmetic and copies ran while one was open for 0% of the time, Pallas kernels for 7%

commit v1 on v0

--- a/solution.py
+++ b/solution.py
@@ -168,8 +168,7 @@
     owner = place * 8 + FIRSTS[color] + ((row - place * count) >> 4)
     hot = owner == lax.broadcasted_iota(jnp.int32, (ROWS[color], HALF), 1)
     hot = jnp.where(hot, 1.0, 0.0).astype(bf16)
-    hot_ref[:, :HALF] = hot
-    hot_ref[:, HALF:] = hot
+    hot_ref[...] = hot
 
 
 def gradient(rows_ref, hot_ref, both, curve_ref):
@@ -177,7 +176,7 @@
     for at in range(0, rows_ref.shape[0], CHUNK):
         part = pl.ds(at, CHUNK)
         logit = nn(rows_ref[part, :], both)
-        hot = hot_ref[part, :HALF].astype(f32)
+        hot = hot_ref[part, :].astype(f32)
         logit = jnp.sum((logit[:, :HALF] + logit[:, HALF:]) * hot, axis=1, keepdims=True)
         prob = 1.0 / (1.0 + jnp.exp(logit))
         curve_ref[part, :] = jnp.broadcast_to(like_weight * prob * (1.0 - prob), (CHUNK, HALF))
@@ -219,21 +218,27 @@
     return alpha + gamma * grown, -gamma * alpha
 
 
-def own_update(on_drift, on_image, drift_ref, image_ref, turn_ref):
+def own_update(on_drift, on_image, drift_ref, image_refs, turn_ref):
     mine = half_of(lax.axis_index("c"))
-    own = pl.ds(pl.multiple_of(lax.axis_index("z") * SLICE, SLICE), SLICE)
-    turn_ref[...] = (on_drift * drift_ref[own, mine] + on_image * image_ref[own, mine]).T
+    z = lax.axis_index("z")
+    own = pl.ds(pl.multiple_of(z * SLICE, SLICE), SLICE)
+    near = pl.ds(pl.multiple_of((z & 1) * SLICE, SLICE), SLICE)
+    image = jnp.where(z < 2, image_refs[0][near, mine], image_refs[1][near, mine])
+    turn_ref[...] = (on_drift * drift_ref[own, mine] + on_image * image).T
     return turn_ref[pl.ds(pl.multiple_of(own_place() * 8, 8), 8), :]
 
 
 def next_kernel(
-    r0, r1, r2, h0, h1, h2, x_ref, drift_ref, image_ref, own_ref, other_ref,
+    r0, r1, r2, h0, h1, h2, x_ref, drift_ref, image_a, image_b, own_ref, other_ref,
     grad_ref, c0, c1, c2, new_ref, out_ref, turn_ref,
 ):
     on_drift, on_image = factors(own_ref, other_ref)
-    out_ref[...] = own_update(on_drift, on_image, drift_ref, image_ref, turn_ref)
-    update = on_drift * drift_ref[...] + on_image * image_ref[...]
-    new_ref[...] = x_ref[...] + move_size * update
+    images = (image_a, image_b)
+    out_ref[...] = own_update(on_drift, on_image, drift_ref, images, turn_ref)
+    for k, image_ref in enumerate(images):
+        near = slice(k * WIDE // 2, (k + 1) * WIDE // 2)
+        update = on_drift * drift_ref[near, :] + on_image * image_ref[...]
+        new_ref[near, :] = x_ref[near, :] + move_size * update
     x = new_ref[:, half_of(lax.axis_index("c"))]
     both = jnp.concatenate(two(x), axis=1)
     total = gradient(r0, h0, both, c0) + gradient(r1, h1, both, c1) + gradient(r2, h2, both, c2)
@@ -241,11 +246,11 @@
 
 
 def last_kernel(
-    drift_ref, image_ref, own_ref, other_ref, before_ref, out_ref, turn_ref
+    drift_ref, image_a, image_b, own_ref, other_ref, before_ref, out_ref, turn_ref
 ):
     on_drift, on_image = factors(own_ref, other_ref)
     out_ref[0] = before_ref[...]
-    out_ref[1] = own_update(on_drift, on_image, drift_ref, image_ref, turn_ref)
+    out_ref[1] = own_update(on_drift, on_image, drift_ref, (image_a, image_b), turn_ref)
 
 
 def similarity(x, kernel_ref):
@@ -268,9 +273,25 @@
     similarity(x_ref[...], kernel_ref)
 
 
+def spread(thirds, weighted_ref, near):
+    return sum(
+        tn(rows_ref[:, near], weighted_ref[k, span(color), :])
+        for color, rows_ref in enumerate(thirds)
+        for k in range(2)
+    )
+
+
+def image_part(thirds, near, x_ref, drift, square, q, weighted_ref):
+    mine = half_of(lax.axis_index("c"))
+    pull = x_ref[near, :] * jnp.sum(q, axis=0, keepdims=True)
+    pull = pull - stacked(two(x_ref[near, mine]), two(q))
+    own = prior_precision * jnp.sum(square, axis=0, keepdims=True) * drift
+    return (spread(thirds, weighted_ref, near) + (own + cross * pull)) / MANY
+
+
 def first_kernel(
-    r0, r1, r2, h0, h1, h2, c0, c1, c2, x_ref, kernel_ref, own_ref, other_ref,
-    drift_ref, image_ref, factor_ref, weighted_ref,
+    r0, r1, r2, c0, c1, c2, x_ref, kernel_ref, own_ref, other_ref,
+    drift_ref, image_ref, factor_ref, weighted_ref, q_ref, square_ref,
 ):
     core = lax.axis_index("c")
     mine = half_of(core)
@@ -283,66 +304,96 @@
     drift_two = two(drift)
     kernel_own = kernel_ref[mine, :]
     square = kernel_own * kernel_own
-    square_two = jnp.concatenate(two(square), axis=0)
+    square_ref[...] = square
     thirds = (r0, r1, r2)
-    for color, (rows_ref, hot_ref, curve_ref) in enumerate(zip(thirds, (h0, h1, h2), (c0, c1, c2))):
+    for color, (rows_ref, curve_ref) in enumerate(zip(thirds, (c0, c1, c2))):
+        count = ROWS[color] // 256
         for at in range(0, ROWS[color], CHUNK):
             part, to = pl.ds(at, CHUNK), pl.ds(STARTS[color] + at, CHUNK)
-            curve = curve_ref[part, :]
-            factor = nn(hot_ref[part, :], square_two) * jnp.concatenate([curve, curve], axis=1)
+            pieces = []
+            for group in range(at // DATA, (at + CHUNK) // DATA):
+                j = group // count * 8 + FIRSTS[color] + group % count
+                curve = curve_ref[pl.ds(group * DATA, DATA), :]
+                wide = jnp.concatenate([curve, curve], axis=1)
+                pieces.append(jnp.broadcast_to(square_ref[j : j + 1, :], wide.shape) * wide)
+            factor = jnp.concatenate(pieces, axis=0)
             factor_ref[to, :] = factor
             rows = rows_ref[part, :]
             high, low = two((nn(rows, drift_two[0]) + nn(rows, drift_two[1])) * factor)
             weighted_ref[0, to, :] = high
             weighted_ref[1, to, :] = low
-    x_own = x_ref[:, mine]
-    x_two = two(x_own)
-    along = stacked(two(x_own.T), drift_two)
+    along = stacked(two(x_ref[:, mine].T), drift_two)
     q = square * (jnp.sum(x * drift, axis=0, keepdims=True) - along)
-    pull = x * jnp.sum(q, axis=0, keepdims=True) - stacked(x_two, two(q))
-    image_ref[...] = (
-        sum(
-            tn(rows_ref[...], weighted_ref[k, span(color), :])
-            for color, rows_ref in enumerate(thirds)
-            for k in range(2)
-        )
-        + (prior_precision * jnp.sum(square, axis=0, keepdims=True) * drift + cross * pull)
-    ) / MANY
+    q_ref[...] = q
+    near = slice(0, WIDE // 2)
+    image_ref[...] = image_part(thirds, near, x_ref, drift[near], square, q, weighted_ref)
+
+
+def rest_kernel(r0, r1, r2, x_ref, kernel_ref, drift_ref, weighted_ref, q_ref, image_ref):
+    kernel_own = kernel_ref[half_of(lax.axis_index("c")), :]
+    near = slice(WIDE // 2, WIDE)
+    image_ref[...] = image_part(
+        (r0, r1, r2), near, x_ref, drift_ref[near, :], kernel_own * kernel_own, q_ref[...],
+        weighted_ref,
+    )
+
+
+def read_image(near, x_ref, drift_ref, image):
+    rounded = image.astype(bf16)
+    wide = rounded.astype(f32)
+    pairs_ = (
+        (drift_ref[near, :], drift_ref[near, :]),
+        (drift_ref[near, :], image),
+        (image, image),
+        (image, wide),
+        (wide, wide),
+        (x_ref[near, :], image),
+    )
+    sums = [jnp.sum(a * b, axis=0, keepdims=True) for a, b in pairs_]
+    x_own = x_ref[near, half_of(lax.axis_index("c"))]
+    return sums, stacked(two(x_own.T), two(image)), rounded
 
 
 def second_kernel(
-    r0, r1, r2, x_ref, kernel_ref, factor_ref, drift_ref, own_ref, other_ref,
+    r0, r1, r2, x_ref, drift_ref, own_ref, other_ref,
+    image_ref, projected_ref, along_ref, sums_ref,
+):
+    near = slice(0, WIDE // 2)
+    image = own_ref[...] + other_ref[...]
+    image_ref[...] = image
+    sums, along, rounded = read_image(near, x_ref, drift_ref, image)
+    along_ref[...] = along
+    for at, value in enumerate(sums):
+        sums_ref[at : at + 1, :] = value
+    sums_ref[6:, :] = jnp.zeros((2, MANY), f32)
+    for color, rows_ref in enumerate((r0, r1, r2)):
+        projected_ref[span(color), :] = nn(rows_ref[:, near], rounded)
+
+
+def third_kernel(
+    r0, r1, r2, x_ref, kernel_ref, factor_ref, drift_ref, projected_ref, along_ref, before_ref,
+    own_ref, other_ref,
     image_ref, sums_ref,
 ):
-    mine = half_of(lax.axis_index("c"))
+    near = slice(WIDE // 2, WIDE)
     image = own_ref[...] + other_ref[...]
     image_ref[...] = image
-    drift = drift_ref[...]
-    image_two = two(image)
-    rounded = image_two[0]
-    wide = rounded.astype(f32)
+    sums, along, rounded = read_image(near, x_ref, drift_ref, image)
+    sums = [value + before_ref[at : at + 1, :] for at, value in enumerate(sums)]
     total = jnp.zeros((1, MANY), f32)
     for color, rows_ref in enumerate((r0, r1, r2)):
         for at in range(0, ROWS[color], CHUNK):
-            projected = nn(rows_ref[pl.ds(at, CHUNK), :], rounded)
-            factor = factor_ref[pl.ds(STARTS[color] + at, CHUNK), :]
-            total += jnp.sum(projected * projected * factor, axis=0, keepdims=True)
-    fit = jnp.sum(image * wide, axis=0, keepdims=True)
-    fit = fit / jnp.maximum(jnp.sum(wide * wide, axis=0, keepdims=True), 1e-30)
+            to = pl.ds(STARTS[color] + at, CHUNK)
+            projected = projected_ref[to, :] + nn(rows_ref[pl.ds(at, CHUNK), near], rounded)
+            total += jnp.sum(projected * projected * factor_ref[to, :], axis=0, keepdims=True)
+    fit = sums[3] / jnp.maximum(sums[4], 1e-30)
     total *= fit * fit
+    mine = half_of(lax.axis_index("c"))
     square = kernel_ref[mine, :] * kernel_ref[mine, :]
-    along = stacked(two(x_ref[:, mine].T), image_two)
-    gap = jnp.sum(x_ref[...] * image, axis=0, keepdims=True) - along
+    gap = sums[5] - (along + along_ref[...])
     total += cross * jnp.sum(square * gap * gap, axis=0, keepdims=True)
-    length = jnp.sum(image * image, axis=0, keepdims=True)
-    total += prior_precision * jnp.sum(square, axis=0, keepdims=True) * length
-    figures = (
-        jnp.sum(drift * drift, axis=0, keepdims=True),
-        jnp.sum(drift * image, axis=0, keepdims=True),
-        length,
-        total / MANY,
-    )
-    for at, value in enumerate(figures):
+    total += prior_precision * jnp.sum(square, axis=0, keepdims=True) * sums[2]
+    for at, value in enumerate((*sums[:3], total / MANY)):
         sums_ref[at : at + 1, :] = jnp.broadcast_to(
             jnp.sum(value, axis=1, keepdims=True), (1, HALF)
         )
@@ -379,10 +430,12 @@
     tall = ((count, MANY), f32)
     square = ((MANY, MANY), f32)
     long = ((WIDE, MANY), f32)
+    wing = ((WIDE // 2, MANY), f32)
+    low = ((HALF, MANY), f32)
     half = ((WIDE, HALF), f32)
     turn = [pltpu.VMEM((HALF, SLICE), f32)]
     rows_of = [((r, WIDE), bf16) for r in ROWS]
-    hot_of = [((r, MANY), bf16) for r in ROWS]
+    hot_of = [((r, HALF), bf16) for r in ROWS]
     curve_of = [((r, HALF), f32) for r in ROWS]
     rows, hot, curve = [None] * 3, [None] * 3, [None] * 3
     rows[0], hot[0], x_own = call(
@@ -402,26 +455,33 @@
         if newton_step > 0:
             grad, *curve, x, update = call(
                 next_kernel, [half, *curve_of, long, ((8, SLICE), f32)],
-                *rows, *hot, x, drift, image, sums, sums_other, scratch=turn,
+                *rows, *hot, x, drift, *image, sums, sums_other, scratch=turn,
             )
         grad_other = swap_cores(grad)
         if newton_step > 0:
             (kernel,) = call(again_kernel, [square], x)
-        drift, image_own, factor = call(
+        drift, own_a, factor, weighted, q = call(
             first_kernel,
-            [long, long, tall],
-            *rows, *hot, *curve, x, kernel, grad, grad_other,
-            scratch=[pltpu.VMEM((2, count, MANY), bf16)],
-        )
-        image, sums = call(
-            second_kernel,
-            [long, ((8, HALF), f32)],
-            *rows, x, kernel, factor, drift, image_own, swap_cores(image_own),
-        )
+            [long, wing, tall, ((2, count, MANY), bf16), low],
+            *rows, *curve, x, kernel, grad, grad_other,
+            scratch=[pltpu.VMEM((HALF, MANY), f32)],
+        )
+        other_a = swap_cores(own_a)
+        (own_b,) = call(rest_kernel, [wing], *rows, x, kernel, drift, weighted, q)
+        other_b = swap_cores(own_b)
+        image_a, projected, along, partial_sums = call(
+            second_kernel, [wing, tall, low, ((8, MANY), f32)],
+            *rows, x, drift, own_a, other_a,
+        )
+        image_b, sums = call(
+            third_kernel, [wing, ((8, HALF), f32)],
+            *rows, x, kernel, factor, drift, projected, along, partial_sums, own_b, other_b,
+        )
+        image = (image_a, image_b)
         sums_other = swap_cores(sums)
     (updates,) = call(
         last_kernel, [((NEWTON, 8, SLICE), f32)],
-        drift, image, sums, sums_other, update, scratch=turn,
+        drift, *image, sums, sums_other, update, scratch=turn,
     )
     return updates
 

time: 87.4 us -> 85.8 us (0.982)
  waiting for transfers between devices: 25.5 us -> 22.3 us
  Pallas kernels: 28.4 us -> 29.6 us
    ppermute x7 -> x9, waiting for transfers between devices: 8.22 us -> 4.96 us  [swap_cores(): return lax.ppermute(x, 'c', [(0, 1), (1, 0)])]
    pallas_call x13 -> x17, Pallas kernels: 28.4 us -> 29.6 us  [call(): pl.pallas_call(kernel, out_shape=[jax.ShapeDtypeStruct(s, t) for s, t in...]
    ppermute x7 -> x9, starting transfers between devices: 5.9 us -> 6.31 us  [swap_cores(): return lax.ppermute(x, 'c', [(0, 1), (1, 0)])]
  transfers between devices with their start and end apart: 19 -> 21, of which waited for: 12 -> 12; matrix products, arithmetic and copies ran while one was open for 0% -> 0% of each run, Pallas kernels for 7% -> 13%
where the time goes in v1:
time: 85.8 us; the launch traced here: 85.6 us
  Pallas kernels  29.6 us (34%)
  waiting for transfers between devices  22.3 us (26%)
  blocking collectives  21.7 us (25%)
  starting transfers between devices  11.6 us (14%)
    pallas_call x17, Pallas kernels, call(): pl.pallas_call(kernel, out_shape=[jax.ShapeDtypeStruct(s, t) for s, t in...  29.6 us
    all_to_all x1, blocking collectives, gathered(): lax.all_to_all(copies, AXES, 0, 0, axis_index_groups=cubes(), tiled=True)  21.7 us
    ppermute x12, waiting for transfers between devices, sent(): out.append(lax.ppermute(part, AXES, pairs(order[step])))  17.3 us
    ppermute x9, starting transfers between devices, swap_cores(): return lax.ppermute(x, 'c', [(0, 1), (1, 0)])  6.31 us
    ppermute x12, starting transfers between devices, sent(): out.append(lax.ppermute(part, AXES, pairs(order[step])))  5.31 us
    ppermute x9, waiting for transfers between devices, swap_cores(): return lax.ppermute(x, 'c', [(0, 1), (1, 0)])  4.96 us
  transfers between devices with their start and end apart: 21, of which 12 were waited for; matrix products, arithmetic and copies ran while one was open for 0% of the time, Pallas kernels for 13%

profile of v1, /device:TPU:1, one launch (start us, length us, event | category | flops | bytes accessed | tf_op | source)
XLA Modules:
  0.0 85.6 jit_solution(11092978782224813767)
XLA Ops:
  0.0 1.9 %shard_map.37 = bf16[8,144,256]{2,1,0:T(8,128)(2,1)} custom-call(f32[8,256]{1,0:T(8,128)} %x_far.1, bf16[8,16,256]{2,1,0:T(8,128)(2,1)} %rows_far.1, s32[8,16]{1,0:T(8,128)} %labels_far.1), custom_call_target="tpu_custom_call" | custom-call | tf_op jit(solution)/shard_map/pallas_call | solution.py:405
  1.9 21.7 %all_to_all.5 = bf16[8,144,256]{2,1,0:T(8,128)(2,1)S(1)} all-to-all(bf16[8,144,256]{2,1,0:T(8,128)(2,1)} %shard_map.37), channel_id=1, replica_groups={{0,1,8,9,32,33,40,41},{2,3,10,11,34,35,42,43},{4,7,28,31,100,103,124,12..., dimensions={0} | all-to-all | bytes 1179648 | tf_op jit(solution)/shard_map/all_to_all | solution.py:70
  23.6 0.1 collective-permute-start
  23.7 0.1 collective-permute-start.4
  23.8 0.1 collective-permute-start.8
  23.9 4.3 %collective-permute-done = bf16[8,48,256]{2,1,0:T(8,128)(2,1)S(1)} collective-permute-done((bf16[8,48,256]{2,1,0:T(8,128)(2,1)S(1)}, bf16[8,48,256]{2,1,0:T(8,128)(2,1)S(1)}, u32[]{:S(2)}, u32[]{:S(2)}) %collective-permute-start) | collective-permute-done | bytes 196640 | tf_op jit(solution)/shard_map/ppermute | solution.py:76
  28.3 0.1 collective-permute-start.2
  28.4 0.1 collective-permute-start.1
  28.5 0.0 collective-permute-done.4
  28.5 1.4 %collective-permute-start.5 = (bf16[16,48,256]{2,1,0:T(8,128)(2,1)S(1)}, bf16[16,48,256]{2,1,0:T(8,128)(2,1)S(1)}, u32[]{:S(2)}, u32[]{:S(2)}) collective-permute-start(bf16[16,48,256]{2,1,0:T(8,128)(2,1)S(1)} %pad_maximum_fusion.1.a), channel_id=1, source_target_pairs={{0,3},{1,2},{2,1},{3,0},{4,5},{5,4},{6,7},{7,6},{8,11},{9,10},{10,... | collective-permute-start | bytes 1179656 | tf_op jit(solution)/shard_map/ppermute | solution.py:76
  30.0 0.0 collective-permute-done.8
  30.0 0.3 collective-permute-start.9
  30.3 5.1 %collective-permute-done.1.b = bf16[16,48,256]{2,1,0:T(8,128)(2,1)S(1)} collective-permute-done((bf16[16,48,256]{2,1,0:T(8,128)(2,1)S(1)}, bf16[16,48,256]{2,1,0:T(8,128)(2,1)S(1)}, u32[]{:S(2)}, u32[]{:S(2)}) %collective-permute-start.1) | collective-permute-done | bytes 393248 | tf_op jit(solution)/shard_map/ppermute | solution.py:76
  35.4 1.4 %collective-permute-start.3 = (bf16[16,48,256]{2,1,0:T(8,128)(2,1)S(1)}, bf16[16,48,256]{2,1,0:T(8,128)(2,1)S(1)}, u32[]{:S(2)}, u32[]{:S(2)}) collective-permute-start(bf16[16,48,256]{2,1,0:T(8,128)(2,1)S(1)} %collective-permute-done.1.b), channel_id=1, source_target_pairs={{0,3},{1,2},{2,1},{3,0},{4,5},{5,4},{6,7},{7,6},{8,11},{9,10},{10,... | collective-permute-start | bytes 1179656 | tf_op jit(solution)/shard_map/ppermute | solution.py:76
  36.7 0.0 collective-permute-start.6
  36.8 2.4 %collective-permute-done.5.b = bf16[16,48,256]{2,1,0:T(8,128)(2,1)S(1)} collective-permute-done((bf16[16,48,256]{2,1,0:T(8,128)(2,1)S(1)}, bf16[16,48,256]{2,1,0:T(8,128)(2,1)S(1)}, u32[]{:S(2)}, u32[]{:S(2)}) %collective-permute-start.5) | collective-permute-done | bytes 393248 | tf_op jit(solution)/shard_map/ppermute | solution.py:76
  39.2 0.3 collective-permute-start.7
  39.5 0.0 collective-permute-done.2.c
  39.5 0.4 collective-permute-start.10
  39.9 0.0 collective-permute-done.9.b
  39.9 1.1 %collective-permute-start.11 = (bf16[16,48,256]{2,1,0:T(8,128)(2,1)S(1)}, bf16[16,48,256]{2,1,0:T(8,128)(2,1)S(1)}, u32[]{:S(2)}, u32[]{:S(2)}) collective-permute-start(bf16[16,48,256]{2,1,0:T(8,128)(2,1)S(1)} %collective-permute-done.9.b), channel_id=1, source_target_pairs={{0,96},{1,97},{2,98},{3,99},{4,36},{5,37},{6,38},{7,39},{8,104},{9... | collective-permute-start | bytes 1179656 | tf_op jit(solution)/shard_map/ppermute | solution.py:76
  41.0 2.7 %collective-permute-done.3.d = bf16[16,48,256]{2,1,0:T(8,128)(2,1)S(1)} collective-permute-done((bf16[16,48,256]{2,1,0:T(8,128)(2,1)S(1)}, bf16[16,48,256]{2,1,0:T(8,128)(2,1)S(1)}, u32[]{:S(2)}, u32[]{:S(2)}) %collective-permute-start.3) | collective-permute-done | bytes 393248 | tf_op jit(solution)/shard_map/ppermute | solution.py:76
  43.7 0.5 shard_map.38
  44.2 1.2 %collective-permute-start.12 = (f32[1024,128]{1,0:T(8,128)S(1)}, f32[1024,128]{1,0:T(8,128)S(1)}, u32[]{:S(2)}, u32[]{:S(2)}) collective-permute-start(f32[1024,128]{1,0:T(8,128)S(1)} %get-tuple-element.49.x_ref.own_ref), channel_id=1, source_target_pairs={{0,4},{4,0},{1,5},{5,1},{2,6},{6,2},{3,7},{7,3},{8,12},{12,8},{9,1... | collective-permute-start | bytes 1572872 | tf_op jit(solution)/shard_map/ppermute | solution.py:66
  45.4 1.0 %shard_map.39 = (f32[1024,128]{1,0:T(8,128)S(1)}, f32[512,128]{1,0:T(8,128)S(1)}) custom-call(bf16[512,1024]{1,0:T(8,128)(2,1)S(1)} %get-tuple-element.48.rows_ref.r0, bf16[512,128]{1,0:T(8,128)(2,1)S(1)} %get-tuple-element.50.hot_ref.h0, f32[1024,128]{1,0:T(8,128)S(1)} %get-tuple-element.49.x_ref.own_ref), custom_call_target="tpu_custom_call" | custom-call | tf_op jit(solution)/shard_map/pallas_call | solution.py:405
  46.4 0.0 collective-permute-done.6.c
  46.4 1.4 %collective-permute-done.7.d = bf16[16,48,256]{2,1,0:T(8,128)(2,1)S(1)} collective-permute-done((bf16[16,48,256]{2,1,0:T(8,128)(2,1)S(1)}, bf16[16,48,256]{2,1,0:T(8,128)(2,1)S(1)}, u32[]{:S(2)}, u32[]{:S(2)}) %collective-permute-start.7) | collective-permute-done | bytes 393248 | tf_op jit(solution)/shard_map/ppermute | solution.py:76
  47.9 1.5 %shard_map.40 = (bf16[768,1024]{1,0:T(8,128)(2,1)S(1)}, bf16[768,128]{1,0:T(8,128)(2,1)S(1)}, f32[1024,128]{1,0:T(8,128)S(1)}, f32[768,128]{1,0:T(8,128)S(1)}) custom-call(bf16[16,48,256]{2,1,0:T(8,128)(2,1)S(1)} %pad_maximum_fusion.1.a, bf16[16,48,256]{2,1,0:T(8,128)(2,1)S(1)} %collective-permute-done.5.b, ...), custom_call_target="tpu_custom_call" | custom-call | tf_op jit(solution)/shard_map/pallas_call | solution.py:405
  49.3 0.0 collective-permute-done.10.c
  49.4 1.3 %collective-permute-done.11.d = bf16[16,48,256]{2,1,0:T(8,128)(2,1)S(1)} collective-permute-done((bf16[16,48,256]{2,1,0:T(8,128)(2,1)S(1)}, bf16[16,48,256]{2,1,0:T(8,128)(2,1)S(1)}, u32[]{:S(2)}, u32[]{:S(2)}) %collective-permute-start.11) | collective-permute-done | bytes 393248 | tf_op jit(solution)/shard_map/ppermute | solution.py:76
  50.7 1.4 %shard_map.41 = (bf16[768,1024]{1,0:T(8,128)(2,1)S(1)}, bf16[768,128]{1,0:T(8,128)(2,1)S(1)}, f32[1024,128]{1,0:T(8,128)S(1)}, f32[768,128]{1,0:T(8,128)S(1)}) custom-call(bf16[16,48,256]{2,1,0:T(8,128)(2,1)S(1)} %pad_maximum_fusion.2.a, bf16[16,48,256]{2,1,0:T(8,128)(2,1)S(1)} %collective-permute-done.9.b, ...), custom_call_target="tpu_custom_call" | custom-call | tf_op jit(solution)/shard_map/pallas_call | solution.py:405
  52.1 2.8 %collective-permute-start.13 = (f32[1024,128]{1,0:T(8,128)S(1)}, f32[1024,128]{1,0:T(8,128)S(1)}, u32[]{:S(2)}, u32[]{:S(2)}) collective-permute-start(f32[1024,128]{1,0:T(8,128)S(1)} %get-tuple-element.62.own_ref), channel_id=1, source_target_pairs={{0,4},{4,0},{1,5},{5,1},{2,6},{6,2},{3,7},{7,3},{8,12},{12,8},{9,1... | collective-permute-start | bytes 1572872 | tf_op jit(solution)/shard_map/ppermute | solution.py:66
  54.9 0.0 collective-permute-done.12.other_ref
  54.9 0.8 shard_map.42
  55.7 0.8 collective-permute-done.13.other_ref
  56.4 5.2 %shard_map.43 = (f32[1024,256]{1,0:T(8,128)S(1)}, f32[512,256]{1,0:T(8,128)S(1)}, f32[2048,256]{1,0:T(8,128)S(1)}, bf16[2,2048,256]{2,1,0:T(8,128)(2,1)S(1)}, f32[128,256]{1,0:T(8,128)S(1)}) custom-call(bf16[512,1024]{1,0:T(8,128)(2,1)S(1)} %get-tuple-element.48.rows_ref.r0, bf16[768,1024]{1,0:T(8,128)(2,1)S(1)} %get-tuple-element.52.r1, ...), custom_call_target="tpu_custom_call" | custom-call | tf_op jit(solution)/shard_map/pallas_call | solution.py:405
  61.6 0.4 collective-permute-start.14
  62.0 1.5 %shard_map.45.own_ref = f32[512,256]{1,0:T(8,128)S(1)} custom-call(bf16[512,1024]{1,0:T(8,128)(2,1)S(1)} %get-tuple-element.48.rows_ref.r0, bf16[768,1024]{1,0:T(8,128)(2,1)S(1)} %get-tuple-element.52.r1, bf16[768,1024]{1,0:T(8,128)(2,1)S(1)} %get-tuple-element.54.r2, f32[1024,256]{1,0:T(8,128)S(1)} %get-tuple-element.57.x_ref, ...), custom_call_target="tpu_custom_call" | custom-call | tf_op jit(solution)/shard_map/pallas_call | solution.py:405
  63.5 0.2 collective-permute-start.15
  63.8 0.0 collective-permute-done.14.other_ref
  63.8 1.0 %shard_map.44 = (f32[512,256]{1,0:T(8,128)S(1)}, f32[2048,256]{1,0:T(8,128)S(1)}, f32[128,256]{1,0:T(8,128)S(1)}, f32[8,256]{1,0:T(8,128)S(1)}) custom-call(bf16[512,1024]{1,0:T(8,128)(2,1)S(1)} %get-tuple-element.48.rows_ref.r0, bf16[768,1024]{1,0:T(8,128)(2,1)S(1)} %get-tuple-element.52.r1, bf16[768,1024]{1,0:T(8,128)(2,1)S(1)} %get-tuple-element.54.r2, ...), custom_call_target="tpu_custom_call" | custom-call | tf_op jit(solution)/shard_map/pallas_call | solution.py:405
  64.7 0.8 collective-permute-done.15.other_ref
  65.5 1.3 %shard_map.46 = (f32[512,256]{1,0:T(8,128)S(1)}, f32[8,128]{1,0:T(8,128)S(1)}) custom-call(bf16[512,1024]{1,0:T(8,128)(2,1)S(1)} %get-tuple-element.48.rows_ref.r0, bf16[768,1024]{1,0:T(8,128)(2,1)S(1)} %get-tuple-element.52.r1, bf16[768,1024]{1,0:T(8,128)(2,1)S(1)} %get-tuple-element.54.r2, f32[1024,256]{1,0:T(8,128)S(1)} %get-tuple-element.57.x_ref, ...), custom_call_target="tpu_custom_call" | custom-call | tf_op jit(solution)/shard_map/pallas_call | solution.py:405
  66.8 0.2 collective-permute-start.16
  67.0 1.0 %collective-permute-done.16.other_ref = f32[8,128]{1,0:T(8,128)S(1)} collective-permute-done((f32[8,128]{1,0:T(8,128)S(1)}, f32[8,128]{1,0:T(8,128)S(1)}, u32[]{:S(2)}, u32[]{:S(2)}) %collective-permute-start.16) | collective-permute-done | bytes 4128 | tf_op jit(solution)/shard_map/ppermute | solution.py:66
  68.0 3.2 %shard_map.47 = (f32[1024,128]{1,0:T(8,128)S(1)}, f32[512,128]{1,0:T(8,128)S(1)}, f32[768,128]{1,0:T(8,128)S(1)}, f32[768,128]{1,0:T(8,128)S(1)}, f32[1024,256]{1,0:T(8,128)S(1)}, /*index=5*/f32[8,256]{1,0:T(8,128)S(1)}) custom-call(bf16[512,1024]{1,0:T(8,128)(2,1)S(1)} %get-tuple-element.48.rows_ref.r0, bf16[768,1024]{1,0:T(8,128)(2,1)S(1)} %get-tuple-element.52.r1, ...), custom_call_target="tpu_custom_call" | custom-call | tf_op jit(solution)/shard_map/pallas_call | solution.py:405
  71.2 0.4 collective-permute-start.17
  71.7 0.7 shard_map.48.kernel_ref
  72.4 1.1 %collective-permute-done.17.other_ref = f32[1024,128]{1,0:T(8,128)S(1)} collective-permute-done((f32[1024,128]{1,0:T(8,128)S(1)}, f32[1024,128]{1,0:T(8,128)S(1)}, u32[]{:S(2)}, u32[]{:S(2)}) %collective-permute-start.17) | collective-permute-done | bytes 524320 | tf_op jit(solution)/shard_map/ppermute | solution.py:66
  73.4 5.2 %shard_map.49 = (f32[1024,256]{1,0:T(8,128)S(1)}, f32[512,256]{1,0:T(8,128)S(1)}, f32[2048,256]{1,0:T(8,128)S(1)}, bf16[2,2048,256]{2,1,0:T(8,128)(2,1)S(1)}, f32[128,256]{1,0:T(8,128)S(1)}) custom-call(bf16[512,1024]{1,0:T(8,128)(2,1)S(1)} %get-tuple-element.48.rows_ref.r0, bf16[768,1024]{1,0:T(8,128)(2,1)S(1)} %get-tuple-element.52.r1, ...), custom_call_target="tpu_custom_call" | custom-call | tf_op jit(solution)/shard_map/pallas_call | solution.py:405
  78.6 0.2 collective-permute-start.18
  78.8 1.5 %shard_map.51.own_ref = f32[512,256]{1,0:T(8,128)S(1)} custom-call(bf16[512,1024]{1,0:T(8,128)(2,1)S(1)} %get-tuple-element.48.rows_ref.r0, bf16[768,1024]{1,0:T(8,128)(2,1)S(1)} %get-tuple-element.52.r1, bf16[768,1024]{1,0:T(8,128)(2,1)S(1)} %get-tuple-element.54.r2, f32[1024,256]{1,0:T(8,128)S(1)} %get-tuple-element.77.x_ref, ...), custom_call_target="tpu_custom_call" | custom-call | tf_op jit(solution)/shard_map/pallas_call | solution.py:405
  80.3 0.5 collective-permute-start.19
  80.8 0.0 collective-permute-done.18.other_ref
  80.8 1.0 %shard_map.50 = (f32[512,256]{1,0:T(8,128)S(1)}, f32[2048,256]{1,0:T(8,128)S(1)}, f32[128,256]{1,0:T(8,128)S(1)}, f32[8,256]{1,0:T(8,128)S(1)}) custom-call(bf16[512,1024]{1,0:T(8,128)(2,1)S(1)} %get-tuple-element.48.rows_ref.r0, bf16[768,1024]{1,0:T(8,128)(2,1)S(1)} %get-tuple-element.52.r1, bf16[768,1024]{1,0:T(8,128)(2,1)S(1)} %get-tuple-element.54.r2, ...), custom_call_target="tpu_custom_call" | custom-call | tf_op jit(solution)/shard_map/pallas_call | solution.py:405
  81.8 0.5 collective-permute-done.19.other_ref
  82.3 1.3 %shard_map.52 = (f32[512,256]{1,0:T(8,128)S(1)}, f32[8,128]{1,0:T(8,128)S(1)}) custom-call(bf16[512,1024]{1,0:T(8,128)(2,1)S(1)} %get-tuple-element.48.rows_ref.r0, bf16[768,1024]{1,0:T(8,128)(2,1)S(1)} %get-tuple-element.52.r1, bf16[768,1024]{1,0:T(8,128)(2,1)S(1)} %get-tuple-element.54.r2, f32[1024,256]{1,0:T(8,128)S(1)} %get-tuple-element.77.x_ref, ...), custom_call_target="tpu_custom_call" | custom-call | tf_op jit(solution)/shard_map/pallas_call | solution.py:405
  83.6 0.4 collective-permute-start.20
  84.0 0.8 collective-permute-done.20.other_ref
  84.8 0.8 shard_map.53
  (4 shorter events, 0.1 us)
Async XLA Ops:
  23.6 4.6 %collective-permute-start = (bf16[8,48,256]{2,1,0:T(8,128)(2,1)S(1)}, bf16[8,48,256]{2,1,0:T(8,128)(2,1)S(1)}, u32[]{:S(2)}, u32[]{:S(2)}) collective-permute-start(bf16[8,48,256]{2,1,0:T(8,128)(2,1)S(1)} %get-tuple-element.93), channel_id=1, source_target_pairs={{0,24},{1,25},{2,26},{3,27},{4,12},{5,13},{6,14},{7,15},{8,16},{9,... | collective-permute-start | bytes 589832 | tf_op jit(solution)/shard_map/ppermute | solution.py:76
  23.7 4.7 %collective-permute-start.4 = (bf16[8,48,256]{2,1,0:T(8,128)(2,1)S(1)}, bf16[8,48,256]{2,1,0:T(8,128)(2,1)S(1)}, u32[]{:S(2)}, u32[]{:S(2)}) collective-permute-start(bf16[8,48,256]{2,1,0:T(8,128)(2,1)S(1)} %get-tuple-element.92), channel_id=1, source_target_pairs={{0,96},{1,97},{2,98},{3,99},{4,36},{5,37},{6,38},{7,39},{8,104},{9... | collective-permute-start | bytes 589832 | tf_op jit(solution)/shard_map/ppermute | solution.py:76
  23.8 6.1 %collective-permute-start.8 = (bf16[8,48,256]{2,1,0:T(8,128)(2,1)S(1)}, bf16[8,48,256]{2,1,0:T(8,128)(2,1)S(1)}, u32[]{:S(2)}, u32[]{:S(2)}) collective-permute-start(bf16[8,48,256]{2,1,0:T(8,128)(2,1)S(1)} %get-tuple-element.91), channel_id=1, source_target_pairs={{0,3},{1,2},{2,1},{3,0},{4,5},{5,4},{6,7},{7,6},{8,11},{9,10},{10,... | collective-permute-start | bytes 589832 | tf_op jit(solution)/shard_map/ppermute | solution.py:76
  28.3 11.2 %collective-permute-start.2 = (bf16[16,48,256]{2,1,0:T(8,128)(2,1)S(1)}, bf16[16,48,256]{2,1,0:T(8,128)(2,1)S(1)}, u32[]{:S(2)}, u32[]{:S(2)}) collective-permute-start(bf16[16,48,256]{2,1,0:T(8,128)(2,1)S(1)} %pad_maximum_fusion.a), channel_id=1, source_target_pairs={{0,3},{1,2},{2,1},{3,0},{4,5},{5,4},{6,7},{7,6},{8,11},{9,10},{10,... | collective-permute-start | bytes 1179656 | tf_op jit(solution)/shard_map/ppermute | solution.py:76
  28.4 7.0 %collective-permute-start.1 = (bf16[16,48,256]{2,1,0:T(8,128)(2,1)S(1)}, bf16[16,48,256]{2,1,0:T(8,128)(2,1)S(1)}, u32[]{:S(2)}, u32[]{:S(2)}) collective-permute-start(bf16[16,48,256]{2,1,0:T(8,128)(2,1)S(1)} %pad_maximum_fusion.a), channel_id=1, source_target_pairs={{0,96},{1,97},{2,98},{3,99},{4,36},{5,37},{6,38},{7,39},{8,104},{9... | collective-permute-start | bytes 1179656 | tf_op jit(solution)/shard_map/ppermute | solution.py:76
  28.5 10.7 %collective-permute-start.5 = (bf16[16,48,256]{2,1,0:T(8,128)(2,1)S(1)}, bf16[16,48,256]{2,1,0:T(8,128)(2,1)S(1)}, u32[]{:S(2)}, u32[]{:S(2)}) collective-permute-start(bf16[16,48,256]{2,1,0:T(8,128)(2,1)S(1)} %pad_maximum_fusion.1.a), channel_id=1, source_target_pairs={{0,3},{1,2},{2,1},{3,0},{4,5},{5,4},{6,7},{7,6},{8,11},{9,10},{10,... | collective-permute-start | bytes 1179656 | tf_op jit(solution)/shard_map/ppermute | solution.py:76
  30.0 9.9 %collective-permute-start.9 = (bf16[16,48,256]{2,1,0:T(8,128)(2,1)S(1)}, bf16[16,48,256]{2,1,0:T(8,128)(2,1)S(1)}, u32[]{:S(2)}, u32[]{:S(2)}) collective-permute-start(bf16[16,48,256]{2,1,0:T(8,128)(2,1)S(1)} %pad_maximum_fusion.2.a), channel_id=1, source_target_pairs={{0,24},{1,25},{2,26},{3,27},{4,12},{5,13},{6,14},{7,15},{8,16},{9,... | collective-permute-start | bytes 1179656 | tf_op jit(solution)/shard_map/ppermute | solution.py:76
  35.4 8.3 %collective-permute-start.3 = (bf16[16,48,256]{2,1,0:T(8,128)(2,1)S(1)}, bf16[16,48,256]{2,1,0:T(8,128)(2,1)S(1)}, u32[]{:S(2)}, u32[]{:S(2)}) collective-permute-start(bf16[16,48,256]{2,1,0:T(8,128)(2,1)S(1)} %collective-permute-done.1.b), channel_id=1, source_target_pairs={{0,3},{1,2},{2,1},{3,0},{4,5},{5,4},{6,7},{7,6},{8,11},{9,10},{10,... | collective-permute-start | bytes 1179656 | tf_op jit(solution)/shard_map/ppermute | solution.py:76
  36.7 9.7 %collective-permute-start.6 = (bf16[16,48,256]{2,1,0:T(8,128)(2,1)S(1)}, bf16[16,48,256]{2,1,0:T(8,128)(2,1)S(1)}, u32[]{:S(2)}, u32[]{:S(2)}) collective-permute-start(bf16[16,48,256]{2,1,0:T(8,128)(2,1)S(1)} %pad_maximum_fusion.1.a), channel_id=1, source_target_pairs={{0,24},{1,25},{2,26},{3,27},{4,12},{5,13},{6,14},{7,15},{8,16},{9,... | collective-permute-start | bytes 1179656 | tf_op jit(solution)/shard_map/ppermute | solution.py:76
  39.2 8.7 %collective-permute-start.7 = (bf16[16,48,256]{2,1,0:T(8,128)(2,1)S(1)}, bf16[16,48,256]{2,1,0:T(8,128)(2,1)S(1)}, u32[]{:S(2)}, u32[]{:S(2)}) collective-permute-start(bf16[16,48,256]{2,1,0:T(8,128)(2,1)S(1)} %collective-permute-done.5.b), channel_id=1, source_target_pairs={{0,24},{1,25},{2,26},{3,27},{4,12},{5,13},{6,14},{7,15},{8,16},{9,... | collective-permute-start | bytes 1179656 | tf_op jit(solution)/shard_map/ppermute | solution.py:76
  39.5 9.8 %collective-permute-start.10 = (bf16[16,48,256]{2,1,0:T(8,128)(2,1)S(1)}, bf16[16,48,256]{2,1,0:T(8,128)(2,1)S(1)}, u32[]{:S(2)}, u32[]{:S(2)}) collective-permute-start(bf16[16,48,256]{2,1,0:T(8,128)(2,1)S(1)} %pad_maximum_fusion.2.a), channel_id=1, source_target_pairs={{0,96},{1,97},{2,98},{3,99},{4,36},{5,37},{6,38},{7,39},{8,104},{9... | collective-permute-start | bytes 1179656 | tf_op jit(solution)/shard_map/ppermute | solution.py:76
  39.9 10.8 %collective-permute-start.11 = (bf16[16,48,256]{2,1,0:T(8,128)(2,1)S(1)}, bf16[16,48,256]{2,1,0:T(8,128)(2,1)S(1)}, u32[]{:S(2)}, u32[]{:S(2)}) collective-permute-start(bf16[16,48,256]{2,1,0:T(8,128)(2,1)S(1)} %collective-permute-done.9.b), channel_id=1, source_target_pairs={{0,96},{1,97},{2,98},{3,99},{4,36},{5,37},{6,38},{7,39},{8,104},{9... | collective-permute-start | bytes 1179656 | tf_op jit(solution)/shard_map/ppermute | solution.py:76
  44.2 10.7 %collective-permute-start.12 = (f32[1024,128]{1,0:T(8,128)S(1)}, f32[1024,128]{1,0:T(8,128)S(1)}, u32[]{:S(2)}, u32[]{:S(2)}) collective-permute-start(f32[1024,128]{1,0:T(8,128)S(1)} %get-tuple-element.49.x_ref.own_ref), channel_id=1, source_target_pairs={{0,4},{4,0},{1,5},{5,1},{2,6},{6,2},{3,7},{7,3},{8,12},{12,8},{9,1... | collective-permute-start | bytes 1572872 | tf_op jit(solution)/shard_map/ppermute | solution.py:66
  52.1 4.3 %collective-permute-start.13 = (f32[1024,128]{1,0:T(8,128)S(1)}, f32[1024,128]{1,0:T(8,128)S(1)}, u32[]{:S(2)}, u32[]{:S(2)}) collective-permute-start(f32[1024,128]{1,0:T(8,128)S(1)} %get-tuple-element.62.own_ref), channel_id=1, source_target_pairs={{0,4},{4,0},{1,5},{5,1},{2,6},{6,2},{3,7},{7,3},{8,12},{12,8},{9,1... | collective-permute-start | bytes 1572872 | tf_op jit(solution)/shard_map/ppermute | solution.py:66
  61.6 2.1 %collective-permute-start.14 = (f32[512,256]{1,0:T(8,128)S(1)}, f32[512,256]{1,0:T(8,128)S(1)}, u32[]{:S(2)}, u32[]{:S(2)}) collective-permute-start(f32[512,256]{1,0:T(8,128)S(1)} %get-tuple-element.64.own_ref), channel_id=1, source_target_pairs={{0,4},{4,0},{1,5},{5,1},{2,6},{6,2},{3,7},{7,3},{8,12},{12,8},{9,1... | collective-permute-start | bytes 1572872 | tf_op jit(solution)/shard_map/ppermute | solution.py:66
  63.5 2.0 %collective-permute-start.15 = (f32[512,256]{1,0:T(8,128)S(1)}, f32[512,256]{1,0:T(8,128)S(1)}, u32[]{:S(2)}, u32[]{:S(2)}) collective-permute-start(f32[512,256]{1,0:T(8,128)S(1)} %shard_map.45.own_ref), channel_id=1, source_target_pairs={{0,4},{4,0},{1,5},{5,1},{2,6},{6,2},{3,7},{7,3},{8,12},{12,8},{9,1... | collective-permute-start | bytes 1572872 | tf_op jit(solution)/shard_map/ppermute | solution.py:66
  66.8 1.2 %collective-permute-start.16 = (f32[8,128]{1,0:T(8,128)S(1)}, f32[8,128]{1,0:T(8,128)S(1)}, u32[]{:S(2)}, u32[]{:S(2)}) collective-permute-start(f32[8,128]{1,0:T(8,128)S(1)} %get-tuple-element.73.own_ref), channel_id=1, source_target_pairs={{0,4},{4,0},{1,5},{5,1},{2,6},{6,2},{3,7},{7,3},{8,12},{12,8},{9,1... | collective-permute-start | bytes 12296 | tf_op jit(solution)/shard_map/ppermute | solution.py:66
  71.2 2.2 %collective-permute-start.17 = (f32[1024,128]{1,0:T(8,128)S(1)}, f32[1024,128]{1,0:T(8,128)S(1)}, u32[]{:S(2)}, u32[]{:S(2)}) collective-permute-start(f32[1024,128]{1,0:T(8,128)S(1)} %get-tuple-element.78.own_ref), channel_id=1, source_target_pairs={{0,4},{4,0},{1,5},{5,1},{2,6},{6,2},{3,7},{7,3},{8,12},{12,8},{9,1... | collective-permute-start | bytes 1572872 | tf_op jit(solution)/shard_map/ppermute | solution.py:66
  78.6 2.1 %collective-permute-start.18 = (f32[512,256]{1,0:T(8,128)S(1)}, f32[512,256]{1,0:T(8,128)S(1)}, u32[]{:S(2)}, u32[]{:S(2)}) collective-permute-start(f32[512,256]{1,0:T(8,128)S(1)} %get-tuple-element.80.own_ref), channel_id=1, source_target_pairs={{0,4},{4,0},{1,5},{5,1},{2,6},{6,2},{3,7},{7,3},{8,12},{12,8},{9,1... | collective-permute-start | bytes 1572872 | tf_op jit(solution)/shard_map/ppermute | solution.py:66
  80.3 2.0 %collective-permute-start.19 = (f32[512,256]{1,0:T(8,128)S(1)}, f32[512,256]{1,0:T(8,128)S(1)}, u32[]{:S(2)}, u32[]{:S(2)}) collective-permute-start(f32[512,256]{1,0:T(8,128)S(1)} %shard_map.51.own_ref), channel_id=1, source_target_pairs={{0,4},{4,0},{1,5},{5,1},{2,6},{6,2},{3,7},{7,3},{8,12},{12,8},{9,1... | collective-permute-start | bytes 1572872 | tf_op jit(solution)/shard_map/ppermute | solution.py:66
  83.6 1.2 %collective-permute-start.20 = (f32[8,128]{1,0:T(8,128)S(1)}, f32[8,128]{1,0:T(8,128)S(1)}, u32[]{:S(2)}, u32[]{:S(2)}) collective-permute-start(f32[8,128]{1,0:T(8,128)S(1)} %get-tuple-element.89.own_ref), channel_id=1, source_target_pairs={{0,4},{4,0},{1,5},{5,1},{2,6},{6,2},{3,7},{7,3},{8,12},{12,8},{9,1... | collective-permute-start | bytes 12296 | tf_op jit(solution)/shard_map/ppermute | solution.py:66

commit v2 on v1

--- a/solution.py
+++ b/solution.py
@@ -150,30 +150,41 @@
         out_ref[k] = whole
 
 
-def land(color, refs, rows_ref, hot_ref, tail_ref=None):
+def land(color, refs, arrived, rows_ref, tail_ref):
     count = ROWS[color] // 16
     order = ORDERS[color]
     for k in range(4):
         slot = pl.ds(pl.multiple_of(slice_at(k) * SLICE, SLICE), SLICE)
         for at in range(16):
             step = {"z": k >> 1, "y": at >> 3, "x": (at >> 1) & 1}
+            which = step[order[2]] * 2 + step[order[1]]
+            if which not in arrived:
+                continue
             unit = step[order[0]] * 8 + ((at >> 2) & 1) * 4 + (at & 1) * 2 + (k & 1)
-            ref = refs[step[order[2]] * 2 + step[order[1]]]
-            rows_ref[at * count : (at + 1) * count, slot] = ref[unit, :count, :]
-            if tail_ref is not None:
+            ref = refs[which]
+            start = STARTS[color] + at * count
+            rows_ref[start : start + count, slot] = ref[unit, :count, :]
+            if color == 0:
                 high, low = ref[unit, 32:40, :], ref[unit, 40:48, :]
                 tail_ref[at * 8 : at * 8 + 8, slot] = high.astype(f32) + low.astype(f32)
-    row = lax.broadcasted_iota(jnp.int32, (ROWS[color], HALF), 0)
-    place = (row * 43691) >> 21 if count == 48 else row >> 5
-    owner = place * 8 + FIRSTS[color] + ((row - place * count) >> 4)
-    hot = owner == lax.broadcasted_iota(jnp.int32, (ROWS[color], HALF), 1)
-    hot = jnp.where(hot, 1.0, 0.0).astype(bf16)
-    hot_ref[...] = hot
-
-
-def gradient(rows_ref, hot_ref, both, curve_ref):
+
+
+def early_kernel(*refs):
+    rows_ref, tail_ref, hot_ref = refs[9:]
+    for color in range(3):
+        land(color, refs[3 * color : 3 * color + 3], (0, 1, 2), rows_ref, tail_ref)
+        count = ROWS[color] // 16
+        row = lax.broadcasted_iota(jnp.int32, (ROWS[color], HALF), 0)
+        place = (row * 43691) >> 21 if count == 48 else row >> 5
+        owner = place * 8 + FIRSTS[color] + ((row - place * count) >> 4)
+        hot = owner == lax.broadcasted_iota(jnp.int32, (ROWS[color], HALF), 1)
+        hot_ref[span(color), :] = jnp.where(hot, 1.0, 0.0).astype(bf16)
+
+
+def gradient(rows_ref, hot_ref, x, curve_ref, start, stop):
+    both = jnp.concatenate(two(x), axis=1)
     weights = []
-    for at in range(0, rows_ref.shape[0], CHUNK):
+    for at in range(start, stop, CHUNK):
         part = pl.ds(at, CHUNK)
         logit = nn(rows_ref[part, :], both)
         hot = hot_ref[part, :].astype(f32)
@@ -181,31 +192,24 @@
         prob = 1.0 / (1.0 + jnp.exp(logit))
         curve_ref[part, :] = jnp.broadcast_to(like_weight * prob * (1.0 - prob), (CHUNK, HALF))
         weights.append(jnp.concatenate(two(like_weight * prob * hot), axis=1))
-    return tn(rows_ref[...], jnp.concatenate(weights, axis=0))
-
-
-def folded(total):
+    total = tn(rows_ref[start:stop, :], jnp.concatenate(weights, axis=0))
     return total[:, :HALF] + total[:, HALF:]
 
 
-def land_kernel(a, b, c, d, rows_ref, hot_ref, x_ref, tail_ref):
-    land(0, (a, b, c, d), rows_ref, hot_ref, tail_ref)
+def position_kernel(_, __, hot_ref, d, rows_ref, tail_ref, x_ref, grad_ref, curve_ref):
+    land(0, (None, None, None, d), (3,), rows_ref, tail_ref)
     for k in range(4):
         x_ref[cols(k), :] = tail_ref[:, cols(k)].T
-
-
-def grad_kernel(rows_ref, hot_ref, x_ref, grad_ref, curve_ref):
     x = x_ref[...]
-    both = jnp.concatenate(two(x), axis=1)
-    grad_ref[...] = folded(gradient(rows_ref, hot_ref, both, curve_ref)) - (
-        prior_precision + 2.0 / scale
-    ) * x
-
-
-def land_grad_kernel(color, a, b, c, d, x_ref, before_ref, rows_ref, hot_ref, grad_ref, curve_ref):
-    land(color, (a, b, c, d), rows_ref, hot_ref)
-    both = jnp.concatenate(two(x_ref[...]), axis=1)
-    grad_ref[...] = before_ref[...] + folded(gradient(rows_ref, hot_ref, both, curve_ref))
+    part = gradient(rows_ref, hot_ref, x, curve_ref, 0, ROWS[0])
+    grad_ref[...] = part - (prior_precision + 2.0 / scale) * x
+
+
+def grad_kernel(color, _, before_ref, __, hot_ref, x_ref, d, rows_ref, grad_ref, curve_ref):
+    land(color, (None, None, None, d), (3,), rows_ref, None)
+    start = STARTS[color]
+    part = gradient(rows_ref, hot_ref, x_ref[...], curve_ref, start, start + ROWS[color])
+    grad_ref[...] = before_ref[...] + part
 
 
 def factors(own_ref, other_ref):
@@ -229,8 +233,8 @@
 
 
 def next_kernel(
-    r0, r1, r2, h0, h1, h2, x_ref, drift_ref, image_a, image_b, own_ref, other_ref,
-    grad_ref, c0, c1, c2, new_ref, out_ref, turn_ref,
+    rows_ref, hot_ref, x_ref, drift_ref, image_a, image_b, own_ref, other_ref,
+    grad_ref, curve_ref, new_ref, out_ref, turn_ref,
 ):
     on_drift, on_image = factors(own_ref, other_ref)
     images = (image_a, image_b)
@@ -240,9 +244,8 @@
         update = on_drift * drift_ref[near, :] + on_image * image_ref[...]
         new_ref[near, :] = x_ref[near, :] + move_size * update
     x = new_ref[:, half_of(lax.axis_index("c"))]
-    both = jnp.concatenate(two(x), axis=1)
-    total = gradient(r0, h0, both, c0) + gradient(r1, h1, both, c1) + gradient(r2, h2, both, c2)
-    grad_ref[...] = folded(total) - (prior_precision + 2.0 / scale) * x
+    part = gradient(rows_ref, hot_ref, x, curve_ref, 0, HALF * DATA)
+    grad_ref[...] = part - (prior_precision + 2.0 / scale) * x
 
 
 def last_kernel(
@@ -273,24 +276,21 @@
     similarity(x_ref[...], kernel_ref)
 
 
-def spread(thirds, weighted_ref, near):
-    return sum(
-        tn(rows_ref[:, near], weighted_ref[k, span(color), :])
-        for color, rows_ref in enumerate(thirds)
-        for k in range(2)
-    )
-
-
-def image_part(thirds, near, x_ref, drift, square, q, weighted_ref):
+def spread(rows_ref, weighted_ref, near):
+    rows = rows_ref[:, near]
+    return tn(rows, weighted_ref[0]) + tn(rows, weighted_ref[1])
+
+
+def image_part(rows_ref, near, x_ref, drift, square, q, weighted_ref):
     mine = half_of(lax.axis_index("c"))
     pull = x_ref[near, :] * jnp.sum(q, axis=0, keepdims=True)
     pull = pull - stacked(two(x_ref[near, mine]), two(q))
     own = prior_precision * jnp.sum(square, axis=0, keepdims=True) * drift
-    return (spread(thirds, weighted_ref, near) + (own + cross * pull)) / MANY
+    return (spread(rows_ref, weighted_ref, near) + (own + cross * pull)) / MANY
 
 
 def first_kernel(
-    r0, r1, r2, c0, c1, c2, x_ref, kernel_ref, own_ref, other_ref,
+    rows_ref, curve_ref, x_ref, kernel_ref, own_ref, other_ref,
     drift_ref, image_ref, factor_ref, weighted_ref, q_ref, square_ref,
 ):
     core = lax.axis_index("c")
@@ -305,20 +305,19 @@
     kernel_own = kernel_ref[mine, :]
     square = kernel_own * kernel_own
     square_ref[...] = square
-    thirds = (r0, r1, r2)
-    for color, (rows_ref, curve_ref) in enumerate(zip(thirds, (c0, c1, c2))):
+    for color in range(3):
         count = ROWS[color] // 256
         for at in range(0, ROWS[color], CHUNK):
-            part, to = pl.ds(at, CHUNK), pl.ds(STARTS[color] + at, CHUNK)
+            to = pl.ds(STARTS[color] + at, CHUNK)
             pieces = []
             for group in range(at // DATA, (at + CHUNK) // DATA):
                 j = group // count * 8 + FIRSTS[color] + group % count
-                curve = curve_ref[pl.ds(group * DATA, DATA), :]
+                curve = curve_ref[pl.ds(STARTS[color] + group * DATA, DATA), :]
                 wide = jnp.concatenate([curve, curve], axis=1)
                 pieces.append(jnp.broadcast_to(square_ref[j : j + 1, :], wide.shape) * wide)
             factor = jnp.concatenate(pieces, axis=0)
             factor_ref[to, :] = factor
-            rows = rows_ref[part, :]
+            rows = rows_ref[to, :]
             high, low = two((nn(rows, drift_two[0]) + nn(rows, drift_two[1])) * factor)
             weighted_ref[0, to, :] = high
             weighted_ref[1, to, :] = low
@@ -326,14 +325,14 @@
     q = square * (jnp.sum(x * drift, axis=0, keepdims=True) - along)
     q_ref[...] = q
     near = slice(0, WIDE // 2)
-    image_ref[...] = image_part(thirds, near, x_ref, drift[near], square, q, weighted_ref)
-
-
-def rest_kernel(r0, r1, r2, x_ref, kernel_ref, drift_ref, weighted_ref, q_ref, image_ref):
+    image_ref[...] = image_part(rows_ref, near, x_ref, drift[near], square, q, weighted_ref)
+
+
+def rest_kernel(rows_ref, x_ref, kernel_ref, drift_ref, weighted_ref, q_ref, image_ref):
     kernel_own = kernel_ref[half_of(lax.axis_index("c")), :]
     near = slice(WIDE // 2, WIDE)
     image_ref[...] = image_part(
-        (r0, r1, r2), near, x_ref, drift_ref[near, :], kernel_own * kernel_own, q_ref[...],
+        rows_ref, near, x_ref, drift_ref[near, :], kernel_own * kernel_own, q_ref[...],
         weighted_ref,
     )
 
@@ -355,7 +354,7 @@
 
 
 def second_kernel(
-    r0, r1, r2, x_ref, drift_ref, own_ref, other_ref,
+    rows_ref, x_ref, drift_ref, own_ref, other_ref,
     image_ref, projected_ref, along_ref, sums_ref,
 ):
     near = slice(0, WIDE // 2)
@@ -366,12 +365,11 @@
     for at, value in enumerate(sums):
         sums_ref[at : at + 1, :] = value
     sums_ref[6:, :] = jnp.zeros((2, MANY), f32)
-    for color, rows_ref in enumerate((r0, r1, r2)):
-        projected_ref[span(color), :] = nn(rows_ref[:, near], rounded)
+    projected_ref[...] = nn(rows_ref[:, near], rounded)
 
 
 def third_kernel(
-    r0, r1, r2, x_ref, kernel_ref, factor_ref, drift_ref, projected_ref, along_ref, before_ref,
+    rows_ref, x_ref, kernel_ref, factor_ref, drift_ref, projected_ref, along_ref, before_ref,
     own_ref, other_ref,
     image_ref, sums_ref,
 ):
@@ -381,11 +379,10 @@
     sums, along, rounded = read_image(near, x_ref, drift_ref, image)
     sums = [value + before_ref[at : at + 1, :] for at, value in enumerate(sums)]
     total = jnp.zeros((1, MANY), f32)
-    for color, rows_ref in enumerate((r0, r1, r2)):
-        for at in range(0, ROWS[color], CHUNK):
-            to = pl.ds(STARTS[color] + at, CHUNK)
-            projected = projected_ref[to, :] + nn(rows_ref[pl.ds(at, CHUNK), near], rounded)
-            total += jnp.sum(projected * projected * factor_ref[to, :], axis=0, keepdims=True)
+    for at in range(0, HALF * DATA, CHUNK):
+        to = pl.ds(at, CHUNK)
+        projected = projected_ref[to, :] + nn(rows_ref[to, near], rounded)
+        total += jnp.sum(projected * projected * factor_ref[to, :], axis=0, keepdims=True)
     fit = sums[3] / jnp.maximum(sums[4], 1e-30)
     total *= fit * fit
     mine = half_of(lax.axis_index("c"))
@@ -400,7 +397,7 @@
     sums_ref[4:, :] = jnp.zeros((4, HALF), f32)
 
 
-def call(kernel, outs, *args, scratch=(), far=False):
+def call(kernel, outs, *args, scratch=(), far=False, aliases=None):
     whole = pl.BlockSpec(memory_space=pltpu.VMEM)
     return pl.pallas_call(
         kernel,
@@ -408,6 +405,7 @@
         in_specs=[pl.BlockSpec(memory_space=pltpu.HBM) if far else whole] * len(args),
         out_specs=[whole] * len(outs),
         scratch_shapes=scratch,
+        input_output_aliases=aliases or {},
         compiler_params=pltpu.CompilerParams(vmem_limit_bytes=(60 if far else 24) * 1024 * 1024),
     )(*args)
 
@@ -434,28 +432,34 @@
     low = ((HALF, MANY), f32)
     half = ((WIDE, HALF), f32)
     turn = [pltpu.VMEM((HALF, SLICE), f32)]
-    rows_of = [((r, WIDE), bf16) for r in ROWS]
-    hot_of = [((r, HALF), bf16) for r in ROWS]
-    curve_of = [((r, HALF), f32) for r in ROWS]
-    rows, hot, curve = [None] * 3, [None] * 3, [None] * 3
-    rows[0], hot[0], x_own = call(
-        land_kernel, [rows_of[0], hot_of[0], half], *pieces[0],
-        scratch=[pltpu.VMEM((HALF, WIDE), f32)],
+    rows_of = ((count, WIDE), bf16)
+    tail_of = ((HALF, WIDE), f32)
+    curve_of = ((count, HALF), f32)
+    rows, tail, hot = call(
+        early_kernel,
+        [rows_of, tail_of, ((count, HALF), bf16)],
+        *(a for four in pieces for a in four[:3]),
+    )
+    rows, tail, x_own, grad, curve = call(
+        position_kernel,
+        [rows_of, tail_of, half, half, curve_of],
+        rows, tail, hot, pieces[0][3],
+        aliases={0: 0, 1: 1},
     )
     x_other = swap_cores(x_own)
-    grad, curve[0] = call(grad_kernel, [half, curve_of[0]], rows[0], hot[0], x_own)
+    for color in (1, 2):
+        rows, grad, curve = call(
+            partial(grad_kernel, color),
+            [rows_of, half, curve_of],
+            rows, grad, curve, hot, x_own, pieces[color][3],
+            aliases={0: 0, 1: 1, 2: 2},
+        )
     kernel, x = call(start_kernel, [square, long], x_own, x_other)
-    for color in (1, 2):
-        rows[color], hot[color], grad, curve[color] = call(
-            partial(land_grad_kernel, color),
-            [rows_of[color], hot_of[color], half, curve_of[color]],
-            *pieces[color], x_own, grad,
-        )
     for newton_step in range(NEWTON):
         if newton_step > 0:
-            grad, *curve, x, update = call(
-                next_kernel, [half, *curve_of, long, ((8, SLICE), f32)],
-                *rows, *hot, x, drift, *image, sums, sums_other, scratch=turn,
+            grad, curve, x, update = call(
+                next_kernel, [half, curve_of, long, ((8, SLICE), f32)],
+                rows, hot, x, drift, *image, sums, sums_other, scratch=turn,
             )
         grad_other = swap_cores(grad)
         if newton_step > 0:
@@ -463,19 +467,19 @@
         drift, own_a, factor, weighted, q = call(
             first_kernel,
             [long, wing, tall, ((2, count, MANY), bf16), low],
-            *rows, *curve, x, kernel, grad, grad_other,
+            rows, curve, x, kernel, grad, grad_other,
             scratch=[pltpu.VMEM((HALF, MANY), f32)],
         )
         other_a = swap_cores(own_a)
-        (own_b,) = call(rest_kernel, [wing], *rows, x, kernel, drift, weighted, q)
+        (own_b,) = call(rest_kernel, [wing], rows, x, kernel, drift, weighted, q)
         other_b = swap_cores(own_b)
         image_a, projected, along, partial_sums = call(
             second_kernel, [wing, tall, low, ((8, MANY), f32)],
-            *rows, x, drift, own_a, other_a,
+            rows, x, drift, own_a, other_a,
         )
         image_b, sums = call(
             third_kernel, [wing, ((8, HALF), f32)],
-            *rows, x, kernel, factor, drift, projected, along, partial_sums, own_b, other_b,
+            rows, x, kernel, factor, drift, projected, along, partial_sums, own_b, other_b,
         )
         image = (image_a, image_b)
         sums_other = swap_cores(sums)

time: 85.8 us -> 81 us (0.944)
  waiting for transfers between devices: 22.3 us -> 19.3 us
  starting transfers between devices: 11.6 us -> 10.2 us
    ppermute x12, waiting for transfers between devices: 17.3 us -> 14.4 us  [sent(): out.append(lax.ppermute(part, AXES, pairs(order[step])))]
    ppermute x9, starting transfers between devices: 6.31 us -> 5.03 us  [swap_cores(): return lax.ppermute(x, 'c', [(0, 1), (1, 0)])]
  transfers between devices with their start and end apart: 21 -> 21, of which waited for: 12 -> 14; matrix products, arithmetic and copies ran while one was open for 0% -> 0% of each run, Pallas kernels for 13% -> 13%
where the time goes in v2:
time: 81 us; the launch traced here: 80.8 us
  Pallas kernels  29.2 us (36%)
  blocking collectives  21.7 us (27%)
  waiting for transfers between devices  19.3 us (24%)
  starting transfers between devices  10.2 us (13%)
    pallas_call x17, Pallas kernels, call(): pl.pallas_call(kernel, out_shape=[jax.ShapeDtypeStruct(s, t) for s, t in...  29.2 us
    all_to_all x1, blocking collectives, gathered(): lax.all_to_all(copies, AXES, 0, 0, axis_index_groups=cubes(), tiled=True)  21.7 us
    ppermute x12, waiting for transfers between devices, sent(): out.append(lax.ppermute(part, AXES, pairs(order[step])))  14.4 us
    ppermute x12, starting transfers between devices, sent(): out.append(lax.ppermute(part, AXES, pairs(order[step])))  5.18 us
    ppermute x9, starting transfers between devices, swap_cores(): return lax.ppermute(x, 'c', [(0, 1), (1, 0)])  5.03 us
    ppermute x9, waiting for transfers between devices, swap_cores(): return lax.ppermute(x, 'c', [(0, 1), (1, 0)])  4.97 us
  transfers between devices with their start and end apart: 21, of which 14 were waited for; matrix products, arithmetic and copies ran while one was open for 0% of the time, Pallas kernels for 13%

profile of v2, /device:TPU:1, one launch (start us, length us, event | category | flops | bytes accessed | tf_op | source)
XLA Modules:
  0.0 80.8 jit_solution(3698124035397843725)
XLA Ops:
  0.0 1.9 %shard_map.37 = bf16[8,144,256]{2,1,0:T(8,128)(2,1)} custom-call(f32[8,256]{1,0:T(8,128)} %x_far.1, bf16[8,16,256]{2,1,0:T(8,128)(2,1)} %rows_far.1, s32[8,16]{1,0:T(8,128)} %labels_far.1), custom_call_target="tpu_custom_call" | custom-call | tf_op jit(solution)/shard_map/pallas_call | solution.py:402
  1.9 21.7 %all_to_all.5 = bf16[8,144,256]{2,1,0:T(8,128)(2,1)S(1)} all-to-all(bf16[8,144,256]{2,1,0:T(8,128)(2,1)} %shard_map.37), channel_id=1, replica_groups={{0,1,8,9,32,33,40,41},{2,3,10,11,34,35,42,43},{4,7,28,31,100,103,124,12..., dimensions={0} | all-to-all | bytes 1179648 | tf_op jit(solution)/shard_map/all_to_all | solution.py:70
  23.6 0.1 collective-permute-start
  23.7 0.1 collective-permute-start.3
  23.8 0.1 collective-permute-start.6
  23.9 4.3 %collective-permute-done = bf16[8,48,256]{2,1,0:T(8,128)(2,1)S(1)} collective-permute-done((bf16[8,48,256]{2,1,0:T(8,128)(2,1)S(1)}, bf16[8,48,256]{2,1,0:T(8,128)(2,1)S(1)}, u32[]{:S(2)}, u32[]{:S(2)}) %collective-permute-start) | collective-permute-done | bytes 196640 | tf_op jit(solution)/shard_map/ppermute | solution.py:76
  28.3 0.1 collective-permute-start.2
  28.4 0.1 collective-permute-start.1
  28.5 0.0 collective-permute-done.3
  28.5 1.4 %collective-permute-start.4 = (bf16[16,48,256]{2,1,0:T(8,128)(2,1)S(1)}, bf16[16,48,256]{2,1,0:T(8,128)(2,1)S(1)}, u32[]{:S(2)}, u32[]{:S(2)}) collective-permute-start(bf16[16,48,256]{2,1,0:T(8,128)(2,1)S(1)} %pad_maximum_fusion.1.refs_3_), channel_id=1, source_target_pairs={{0,3},{1,2},{2,1},{3,0},{4,5},{5,4},{6,7},{7,6},{8,11},{9,10},{10,... | collective-permute-start | bytes 1179656 | tf_op jit(solution)/shard_map/ppermute | solution.py:76
  30.0 0.0 collective-permute-done.6
  30.0 0.3 collective-permute-start.7
  30.3 1.3 %collective-permute-start.5 = (bf16[16,48,256]{2,1,0:T(8,128)(2,1)S(1)}, bf16[16,48,256]{2,1,0:T(8,128)(2,1)S(1)}, u32[]{:S(2)}, u32[]{:S(2)}) collective-permute-start(bf16[16,48,256]{2,1,0:T(8,128)(2,1)S(1)} %pad_maximum_fusion.1.refs_3_), channel_id=1, source_target_pairs={{0,24},{1,25},{2,26},{3,27},{4,12},{5,13},{6,14},{7,15},{8,16},{9,... | collective-permute-start | bytes 1179656 | tf_op jit(solution)/shard_map/ppermute | solution.py:76
  31.5 3.7 %collective-permute-done.2.refs_2_ = bf16[16,48,256]{2,1,0:T(8,128)(2,1)S(1)} collective-permute-done((bf16[16,48,256]{2,1,0:T(8,128)(2,1)S(1)}, bf16[16,48,256]{2,1,0:T(8,128)(2,1)S(1)}, u32[]{:S(2)}, u32[]{:S(2)}) %collective-permute-start.2) | collective-permute-done | bytes 393248 | tf_op jit(solution)/shard_map/ppermute | solution.py:76
  35.3 0.0 collective-permute-start.8
  35.3 0.1 collective-permute-done.1.refs_1_
  35.4 1.4 %collective-permute-start.9 = (bf16[16,48,256]{2,1,0:T(8,128)(2,1)S(1)}, bf16[16,48,256]{2,1,0:T(8,128)(2,1)S(1)}, u32[]{:S(2)}, u32[]{:S(2)}) collective-permute-start(bf16[16,48,256]{2,1,0:T(8,128)(2,1)S(1)} %collective-permute-done.1.refs_1_), channel_id=1, source_target_pairs={{0,3},{1,2},{2,1},{3,0},{4,5},{5,4},{6,7},{7,6},{8,11},{9,10},{10,... | collective-permute-start | bytes 1179656 | tf_op jit(solution)/shard_map/ppermute | solution.py:76
  36.8 2.7 %collective-permute-done.4.refs_4_ = bf16[16,48,256]{2,1,0:T(8,128)(2,1)S(1)} collective-permute-done((bf16[16,48,256]{2,1,0:T(8,128)(2,1)S(1)}, bf16[16,48,256]{2,1,0:T(8,128)(2,1)S(1)}, u32[]{:S(2)}, u32[]{:S(2)}) %collective-permute-start.4) | collective-permute-done | bytes 393248 | tf_op jit(solution)/shard_map/ppermute | solution.py:76
  39.5 0.0 collective-permute-start.10
  39.5 0.0 collective-permute-done.7.refs_7_
  39.5 0.4 collective-permute-start.11
  39.9 1.3 %collective-permute-done.5.refs_5_ = bf16[16,48,256]{2,1,0:T(8,128)(2,1)S(1)} collective-permute-done((bf16[16,48,256]{2,1,0:T(8,128)(2,1)S(1)}, bf16[16,48,256]{2,1,0:T(8,128)(2,1)S(1)}, u32[]{:S(2)}, u32[]{:S(2)}) %collective-permute-start.5) | collective-permute-done | bytes 393248 | tf_op jit(solution)/shard_map/ppermute | solution.py:76
  41.2 1.0 %collective-permute-done.8.refs_8_ = bf16[16,48,256]{2,1,0:T(8,128)(2,1)S(1)} collective-permute-done((bf16[16,48,256]{2,1,0:T(8,128)(2,1)S(1)}, bf16[16,48,256]{2,1,0:T(8,128)(2,1)S(1)}, u32[]{:S(2)}, u32[]{:S(2)}) %collective-permute-start.8) | collective-permute-done | bytes 393248 | tf_op jit(solution)/shard_map/ppermute | solution.py:76
  42.2 0.7 shard_map.38
  42.9 0.8 collective-permute-done.9.d
  43.7 1.1 %shard_map.39 = (bf16[2048,1024]{1,0:T(8,128)(2,1)S(1)}, f32[128,1024]{1,0:T(8,128)S(1)}, f32[1024,128]{1,0:T(8,128)S(1)}, f32[1024,128]{1,0:T(8,128)S(1)}, f32[2048,128]{1,0:T(8,128)S(1)}) custom-call(bf16[2048,1024]{1,0:T(8,128)(2,1)S(1)} %get-tuple-element.46._, ...), custom_call_target="tpu_custom_call", output_to_operand_aliasing={{0}: (0, {}), {1}: (1, {})} | custom-call | tf_op jit(solution)/shard_map/pallas_call | solution.py:402
  44.8 1.2 %collective-permute-start.12 = (f32[1024,128]{1,0:T(8,128)S(1)}, f32[1024,128]{1,0:T(8,128)S(1)}, u32[]{:S(2)}, u32[]{:S(2)}) collective-permute-start(f32[1024,128]{1,0:T(8,128)S(1)} %get-tuple-element.52.x_ref.own_ref), channel_id=1, source_target_pairs={{0,4},{4,0},{1,5},{5,1},{2,6},{6,2},{3,7},{7,3},{8,12},{12,8},{9,1... | collective-permute-start | bytes 1572872 | tf_op jit(solution)/shard_map/ppermute | solution.py:66
  46.1 0.4 collective-permute-done.10.d
  46.4 1.3 %shard_map.40 = (bf16[2048,1024]{1,0:T(8,128)(2,1)S(1)}, f32[1024,128]{1,0:T(8,128)S(1)}, f32[2048,128]{1,0:T(8,128)S(1)}) custom-call(bf16[2048,1024]{1,0:T(8,128)(2,1)S(1)} %get-tuple-element.49._, f32[1024,128]{1,0:T(8,128)S(1)} %get-tuple-element.50.before_ref, ...), custom_call_target="tpu_custom_call", output_to_operand_aliasing={{0}: (0, {}), {1}: (1, {}), {2}: (2, {})} | custom-call | tf_op jit(solution)/shard_map/pallas_call | solution.py:402
  47.7 0.0 collective-permute-done.11.d
  47.7 1.3 %shard_map.41 = (bf16[2048,1024]{1,0:T(8,128)(2,1)S(1)}, f32[1024,128]{1,0:T(8,128)S(1)}, f32[2048,128]{1,0:T(8,128)S(1)}) custom-call(bf16[2048,1024]{1,0:T(8,128)(2,1)S(1)} %get-tuple-element.53._, f32[1024,128]{1,0:T(8,128)S(1)} %get-tuple-element.54.before_ref, ...), custom_call_target="tpu_custom_call", output_to_operand_aliasing={{0}: (0, {}), {1}: (1, {}), {2}: (2, {})} | custom-call | tf_op jit(solution)/shard_map/pallas_call | solution.py:402
  49.0 1.5 %collective-permute-start.13 = (f32[1024,128]{1,0:T(8,128)S(1)}, f32[1024,128]{1,0:T(8,128)S(1)}, u32[]{:S(2)}, u32[]{:S(2)}) collective-permute-start(f32[1024,128]{1,0:T(8,128)S(1)} %get-tuple-element.60.own_ref), channel_id=1, source_target_pairs={{0,4},{4,0},{1,5},{5,1},{2,6},{6,2},{3,7},{7,3},{8,12},{12,8},{9,1... | collective-permute-start | bytes 1572872 | tf_op jit(solution)/shard_map/ppermute | solution.py:66
  50.5 0.0 collective-permute-done.12.other_ref
  50.5 0.8 shard_map.42
  51.3 0.8 collective-permute-done.13.other_ref
  52.1 5.2 %shard_map.43 = (f32[1024,256]{1,0:T(8,128)S(1)}, f32[512,256]{1,0:T(8,128)S(1)}, f32[2048,256]{1,0:T(8,128)S(1)}, bf16[2,2048,256]{2,1,0:T(8,128)(2,1)S(1)}, f32[128,256]{1,0:T(8,128)S(1)}) custom-call(bf16[2048,1024]{1,0:T(8,128)(2,1)S(1)} %get-tuple-element.56.rows_ref, f32[2048,128]{1,0:T(8,128)S(1)} %get-tuple-element.58.curve_ref, ...), custom_call_target="tpu_custom_call" | custom-call | tf_op jit(solution)/shard_map/pallas_call | solution.py:402
  57.3 0.4 collective-permute-start.14
  57.7 1.4 %shard_map.45.own_ref = f32[512,256]{1,0:T(8,128)S(1)} custom-call(bf16[2048,1024]{1,0:T(8,128)(2,1)S(1)} %get-tuple-element.56.rows_ref, f32[1024,256]{1,0:T(8,128)S(1)} %get-tuple-element.57.x_ref, f32[256,256]{1,0:T(8,128)S(1)} %get-tuple-element.59.kernel_ref, f32[1024,256]{1,0:T(8,128)S(1)} %get-tuple-element.61.drift_ref, ...), custom_call_target="tpu_custom_call" | custom-call | tf_op jit(solution)/shard_map/pallas_call | solution.py:402
  59.2 0.2 collective-permute-start.15
  59.4 0.0 collective-permute-done.14.other_ref
  59.4 1.0 %shard_map.44 = (f32[512,256]{1,0:T(8,128)S(1)}, f32[2048,256]{1,0:T(8,128)S(1)}, f32[128,256]{1,0:T(8,128)S(1)}, f32[8,256]{1,0:T(8,128)S(1)}) custom-call(bf16[2048,1024]{1,0:T(8,128)(2,1)S(1)} %get-tuple-element.56.rows_ref, f32[1024,256]{1,0:T(8,128)S(1)} %get-tuple-element.57.x_ref, f32[1024,256]{1,0:T(8,128)S(1)} %get-tuple-element.61.drift_ref, ...), custom_call_target="tpu_custom_call" | custom-call | tf_op jit(solution)/shard_map/pallas_call | solution.py:402
  60.4 0.8 collective-permute-done.15.other_ref
  61.2 1.2 %shard_map.46 = (f32[512,256]{1,0:T(8,128)S(1)}, f32[8,128]{1,0:T(8,128)S(1)}) custom-call(bf16[2048,1024]{1,0:T(8,128)(2,1)S(1)} %get-tuple-element.56.rows_ref, f32[1024,256]{1,0:T(8,128)S(1)} %get-tuple-element.57.x_ref, f32[256,256]{1,0:T(8,128)S(1)} %get-tuple-element.59.kernel_ref, f32[2048,256]{1,0:T(8,128)S(1)} %get-tuple-element.64.factor_ref, ...), custom_call_target="tpu_custom_call" | custom-call | tf_op jit(solution)/shard_map/pallas_call | solution.py:402
  62.4 0.1 collective-permute-start.16
  62.6 1.0 %collective-permute-done.16.other_ref = f32[8,128]{1,0:T(8,128)S(1)} collective-permute-done((f32[8,128]{1,0:T(8,128)S(1)}, f32[8,128]{1,0:T(8,128)S(1)}, u32[]{:S(2)}, u32[]{:S(2)}) %collective-permute-start.16) | collective-permute-done | bytes 4128 | tf_op jit(solution)/shard_map/ppermute | solution.py:66
  63.6 2.9 %shard_map.47 = (f32[1024,128]{1,0:T(8,128)S(1)}, f32[2048,128]{1,0:T(8,128)S(1)}, f32[1024,256]{1,0:T(8,128)S(1)}, f32[8,256]{1,0:T(8,128)S(1)}) custom-call(bf16[2048,1024]{1,0:T(8,128)(2,1)S(1)} %get-tuple-element.56.rows_ref, bf16[2048,128]{1,0:T(8,128)(2,1)S(1)} %get-tuple-element.48.hot_ref, f32[1024,256]{1,0:T(8,128)S(1)} %get-tuple-element.57.x_ref, ...), custom_call_target="tpu_custom_call" | custom-call | tf_op jit(solution)/shard_map/pallas_call | solution.py:402
  66.5 0.4 collective-permute-start.17
  67.0 0.7 shard_map.48.kernel_ref
  67.7 1.1 %collective-permute-done.17.other_ref = f32[1024,128]{1,0:T(8,128)S(1)} collective-permute-done((f32[1024,128]{1,0:T(8,128)S(1)}, f32[1024,128]{1,0:T(8,128)S(1)}, u32[]{:S(2)}, u32[]{:S(2)}) %collective-permute-start.17) | collective-permute-done | bytes 524320 | tf_op jit(solution)/shard_map/ppermute | solution.py:66
  68.8 5.2 %shard_map.49 = (f32[1024,256]{1,0:T(8,128)S(1)}, f32[512,256]{1,0:T(8,128)S(1)}, f32[2048,256]{1,0:T(8,128)S(1)}, bf16[2,2048,256]{2,1,0:T(8,128)(2,1)S(1)}, f32[128,256]{1,0:T(8,128)S(1)}) custom-call(bf16[2048,1024]{1,0:T(8,128)(2,1)S(1)} %get-tuple-element.56.rows_ref, f32[2048,128]{1,0:T(8,128)S(1)} %get-tuple-element.72.curve_ref, ...), custom_call_target="tpu_custom_call" | custom-call | tf_op jit(solution)/shard_map/pallas_call | solution.py:402
  74.0 0.2 collective-permute-start.18
  74.2 1.4 %shard_map.51.own_ref = f32[512,256]{1,0:T(8,128)S(1)} custom-call(bf16[2048,1024]{1,0:T(8,128)(2,1)S(1)} %get-tuple-element.56.rows_ref, f32[1024,256]{1,0:T(8,128)S(1)} %get-tuple-element.73.x_ref, f32[256,256]{1,0:T(8,128)S(1)} %shard_map.48.kernel_ref, f32[1024,256]{1,0:T(8,128)S(1)} %get-tuple-element.75.drift_ref, ...), custom_call_target="tpu_custom_call" | custom-call | tf_op jit(solution)/shard_map/pallas_call | solution.py:402
  75.6 0.5 collective-permute-start.19
  76.1 0.0 collective-permute-done.18.other_ref
  76.1 1.0 %shard_map.50 = (f32[512,256]{1,0:T(8,128)S(1)}, f32[2048,256]{1,0:T(8,128)S(1)}, f32[128,256]{1,0:T(8,128)S(1)}, f32[8,256]{1,0:T(8,128)S(1)}) custom-call(bf16[2048,1024]{1,0:T(8,128)(2,1)S(1)} %get-tuple-element.56.rows_ref, f32[1024,256]{1,0:T(8,128)S(1)} %get-tuple-element.73.x_ref, f32[1024,256]{1,0:T(8,128)S(1)} %get-tuple-element.75.drift_ref, ...), custom_call_target="tpu_custom_call" | custom-call | tf_op jit(solution)/shard_map/pallas_call | solution.py:402
  77.1 0.5 collective-permute-done.19.other_ref
  77.6 1.2 %shard_map.52 = (f32[512,256]{1,0:T(8,128)S(1)}, f32[8,128]{1,0:T(8,128)S(1)}) custom-call(bf16[2048,1024]{1,0:T(8,128)(2,1)S(1)} %get-tuple-element.56.rows_ref, f32[1024,256]{1,0:T(8,128)S(1)} %get-tuple-element.73.x_ref, f32[256,256]{1,0:T(8,128)S(1)} %shard_map.48.kernel_ref, f32[2048,256]{1,0:T(8,128)S(1)} %get-tuple-element.78.factor_ref, ...), custom_call_target="tpu_custom_call" | custom-call | tf_op jit(solution)/shard_map/pallas_call | solution.py:402
  78.8 0.4 collective-permute-start.20
  79.2 0.8 %collective-permute-done.20.other_ref = f32[8,128]{1,0:T(8,128)S(1)} collective-permute-done((f32[8,128]{1,0:T(8,128)S(1)}, f32[8,128]{1,0:T(8,128)S(1)}, u32[]{:S(2)}, u32[]{:S(2)}) %collective-permute-start.20) | collective-permute-done | bytes 4128 | tf_op jit(solution)/shard_map/ppermute | solution.py:66
  80.0 0.8 shard_map.53
  (4 shorter events, 0.1 us)
Async XLA Ops:
  23.6 4.6 %collective-permute-start = (bf16[8,48,256]{2,1,0:T(8,128)(2,1)S(1)}, bf16[8,48,256]{2,1,0:T(8,128)(2,1)S(1)}, u32[]{:S(2)}, u32[]{:S(2)}) collective-permute-start(bf16[8,48,256]{2,1,0:T(8,128)(2,1)S(1)} %get-tuple-element.89), channel_id=1, source_target_pairs={{0,24},{1,25},{2,26},{3,27},{4,12},{5,13},{6,14},{7,15},{8,16},{9,... | collective-permute-start | bytes 589832 | tf_op jit(solution)/shard_map/ppermute | solution.py:76
  23.7 4.7 %collective-permute-start.3 = (bf16[8,48,256]{2,1,0:T(8,128)(2,1)S(1)}, bf16[8,48,256]{2,1,0:T(8,128)(2,1)S(1)}, u32[]{:S(2)}, u32[]{:S(2)}) collective-permute-start(bf16[8,48,256]{2,1,0:T(8,128)(2,1)S(1)} %get-tuple-element.88), channel_id=1, source_target_pairs={{0,96},{1,97},{2,98},{3,99},{4,36},{5,37},{6,38},{7,39},{8,104},{9... | collective-permute-start | bytes 589832 | tf_op jit(solution)/shard_map/ppermute | solution.py:76
  23.8 6.1 %collective-permute-start.6 = (bf16[8,48,256]{2,1,0:T(8,128)(2,1)S(1)}, bf16[8,48,256]{2,1,0:T(8,128)(2,1)S(1)}, u32[]{:S(2)}, u32[]{:S(2)}) collective-permute-start(bf16[8,48,256]{2,1,0:T(8,128)(2,1)S(1)} %get-tuple-element.87), channel_id=1, source_target_pairs={{0,3},{1,2},{2,1},{3,0},{4,5},{5,4},{6,7},{7,6},{8,11},{9,10},{10,... | collective-permute-start | bytes 589832 | tf_op jit(solution)/shard_map/ppermute | solution.py:76
  28.3 7.0 %collective-permute-start.2 = (bf16[16,48,256]{2,1,0:T(8,128)(2,1)S(1)}, bf16[16,48,256]{2,1,0:T(8,128)(2,1)S(1)}, u32[]{:S(2)}, u32[]{:S(2)}) collective-permute-start(bf16[16,48,256]{2,1,0:T(8,128)(2,1)S(1)} %pad_maximum_fusion.refs_0_), channel_id=1, source_target_pairs={{0,3},{1,2},{2,1},{3,0},{4,5},{5,4},{6,7},{7,6},{8,11},{9,10},{10,... | collective-permute-start | bytes 1179656 | tf_op jit(solution)/shard_map/ppermute | solution.py:76
  28.4 7.0 %collective-permute-start.1 = (bf16[16,48,256]{2,1,0:T(8,128)(2,1)S(1)}, bf16[16,48,256]{2,1,0:T(8,128)(2,1)S(1)}, u32[]{:S(2)}, u32[]{:S(2)}) collective-permute-start(bf16[16,48,256]{2,1,0:T(8,128)(2,1)S(1)} %pad_maximum_fusion.refs_0_), channel_id=1, source_target_pairs={{0,96},{1,97},{2,98},{3,99},{4,36},{5,37},{6,38},{7,39},{8,104},{9... | collective-permute-start | bytes 1179656 | tf_op jit(solution)/shard_map/ppermute | solution.py:76
  28.5 11.0 %collective-permute-start.4 = (bf16[16,48,256]{2,1,0:T(8,128)(2,1)S(1)}, bf16[16,48,256]{2,1,0:T(8,128)(2,1)S(1)}, u32[]{:S(2)}, u32[]{:S(2)}) collective-permute-start(bf16[16,48,256]{2,1,0:T(8,128)(2,1)S(1)} %pad_maximum_fusion.1.refs_3_), channel_id=1, source_target_pairs={{0,3},{1,2},{2,1},{3,0},{4,5},{5,4},{6,7},{7,6},{8,11},{9,10},{10,... | collective-permute-start | bytes 1179656 | tf_op jit(solution)/shard_map/ppermute | solution.py:76
  30.0 9.5 %collective-permute-start.7 = (bf16[16,48,256]{2,1,0:T(8,128)(2,1)S(1)}, bf16[16,48,256]{2,1,0:T(8,128)(2,1)S(1)}, u32[]{:S(2)}, u32[]{:S(2)}) collective-permute-start(bf16[16,48,256]{2,1,0:T(8,128)(2,1)S(1)} %pad_maximum_fusion.2.refs_6_), channel_id=1, source_target_pairs={{0,24},{1,25},{2,26},{3,27},{4,12},{5,13},{6,14},{7,15},{8,16},{9,... | collective-permute-start | bytes 1179656 | tf_op jit(solution)/shard_map/ppermute | solution.py:76
  30.3 10.9 %collective-permute-start.5 = (bf16[16,48,256]{2,1,0:T(8,128)(2,1)S(1)}, bf16[16,48,256]{2,1,0:T(8,128)(2,1)S(1)}, u32[]{:S(2)}, u32[]{:S(2)}) collective-permute-start(bf16[16,48,256]{2,1,0:T(8,128)(2,1)S(1)} %pad_maximum_fusion.1.refs_3_), channel_id=1, source_target_pairs={{0,24},{1,25},{2,26},{3,27},{4,12},{5,13},{6,14},{7,15},{8,16},{9,... | collective-permute-start | bytes 1179656 | tf_op jit(solution)/shard_map/ppermute | solution.py:76
  35.3 6.9 %collective-permute-start.8 = (bf16[16,48,256]{2,1,0:T(8,128)(2,1)S(1)}, bf16[16,48,256]{2,1,0:T(8,128)(2,1)S(1)}, u32[]{:S(2)}, u32[]{:S(2)}) collective-permute-start(bf16[16,48,256]{2,1,0:T(8,128)(2,1)S(1)} %pad_maximum_fusion.2.refs_6_), channel_id=1, source_target_pairs={{0,96},{1,97},{2,98},{3,99},{4,36},{5,37},{6,38},{7,39},{8,104},{9... | collective-permute-start | bytes 1179656 | tf_op jit(solution)/shard_map/ppermute | solution.py:76
  35.4 8.3 %collective-permute-start.9 = (bf16[16,48,256]{2,1,0:T(8,128)(2,1)S(1)}, bf16[16,48,256]{2,1,0:T(8,128)(2,1)S(1)}, u32[]{:S(2)}, u32[]{:S(2)}) collective-permute-start(bf16[16,48,256]{2,1,0:T(8,128)(2,1)S(1)} %collective-permute-done.1.refs_1_), channel_id=1, source_target_pairs={{0,3},{1,2},{2,1},{3,0},{4,5},{5,4},{6,7},{7,6},{8,11},{9,10},{10,... | collective-permute-start | bytes 1179656 | tf_op jit(solution)/shard_map/ppermute | solution.py:76
  39.5 6.9 %collective-permute-start.10 = (bf16[16,48,256]{2,1,0:T(8,128)(2,1)S(1)}, bf16[16,48,256]{2,1,0:T(8,128)(2,1)S(1)}, u32[]{:S(2)}, u32[]{:S(2)}) collective-permute-start(bf16[16,48,256]{2,1,0:T(8,128)(2,1)S(1)} %collective-permute-done.4.refs_4_), channel_id=1, source_target_pairs={{0,24},{1,25},{2,26},{3,27},{4,12},{5,13},{6,14},{7,15},{8,16},{9,... | collective-permute-start | bytes 1179656 | tf_op jit(solution)/shard_map/ppermute | solution.py:76
  39.5 8.2 %collective-permute-start.11 = (bf16[16,48,256]{2,1,0:T(8,128)(2,1)S(1)}, bf16[16,48,256]{2,1,0:T(8,128)(2,1)S(1)}, u32[]{:S(2)}, u32[]{:S(2)}) collective-permute-start(bf16[16,48,256]{2,1,0:T(8,128)(2,1)S(1)} %collective-permute-done.7.refs_7_), channel_id=1, source_target_pairs={{0,96},{1,97},{2,98},{3,99},{4,36},{5,37},{6,38},{7,39},{8,104},{9... | collective-permute-start | bytes 1179656 | tf_op jit(solution)/shard_map/ppermute | solution.py:76
  44.8 5.7 %collective-permute-start.12 = (f32[1024,128]{1,0:T(8,128)S(1)}, f32[1024,128]{1,0:T(8,128)S(1)}, u32[]{:S(2)}, u32[]{:S(2)}) collective-permute-start(f32[1024,128]{1,0:T(8,128)S(1)} %get-tuple-element.52.x_ref.own_ref), channel_id=1, source_target_pairs={{0,4},{4,0},{1,5},{5,1},{2,6},{6,2},{3,7},{7,3},{8,12},{12,8},{9,1... | collective-permute-start | bytes 1572872 | tf_op jit(solution)/shard_map/ppermute | solution.py:66
  49.0 3.0 %collective-permute-start.13 = (f32[1024,128]{1,0:T(8,128)S(1)}, f32[1024,128]{1,0:T(8,128)S(1)}, u32[]{:S(2)}, u32[]{:S(2)}) collective-permute-start(f32[1024,128]{1,0:T(8,128)S(1)} %get-tuple-element.60.own_ref), channel_id=1, source_target_pairs={{0,4},{4,0},{1,5},{5,1},{2,6},{6,2},{3,7},{7,3},{8,12},{12,8},{9,1... | collective-permute-start | bytes 1572872 | tf_op jit(solution)/shard_map/ppermute | solution.py:66
  57.3 2.1 %collective-permute-start.14 = (f32[512,256]{1,0:T(8,128)S(1)}, f32[512,256]{1,0:T(8,128)S(1)}, u32[]{:S(2)}, u32[]{:S(2)}) collective-permute-start(f32[512,256]{1,0:T(8,128)S(1)} %get-tuple-element.62.own_ref), channel_id=1, source_target_pairs={{0,4},{4,0},{1,5},{5,1},{2,6},{6,2},{3,7},{7,3},{8,12},{12,8},{9,1... | collective-permute-start | bytes 1572872 | tf_op jit(solution)/shard_map/ppermute | solution.py:66
  59.2 2.0 %collective-permute-start.15 = (f32[512,256]{1,0:T(8,128)S(1)}, f32[512,256]{1,0:T(8,128)S(1)}, u32[]{:S(2)}, u32[]{:S(2)}) collective-permute-start(f32[512,256]{1,0:T(8,128)S(1)} %shard_map.45.own_ref), channel_id=1, source_target_pairs={{0,4},{4,0},{1,5},{5,1},{2,6},{6,2},{3,7},{7,3},{8,12},{12,8},{9,1... | collective-permute-start | bytes 1572872 | tf_op jit(solution)/shard_map/ppermute | solution.py:66
  62.4 1.2 %collective-permute-start.16 = (f32[8,128]{1,0:T(8,128)S(1)}, f32[8,128]{1,0:T(8,128)S(1)}, u32[]{:S(2)}, u32[]{:S(2)}) collective-permute-start(f32[8,128]{1,0:T(8,128)S(1)} %get-tuple-element.71.own_ref), channel_id=1, source_target_pairs={{0,4},{4,0},{1,5},{5,1},{2,6},{6,2},{3,7},{7,3},{8,12},{12,8},{9,1... | collective-permute-start | bytes 12296 | tf_op jit(solution)/shard_map/ppermute | solution.py:66
  66.5 2.2 %collective-permute-start.17 = (f32[1024,128]{1,0:T(8,128)S(1)}, f32[1024,128]{1,0:T(8,128)S(1)}, u32[]{:S(2)}, u32[]{:S(2)}) collective-permute-start(f32[1024,128]{1,0:T(8,128)S(1)} %get-tuple-element.74.own_ref), channel_id=1, source_target_pairs={{0,4},{4,0},{1,5},{5,1},{2,6},{6,2},{3,7},{7,3},{8,12},{12,8},{9,1... | collective-permute-start | bytes 1572872 | tf_op jit(solution)/shard_map/ppermute | solution.py:66
  74.0 2.1 %collective-permute-start.18 = (f32[512,256]{1,0:T(8,128)S(1)}, f32[512,256]{1,0:T(8,128)S(1)}, u32[]{:S(2)}, u32[]{:S(2)}) collective-permute-start(f32[512,256]{1,0:T(8,128)S(1)} %get-tuple-element.76.own_ref), channel_id=1, source_target_pairs={{0,4},{4,0},{1,5},{5,1},{2,6},{6,2},{3,7},{7,3},{8,12},{12,8},{9,1... | collective-permute-start | bytes 1572872 | tf_op jit(solution)/shard_map/ppermute | solution.py:66
  75.6 2.0 %collective-permute-start.19 = (f32[512,256]{1,0:T(8,128)S(1)}, f32[512,256]{1,0:T(8,128)S(1)}, u32[]{:S(2)}, u32[]{:S(2)}) collective-permute-start(f32[512,256]{1,0:T(8,128)S(1)} %shard_map.51.own_ref), channel_id=1, source_target_pairs={{0,4},{4,0},{1,5},{5,1},{2,6},{6,2},{3,7},{7,3},{8,12},{12,8},{9,1... | collective-permute-start | bytes 1572872 | tf_op jit(solution)/shard_map/ppermute | solution.py:66
  78.8 1.2 %collective-permute-start.20 = (f32[8,128]{1,0:T(8,128)S(1)}, f32[8,128]{1,0:T(8,128)S(1)}, u32[]{:S(2)}, u32[]{:S(2)}) collective-permute-start(f32[8,128]{1,0:T(8,128)S(1)} %get-tuple-element.85.own_ref), channel_id=1, source_target_pairs={{0,4},{4,0},{1,5},{5,1},{2,6},{6,2},{3,7},{7,3},{8,12},{12,8},{9,1... | collective-permute-start | bytes 12296 | tf_op jit(solution)/shard_map/ppermute | solution.py:66

commit v3 on v2

--- a/solution.py
+++ b/solution.py
@@ -34,6 +34,7 @@
 ROWS = (512, 768, 768)
 STARTS = (0, 512, 1280)
 CHUNK = 256
+LONG_CHUNK = 256
 
 
 def places():
@@ -121,6 +122,13 @@
 
 def span(color):
     return slice(STARTS[color], STARTS[color] + ROWS[color])
+
+
+def owner_of(row):
+    color = sum(row >= s for s in STARTS[1:])
+    count = ROWS[color] // 256
+    group = (row - STARTS[color]) // DATA
+    return group // count * 8 + FIRSTS[color] + group % count
 
 
 def half_of(core):
@@ -222,24 +230,26 @@
     return alpha + gamma * grown, -gamma * alpha
 
 
-def own_update(on_drift, on_image, drift_ref, image_refs, turn_ref):
+def own_kernel(drift_ref, image_a, image_b, out_ref, turn_ref):
     mine = half_of(lax.axis_index("c"))
     z = lax.axis_index("z")
     own = pl.ds(pl.multiple_of(z * SLICE, SLICE), SLICE)
     near = pl.ds(pl.multiple_of((z & 1) * SLICE, SLICE), SLICE)
-    image = jnp.where(z < 2, image_refs[0][near, mine], image_refs[1][near, mine])
-    turn_ref[...] = (on_drift * drift_ref[own, mine] + on_image * image).T
-    return turn_ref[pl.ds(pl.multiple_of(own_place() * 8, 8), 8), :]
+    image = jnp.where(z < 2, image_a[near, mine], image_b[near, mine])
+    for k, value in enumerate((drift_ref[own, mine], image)):
+        turn_ref[...] = value.T
+        out_ref[k] = turn_ref[pl.ds(pl.multiple_of(own_place() * 8, 8), 8), :]
 
 
 def next_kernel(
     rows_ref, hot_ref, x_ref, drift_ref, image_a, image_b, own_ref, other_ref,
-    grad_ref, curve_ref, new_ref, out_ref, turn_ref,
+    grad_ref, curve_ref, new_ref, factors_ref,
 ):
     on_drift, on_image = factors(own_ref, other_ref)
-    images = (image_a, image_b)
-    out_ref[...] = own_update(on_drift, on_image, drift_ref, images, turn_ref)
-    for k, image_ref in enumerate(images):
+    factors_ref[0:1, :] = jnp.broadcast_to(on_drift, (1, HALF))
+    factors_ref[1:2, :] = jnp.broadcast_to(on_image, (1, HALF))
+    factors_ref[2:, :] = jnp.zeros((6, HALF), f32)
+    for k, image_ref in enumerate((image_a, image_b)):
         near = slice(k * WIDE // 2, (k + 1) * WIDE // 2)
         update = on_drift * drift_ref[near, :] + on_image * image_ref[...]
         new_ref[near, :] = x_ref[near, :] + move_size * update
@@ -248,37 +258,42 @@
     grad_ref[...] = part - (prior_precision + 2.0 / scale) * x
 
 
-def last_kernel(
-    drift_ref, image_a, image_b, own_ref, other_ref, before_ref, out_ref, turn_ref
-):
-    on_drift, on_image = factors(own_ref, other_ref)
-    out_ref[0] = before_ref[...]
-    out_ref[1] = own_update(on_drift, on_image, drift_ref, (image_a, image_b), turn_ref)
-
-
-def similarity(x, kernel_ref):
+def last_kernel(before_ref, factors_ref, own_ref, sums_ref, other_ref, out_ref):
+    out_ref[0] = factors_ref[:1, :1] * before_ref[0] + factors_ref[1:2, :1] * before_ref[1]
+    on_drift, on_image = factors(sums_ref, other_ref)
+    out_ref[1] = on_drift * own_ref[0] + on_image * own_ref[1]
+
+
+def similarity(x, grad_ref, kernel_ref, drift_ref):
     high, low = two(x)
     gram = tn(high, high) + (tn(high, low) + tn(low, high))
     shape = (MANY, MANY)
     same = lax.broadcasted_iota(jnp.int32, shape, 0) == lax.broadcasted_iota(jnp.int32, shape, 1)
     diag = jnp.where(same, gram, 0.0)
     squares = jnp.sum(diag, axis=1, keepdims=True) + jnp.sum(diag, axis=0, keepdims=True)
-    kernel_ref[...] = jnp.exp((2.0 * gram - squares) / scale)
-
-
-def start_kernel(own_ref, other_ref, kernel_ref, x_ref):
+    kernel = jnp.exp((2.0 * gram - squares) / scale)
+    kernel_ref[...] = kernel
+    total = jnp.sum(kernel, axis=0, keepdims=True)
+    own = two(kernel_ref[half_of(lax.axis_index("c")), :])
+    drift_ref[...] = (2.0 / scale) * total * x + stacked(two(grad_ref[...]), own)
+
+
+def start_kernel(grad_ref, own_ref, other_ref, kernel_ref, drift_ref, x_ref):
     x = in_order(lax.axis_index("c"), own_ref[...], other_ref[...], 1)
     x_ref[...] = x
-    similarity(x, kernel_ref)
-
-
-def again_kernel(x_ref, kernel_ref):
-    similarity(x_ref[...], kernel_ref)
+    similarity(x, grad_ref, kernel_ref, drift_ref)
+
+
+def again_kernel(grad_ref, x_ref, kernel_ref, drift_ref):
+    similarity(x_ref[...], grad_ref, kernel_ref, drift_ref)
 
 
 def spread(rows_ref, weighted_ref, near):
-    rows = rows_ref[:, near]
-    return tn(rows, weighted_ref[0]) + tn(rows, weighted_ref[1])
+    return sum(
+        tn(rows_ref[span(color), near], weighted_ref[k, span(color), :])
+        for color in range(3)
+        for k in range(2)
+    )
 
 
 def image_part(rows_ref, near, x_ref, drift, square, q, weighted_ref):
@@ -296,31 +311,26 @@
     core = lax.axis_index("c")
     mine = half_of(core)
     x = x_ref[...]
-    grad = in_order(core, own_ref[...], other_ref[...], 1)
-    drift = stacked(two(grad), two(kernel_ref[...]))
-    total = jnp.sum(kernel_ref[...], axis=0, keepdims=True)
-    drift = (drift + (2.0 / scale) * total * x) / MANY
+    drift = (own_ref[...] + stacked(two(other_ref[...]), two(kernel_ref[half_of(1 - core), :]))) / MANY
     drift_ref[...] = drift
     drift_two = two(drift)
     kernel_own = kernel_ref[mine, :]
     square = kernel_own * kernel_own
     square_ref[...] = square
-    for color in range(3):
-        count = ROWS[color] // 256
-        for at in range(0, ROWS[color], CHUNK):
-            to = pl.ds(STARTS[color] + at, CHUNK)
-            pieces = []
-            for group in range(at // DATA, (at + CHUNK) // DATA):
-                j = group // count * 8 + FIRSTS[color] + group % count
-                curve = curve_ref[pl.ds(STARTS[color] + group * DATA, DATA), :]
-                wide = jnp.concatenate([curve, curve], axis=1)
-                pieces.append(jnp.broadcast_to(square_ref[j : j + 1, :], wide.shape) * wide)
-            factor = jnp.concatenate(pieces, axis=0)
-            factor_ref[to, :] = factor
-            rows = rows_ref[to, :]
-            high, low = two((nn(rows, drift_two[0]) + nn(rows, drift_two[1])) * factor)
-            weighted_ref[0, to, :] = high
-            weighted_ref[1, to, :] = low
+    for at in range(0, HALF * DATA, LONG_CHUNK):
+        to = pl.ds(at, LONG_CHUNK)
+        pieces = []
+        for start in range(at, at + LONG_CHUNK, DATA):
+            j = owner_of(start)
+            curve = curve_ref[pl.ds(start, DATA), :]
+            wide = jnp.concatenate([curve, curve], axis=1)
+            pieces.append(jnp.broadcast_to(square_ref[j : j + 1, :], wide.shape) * wide)
+        factor = jnp.concatenate(pieces, axis=0)
+        factor_ref[to, :] = factor
+        rows = rows_ref[to, :]
+        high, low = two((nn(rows, drift_two[0]) + nn(rows, drift_two[1])) * factor)
+        weighted_ref[0, to, :] = high
+        weighted_ref[1, to, :] = low
     along = stacked(two(x_ref[:, mine].T), drift_two)
     q = square * (jnp.sum(x * drift, axis=0, keepdims=True) - along)
     q_ref[...] = q
@@ -401,7 +411,7 @@
     whole = pl.BlockSpec(memory_space=pltpu.VMEM)
     return pl.pallas_call(
         kernel,
-        out_shape=[jax.ShapeDtypeStruct(s, t) for s, t in outs],
+        out_shape=[pltpu.VMEM(s, t) if far else jax.ShapeDtypeStruct(s, t) for s, t in outs],
         in_specs=[pl.BlockSpec(memory_space=pltpu.HBM) if far else whole] * len(args),
         out_specs=[whole] * len(outs),
         scratch_shapes=scratch,
@@ -454,20 +464,23 @@
             rows, grad, curve, hot, x_own, pieces[color][3],
             aliases={0: 0, 1: 1, 2: 2},
         )
-    kernel, x = call(start_kernel, [square, long], x_own, x_other)
+    kernel, partial_drift, x = call(
+        start_kernel, [square, long, long], grad, x_own, x_other
+    )
+    own = []
     for newton_step in range(NEWTON):
         if newton_step > 0:
-            grad, curve, x, update = call(
-                next_kernel, [half, curve_of, long, ((8, SLICE), f32)],
-                rows, hot, x, drift, *image, sums, sums_other, scratch=turn,
+            grad, curve, x, weights = call(
+                next_kernel, [half, curve_of, long, ((8, HALF), f32)],
+                rows, hot, x, drift, *image, sums, sums_other,
             )
         grad_other = swap_cores(grad)
         if newton_step > 0:
-            (kernel,) = call(again_kernel, [square], x)
+            kernel, partial_drift = call(again_kernel, [square, long], grad, x)
         drift, own_a, factor, weighted, q = call(
             first_kernel,
             [long, wing, tall, ((2, count, MANY), bf16), low],
-            rows, curve, x, kernel, grad, grad_other,
+            rows, curve, x, kernel, partial_drift, grad_other,
             scratch=[pltpu.VMEM((HALF, MANY), f32)],
         )
         other_a = swap_cores(own_a)
@@ -483,9 +496,9 @@
         )
         image = (image_a, image_b)
         sums_other = swap_cores(sums)
+        own += call(own_kernel, [((2, 8, SLICE), f32)], drift, *image, scratch=turn)
     (updates,) = call(
-        last_kernel, [((NEWTON, 8, SLICE), f32)],
-        drift, *image, sums, sums_other, update, scratch=turn,
+        last_kernel, [((NEWTON, 8, SLICE), f32)], own[0], weights, own[1], sums, sums_other
     )
     return updates
 

time: 81 us -> 78.7 us (0.972)
  waiting for transfers between devices: 19.3 us -> 17 us
    ppermute x9, waiting for transfers between devices: 4.97 us -> 2.69 us  [swap_cores(): return lax.ppermute(x, 'c', [(0, 1), (1, 0)])]
    pallas_call x17 -> x19, Pallas kernels: 29.2 us -> 29.2 us  [call(): pl.pallas_call(kernel, out_shape=[pltpu.VMEM(s, t) if far else jax.ShapeD...]
  transfers between devices with their start and end apart: 21 -> 21, of which waited for: 14 -> 12; matrix products, arithmetic and copies ran while one was open for 0% -> 0% of each run, Pallas kernels for 13% -> 16%
where the time goes in v3:
time: 78.7 us; the launch traced here: 78.5 us
  Pallas kernels  29.2 us (37%)
  blocking collectives  21.5 us (27%)
  waiting for transfers between devices  17 us (22%)
  starting transfers between devices  10.4 us (13%)
    pallas_call x19, Pallas kernels, call(): pl.pallas_call(kernel, out_shape=[pltpu.VMEM(s, t) if far else jax.ShapeD...  29.2 us
    all_to_all x1, blocking collectives, gathered(): lax.all_to_all(copies, AXES, 0, 0, axis_index_groups=cubes(), tiled=True)  21.5 us
    ppermute x12, waiting for transfers between devices, sent(): out.append(lax.ppermute(part, AXES, pairs(order[step])))  14.4 us
    ppermute x9, starting transfers between devices, swap_cores(): return lax.ppermute(x, 'c', [(0, 1), (1, 0)])  5.26 us
    ppermute x12, starting transfers between devices, sent(): out.append(lax.ppermute(part, AXES, pairs(order[step])))  5.18 us
    ppermute x9, waiting for transfers between devices, swap_cores(): return lax.ppermute(x, 'c', [(0, 1), (1, 0)])  2.69 us
  transfers between devices with their start and end apart: 21, of which 12 were waited for; matrix products, arithmetic and copies ran while one was open for 0% of the time, Pallas kernels for 16%

profile of v3, /device:TPU:1, one launch (start us, length us, event | category | flops | bytes accessed | tf_op | source)
XLA Modules:
  0.0 78.5 jit_solution(3262257046351694301)
XLA Ops:
  0.0 1.1 %shard_map.37 = bf16[8,144,256]{2,1,0:T(8,128)(2,1)S(1)} custom-call(f32[8,256]{1,0:T(8,128)} %x_far.1, bf16[8,16,256]{2,1,0:T(8,128)(2,1)} %rows_far.1, s32[8,16]{1,0:T(8,128)} %labels_far.1), custom_call_target="tpu_custom_call" | custom-call | tf_op jit(solution)/shard_map/pallas_call | solution.py:412
  1.1 21.5 %all_to_all.5 = bf16[8,144,256]{2,1,0:T(8,128)(2,1)S(1)} all-to-all(bf16[8,144,256]{2,1,0:T(8,128)(2,1)S(1)} %shard_map.37), channel_id=1, replica_groups={{0,1,8,9,32,33,40,41},{2,3,10,11,34,35,42,43},{4,7,28,31,100,103,124,12..., dimensions={0} | all-to-all | bytes 1179648 | tf_op jit(solution)/shard_map/all_to_all | solution.py:71
  22.6 0.1 collective-permute-start
  22.7 0.1 collective-permute-start.3
  22.8 0.1 collective-permute-start.6
  22.9 4.3 %collective-permute-done = bf16[8,48,256]{2,1,0:T(8,128)(2,1)S(1)} collective-permute-done((bf16[8,48,256]{2,1,0:T(8,128)(2,1)S(1)}, bf16[8,48,256]{2,1,0:T(8,128)(2,1)S(1)}, u32[]{:S(2)}, u32[]{:S(2)}) %collective-permute-start) | collective-permute-done | bytes 196640 | tf_op jit(solution)/shard_map/ppermute | solution.py:77
  27.3 0.1 collective-permute-start.2
  27.3 0.1 collective-permute-start.1
  27.4 0.0 collective-permute-done.3
  27.5 1.4 %collective-permute-start.4 = (bf16[16,48,256]{2,1,0:T(8,128)(2,1)S(1)}, bf16[16,48,256]{2,1,0:T(8,128)(2,1)S(1)}, u32[]{:S(2)}, u32[]{:S(2)}) collective-permute-start(bf16[16,48,256]{2,1,0:T(8,128)(2,1)S(1)} %pad_maximum_fusion.1.refs_3_), channel_id=1, source_target_pairs={{0,3},{1,2},{2,1},{3,0},{4,5},{5,4},{6,7},{7,6},{8,11},{9,10},{10,... | collective-permute-start | bytes 1179656 | tf_op jit(solution)/shard_map/ppermute | solution.py:77
  28.9 0.0 collective-permute-done.6
  29.0 0.3 collective-permute-start.7
  29.2 1.3 %collective-permute-start.5 = (bf16[16,48,256]{2,1,0:T(8,128)(2,1)S(1)}, bf16[16,48,256]{2,1,0:T(8,128)(2,1)S(1)}, u32[]{:S(2)}, u32[]{:S(2)}) collective-permute-start(bf16[16,48,256]{2,1,0:T(8,128)(2,1)S(1)} %pad_maximum_fusion.1.refs_3_), channel_id=1, source_target_pairs={{0,24},{1,25},{2,26},{3,27},{4,12},{5,13},{6,14},{7,15},{8,16},{9,... | collective-permute-start | bytes 1179656 | tf_op jit(solution)/shard_map/ppermute | solution.py:77
  30.5 3.7 %collective-permute-done.2.refs_2_ = bf16[16,48,256]{2,1,0:T(8,128)(2,1)S(1)} collective-permute-done((bf16[16,48,256]{2,1,0:T(8,128)(2,1)S(1)}, bf16[16,48,256]{2,1,0:T(8,128)(2,1)S(1)}, u32[]{:S(2)}, u32[]{:S(2)}) %collective-permute-start.2) | collective-permute-done | bytes 393248 | tf_op jit(solution)/shard_map/ppermute | solution.py:77
  34.3 0.0 collective-permute-start.8
  34.3 0.1 collective-permute-done.1.refs_1_
  34.4 1.4 %collective-permute-start.9 = (bf16[16,48,256]{2,1,0:T(8,128)(2,1)S(1)}, bf16[16,48,256]{2,1,0:T(8,128)(2,1)S(1)}, u32[]{:S(2)}, u32[]{:S(2)}) collective-permute-start(bf16[16,48,256]{2,1,0:T(8,128)(2,1)S(1)} %collective-permute-done.1.refs_1_), channel_id=1, source_target_pairs={{0,3},{1,2},{2,1},{3,0},{4,5},{5,4},{6,7},{7,6},{8,11},{9,10},{10,... | collective-permute-start | bytes 1179656 | tf_op jit(solution)/shard_map/ppermute | solution.py:77
  35.7 2.7 %collective-permute-done.4.refs_4_ = bf16[16,48,256]{2,1,0:T(8,128)(2,1)S(1)} collective-permute-done((bf16[16,48,256]{2,1,0:T(8,128)(2,1)S(1)}, bf16[16,48,256]{2,1,0:T(8,128)(2,1)S(1)}, u32[]{:S(2)}, u32[]{:S(2)}) %collective-permute-start.4) | collective-permute-done | bytes 393248 | tf_op jit(solution)/shard_map/ppermute | solution.py:77
  38.5 0.0 collective-permute-start.10
  38.5 0.0 collective-permute-done.7.refs_7_
  38.5 0.4 collective-permute-start.11
  38.9 1.3 %collective-permute-done.5.refs_5_ = bf16[16,48,256]{2,1,0:T(8,128)(2,1)S(1)} collective-permute-done((bf16[16,48,256]{2,1,0:T(8,128)(2,1)S(1)}, bf16[16,48,256]{2,1,0:T(8,128)(2,1)S(1)}, u32[]{:S(2)}, u32[]{:S(2)}) %collective-permute-start.5) | collective-permute-done | bytes 393248 | tf_op jit(solution)/shard_map/ppermute | solution.py:77
  40.2 1.0 %collective-permute-done.8.refs_8_ = bf16[16,48,256]{2,1,0:T(8,128)(2,1)S(1)} collective-permute-done((bf16[16,48,256]{2,1,0:T(8,128)(2,1)S(1)}, bf16[16,48,256]{2,1,0:T(8,128)(2,1)S(1)}, u32[]{:S(2)}, u32[]{:S(2)}) %collective-permute-start.8) | collective-permute-done | bytes 393248 | tf_op jit(solution)/shard_map/ppermute | solution.py:77
  41.2 0.7 shard_map.38
  41.9 0.8 collective-permute-done.9.d
  42.7 1.1 %shard_map.39 = (bf16[2048,1024]{1,0:T(8,128)(2,1)S(1)}, f32[128,1024]{1,0:T(8,128)S(1)}, f32[1024,128]{1,0:T(8,128)S(1)}, f32[1024,128]{1,0:T(8,128)S(1)}, f32[2048,128]{1,0:T(8,128)S(1)}) custom-call(bf16[2048,1024]{1,0:T(8,128)(2,1)S(1)} %get-tuple-element.49._, ...), custom_call_target="tpu_custom_call", output_to_operand_aliasing={{0}: (0, {}), {1}: (1, {})} | custom-call | tf_op jit(solution)/shard_map/pallas_call | solution.py:412
  43.8 1.2 %collective-permute-start.12 = (f32[1024,128]{1,0:T(8,128)S(1)}, f32[1024,128]{1,0:T(8,128)S(1)}, u32[]{:S(2)}, u32[]{:S(2)}) collective-permute-start(f32[1024,128]{1,0:T(8,128)S(1)} %get-tuple-element.55.x_ref.own_ref), channel_id=1, source_target_pairs={{0,4},{4,0},{1,5},{5,1},{2,6},{6,2},{3,7},{7,3},{8,12},{12,8},{9,1... | collective-permute-start | bytes 1572872 | tf_op jit(solution)/shard_map/ppermute | solution.py:67
  45.0 0.4 collective-permute-done.10.d
  45.4 1.3 %shard_map.40 = (bf16[2048,1024]{1,0:T(8,128)(2,1)S(1)}, f32[1024,128]{1,0:T(8,128)S(1)}, f32[2048,128]{1,0:T(8,128)S(1)}) custom-call(bf16[2048,1024]{1,0:T(8,128)(2,1)S(1)} %get-tuple-element.52._, f32[1024,128]{1,0:T(8,128)S(1)} %get-tuple-element.53.before_ref, ...), custom_call_target="tpu_custom_call", output_to_operand_aliasing={{0}: (0, {}), {1}: (1, {}), {2}: (2, {})} | custom-call | tf_op jit(solution)/shard_map/pallas_call | solution.py:412
  46.7 0.0 collective-permute-done.11.d
  46.7 1.3 %shard_map.41 = (bf16[2048,1024]{1,0:T(8,128)(2,1)S(1)}, f32[1024,128]{1,0:T(8,128)S(1)}, f32[2048,128]{1,0:T(8,128)S(1)}) custom-call(bf16[2048,1024]{1,0:T(8,128)(2,1)S(1)} %get-tuple-element.56._, f32[1024,128]{1,0:T(8,128)S(1)} %get-tuple-element.57.before_ref, ...), custom_call_target="tpu_custom_call", output_to_operand_aliasing={{0}: (0, {}), {1}: (1, {}), {2}: (2, {})} | custom-call | tf_op jit(solution)/shard_map/pallas_call | solution.py:412
  48.0 1.5 %collective-permute-start.13 = (f32[1024,128]{1,0:T(8,128)S(1)}, f32[1024,128]{1,0:T(8,128)S(1)}, u32[]{:S(2)}, u32[]{:S(2)}) collective-permute-start(f32[1024,128]{1,0:T(8,128)S(1)} %get-tuple-element.61.grad_ref), channel_id=1, source_target_pairs={{0,4},{4,0},{1,5},{5,1},{2,6},{6,2},{3,7},{7,3},{8,12},{12,8},{9,1... | collective-permute-start | bytes 1572872 | tf_op jit(solution)/shard_map/ppermute | solution.py:67
  49.5 0.0 collective-permute-done.12.other_ref
  49.5 1.7 %shard_map.42 = (f32[256,256]{1,0:T(8,128)S(1)}, f32[1024,256]{1,0:T(8,128)S(1)}, f32[1024,256]{1,0:T(8,128)S(1)}) custom-call(f32[1024,128]{1,0:T(8,128)S(1)} %get-tuple-element.61.grad_ref, f32[1024,128]{1,0:T(8,128)S(1)} %get-tuple-element.55.x_ref.own_ref, f32[1024,128]{1,0:T(8,128)S(1)} %collective-permute-done.12.other_ref), custom_call_target="tpu_custom_call" | custom-call | tf_op jit(solution)/shard_map/pallas_call | solution.py:412
  51.2 0.0 collective-permute-done.13.other_ref
  51.2 4.7 %shard_map.43 = (f32[1024,256]{1,0:T(8,128)S(1)}, f32[512,256]{1,0:T(8,128)S(1)}, f32[2048,256]{1,0:T(8,128)S(1)}, bf16[2,2048,256]{2,1,0:T(8,128)(2,1)S(1)}, f32[128,256]{1,0:T(8,128)S(1)}) custom-call(bf16[2048,1024]{1,0:T(8,128)(2,1)S(1)} %get-tuple-element.59.rows_ref, f32[2048,128]{1,0:T(8,128)S(1)} %get-tuple-element.60.curve_ref, ...), custom_call_target="tpu_custom_call" | custom-call | tf_op jit(solution)/shard_map/pallas_call | solution.py:412
  55.9 0.3 collective-permute-start.14
  56.2 1.4 %shard_map.45.own_ref = f32[512,256]{1,0:T(8,128)S(1)} custom-call(bf16[2048,1024]{1,0:T(8,128)(2,1)S(1)} %get-tuple-element.59.rows_ref, f32[1024,256]{1,0:T(8,128)S(1)} %get-tuple-element.62.x_ref, f32[256,256]{1,0:T(8,128)S(1)} %get-tuple-element.63.kernel_ref, f32[1024,256]{1,0:T(8,128)S(1)} %get-tuple-element.65.drift_ref, ...), custom_call_target="tpu_custom_call" | custom-call | tf_op jit(solution)/shard_map/pallas_call | solution.py:412
  57.6 0.4 collective-permute-start.15
  58.0 0.0 collective-permute-done.14.other_ref
  58.0 1.0 %shard_map.44 = (f32[512,256]{1,0:T(8,128)S(1)}, f32[2048,256]{1,0:T(8,128)S(1)}, f32[128,256]{1,0:T(8,128)S(1)}, f32[8,256]{1,0:T(8,128)S(1)}) custom-call(bf16[2048,1024]{1,0:T(8,128)(2,1)S(1)} %get-tuple-element.59.rows_ref, f32[1024,256]{1,0:T(8,128)S(1)} %get-tuple-element.62.x_ref, f32[1024,256]{1,0:T(8,128)S(1)} %get-tuple-element.65.drift_ref, ...), custom_call_target="tpu_custom_call" | custom-call | tf_op jit(solution)/shard_map/pallas_call | solution.py:412
  59.0 0.6 collective-permute-done.15.other_ref
  59.6 1.2 %shard_map.46 = (f32[512,256]{1,0:T(8,128)S(1)}, f32[8,128]{1,0:T(8,128)S(1)}) custom-call(bf16[2048,1024]{1,0:T(8,128)(2,1)S(1)} %get-tuple-element.59.rows_ref, f32[1024,256]{1,0:T(8,128)S(1)} %get-tuple-element.62.x_ref, f32[256,256]{1,0:T(8,128)S(1)} %get-tuple-element.63.kernel_ref, f32[2048,256]{1,0:T(8,128)S(1)} %get-tuple-element.68.factor_ref, ...), custom_call_target="tpu_custom_call" | custom-call | tf_op jit(solution)/shard_map/pallas_call | solution.py:412
  60.8 0.3 collective-permute-start.16
  61.1 0.9 %collective-permute-done.16.other_ref = f32[8,128]{1,0:T(8,128)S(1)} collective-permute-done((f32[8,128]{1,0:T(8,128)S(1)}, f32[8,128]{1,0:T(8,128)S(1)}, u32[]{:S(2)}, u32[]{:S(2)}) %collective-permute-start.16) | collective-permute-done | bytes 4128 | tf_op jit(solution)/shard_map/ppermute | solution.py:67
  62.0 2.9 %shard_map.48 = (f32[1024,128]{1,0:T(8,128)S(1)}, f32[2048,128]{1,0:T(8,128)S(1)}, f32[1024,256]{1,0:T(8,128)S(1)}, f32[8,128]{1,0:T(8,128)S(1)}) custom-call(bf16[2048,1024]{1,0:T(8,128)(2,1)S(1)} %get-tuple-element.59.rows_ref, bf16[2048,128]{1,0:T(8,128)(2,1)S(1)} %get-tuple-element.51.hot_ref, f32[1024,256]{1,0:T(8,128)S(1)} %get-tuple-element.62.x_ref, ...), custom_call_target="tpu_custom_call" | custom-call | tf_op jit(solution)/shard_map/pallas_call | solution.py:412
  64.8 0.6 collective-permute-start.17
  65.4 1.6 %shard_map.49 = (f32[256,256]{1,0:T(8,128)S(1)}, f32[1024,256]{1,0:T(8,128)S(1)}) custom-call(f32[1024,128]{1,0:T(8,128)S(1)} %get-tuple-element.79.grad_ref, f32[1024,256]{1,0:T(8,128)S(1)} %get-tuple-element.78.x_ref), custom_call_target="tpu_custom_call" | custom-call | tf_op jit(solution)/shard_map/pallas_call | solution.py:412
  67.0 0.0 collective-permute-done.17.other_ref
  67.1 4.7 %shard_map.50 = (f32[1024,256]{1,0:T(8,128)S(1)}, f32[512,256]{1,0:T(8,128)S(1)}, f32[2048,256]{1,0:T(8,128)S(1)}, bf16[2,2048,256]{2,1,0:T(8,128)(2,1)S(1)}, f32[128,256]{1,0:T(8,128)S(1)}) custom-call(bf16[2048,1024]{1,0:T(8,128)(2,1)S(1)} %get-tuple-element.59.rows_ref, f32[2048,128]{1,0:T(8,128)S(1)} %get-tuple-element.77.curve_ref, ...), custom_call_target="tpu_custom_call" | custom-call | tf_op jit(solution)/shard_map/pallas_call | solution.py:412
  71.7 0.3 collective-permute-start.18
  72.0 1.4 %shard_map.52.own_ref = f32[512,256]{1,0:T(8,128)S(1)} custom-call(bf16[2048,1024]{1,0:T(8,128)(2,1)S(1)} %get-tuple-element.59.rows_ref, f32[1024,256]{1,0:T(8,128)S(1)} %get-tuple-element.78.x_ref, f32[256,256]{1,0:T(8,128)S(1)} %get-tuple-element.80.kernel_ref, f32[1024,256]{1,0:T(8,128)S(1)} %get-tuple-element.82.drift_ref, ...), custom_call_target="tpu_custom_call" | custom-call | tf_op jit(solution)/shard_map/pallas_call | solution.py:412
  73.5 0.4 collective-permute-start.19
  73.9 0.0 collective-permute-done.18.other_ref
  73.9 1.0 %shard_map.51 = (f32[512,256]{1,0:T(8,128)S(1)}, f32[2048,256]{1,0:T(8,128)S(1)}, f32[128,256]{1,0:T(8,128)S(1)}, f32[8,256]{1,0:T(8,128)S(1)}) custom-call(bf16[2048,1024]{1,0:T(8,128)(2,1)S(1)} %get-tuple-element.59.rows_ref, f32[1024,256]{1,0:T(8,128)S(1)} %get-tuple-element.78.x_ref, f32[1024,256]{1,0:T(8,128)S(1)} %get-tuple-element.82.drift_ref, ...), custom_call_target="tpu_custom_call" | custom-call | tf_op jit(solution)/shard_map/pallas_call | solution.py:412
  74.8 0.6 collective-permute-done.19.other_ref
  75.5 1.2 %shard_map.53 = (f32[512,256]{1,0:T(8,128)S(1)}, f32[8,128]{1,0:T(8,128)S(1)}) custom-call(bf16[2048,1024]{1,0:T(8,128)(2,1)S(1)} %get-tuple-element.59.rows_ref, f32[1024,256]{1,0:T(8,128)S(1)} %get-tuple-element.78.x_ref, f32[256,256]{1,0:T(8,128)S(1)} %get-tuple-element.80.kernel_ref, f32[2048,256]{1,0:T(8,128)S(1)} %get-tuple-element.85.factor_ref, ...), custom_call_target="tpu_custom_call" | custom-call | tf_op jit(solution)/shard_map/pallas_call | solution.py:412
  76.7 0.3 collective-permute-start.20
  76.9 0.1 shard_map.47.before_ref
  77.1 0.1 shard_map.54.own_ref
  77.2 0.6 collective-permute-done.20.other_ref
  77.8 0.7 shard_map.55
  (4 shorter events, 0.1 us)
Async XLA Ops:
  22.6 4.6 %collective-permute-start = (bf16[8,48,256]{2,1,0:T(8,128)(2,1)S(1)}, bf16[8,48,256]{2,1,0:T(8,128)(2,1)S(1)}, u32[]{:S(2)}, u32[]{:S(2)}) collective-permute-start(bf16[8,48,256]{2,1,0:T(8,128)(2,1)S(1)} %get-tuple-element.95), channel_id=1, source_target_pairs={{0,24},{1,25},{2,26},{3,27},{4,12},{5,13},{6,14},{7,15},{8,16},{9,... | collective-permute-start | bytes 589832 | tf_op jit(solution)/shard_map/ppermute | solution.py:77
  22.7 4.7 %collective-permute-start.3 = (bf16[8,48,256]{2,1,0:T(8,128)(2,1)S(1)}, bf16[8,48,256]{2,1,0:T(8,128)(2,1)S(1)}, u32[]{:S(2)}, u32[]{:S(2)}) collective-permute-start(bf16[8,48,256]{2,1,0:T(8,128)(2,1)S(1)} %get-tuple-element.94), channel_id=1, source_target_pairs={{0,96},{1,97},{2,98},{3,99},{4,36},{5,37},{6,38},{7,39},{8,104},{9... | collective-permute-start | bytes 589832 | tf_op jit(solution)/shard_map/ppermute | solution.py:77
  22.8 6.1 %collective-permute-start.6 = (bf16[8,48,256]{2,1,0:T(8,128)(2,1)S(1)}, bf16[8,48,256]{2,1,0:T(8,128)(2,1)S(1)}, u32[]{:S(2)}, u32[]{:S(2)}) collective-permute-start(bf16[8,48,256]{2,1,0:T(8,128)(2,1)S(1)} %get-tuple-element.93), channel_id=1, source_target_pairs={{0,3},{1,2},{2,1},{3,0},{4,5},{5,4},{6,7},{7,6},{8,11},{9,10},{10,... | collective-permute-start | bytes 589832 | tf_op jit(solution)/shard_map/ppermute | solution.py:77
  27.3 7.0 %collective-permute-start.2 = (bf16[16,48,256]{2,1,0:T(8,128)(2,1)S(1)}, bf16[16,48,256]{2,1,0:T(8,128)(2,1)S(1)}, u32[]{:S(2)}, u32[]{:S(2)}) collective-permute-start(bf16[16,48,256]{2,1,0:T(8,128)(2,1)S(1)} %pad_maximum_fusion.refs_0_), channel_id=1, source_target_pairs={{0,3},{1,2},{2,1},{3,0},{4,5},{5,4},{6,7},{7,6},{8,11},{9,10},{10,... | collective-permute-start | bytes 1179656 | tf_op jit(solution)/shard_map/ppermute | solution.py:77
  27.3 7.0 %collective-permute-start.1 = (bf16[16,48,256]{2,1,0:T(8,128)(2,1)S(1)}, bf16[16,48,256]{2,1,0:T(8,128)(2,1)S(1)}, u32[]{:S(2)}, u32[]{:S(2)}) collective-permute-start(bf16[16,48,256]{2,1,0:T(8,128)(2,1)S(1)} %pad_maximum_fusion.refs_0_), channel_id=1, source_target_pairs={{0,96},{1,97},{2,98},{3,99},{4,36},{5,37},{6,38},{7,39},{8,104},{9... | collective-permute-start | bytes 1179656 | tf_op jit(solution)/shard_map/ppermute | solution.py:77
  27.5 11.0 %collective-permute-start.4 = (bf16[16,48,256]{2,1,0:T(8,128)(2,1)S(1)}, bf16[16,48,256]{2,1,0:T(8,128)(2,1)S(1)}, u32[]{:S(2)}, u32[]{:S(2)}) collective-permute-start(bf16[16,48,256]{2,1,0:T(8,128)(2,1)S(1)} %pad_maximum_fusion.1.refs_3_), channel_id=1, source_target_pairs={{0,3},{1,2},{2,1},{3,0},{4,5},{5,4},{6,7},{7,6},{8,11},{9,10},{10,... | collective-permute-start | bytes 1179656 | tf_op jit(solution)/shard_map/ppermute | solution.py:77
  29.0 9.5 %collective-permute-start.7 = (bf16[16,48,256]{2,1,0:T(8,128)(2,1)S(1)}, bf16[16,48,256]{2,1,0:T(8,128)(2,1)S(1)}, u32[]{:S(2)}, u32[]{:S(2)}) collective-permute-start(bf16[16,48,256]{2,1,0:T(8,128)(2,1)S(1)} %pad_maximum_fusion.2.refs_6_), channel_id=1, source_target_pairs={{0,24},{1,25},{2,26},{3,27},{4,12},{5,13},{6,14},{7,15},{8,16},{9,... | collective-permute-start | bytes 1179656 | tf_op jit(solution)/shard_map/ppermute | solution.py:77
  29.2 10.9 %collective-permute-start.5 = (bf16[16,48,256]{2,1,0:T(8,128)(2,1)S(1)}, bf16[16,48,256]{2,1,0:T(8,128)(2,1)S(1)}, u32[]{:S(2)}, u32[]{:S(2)}) collective-permute-start(bf16[16,48,256]{2,1,0:T(8,128)(2,1)S(1)} %pad_maximum_fusion.1.refs_3_), channel_id=1, source_target_pairs={{0,24},{1,25},{2,26},{3,27},{4,12},{5,13},{6,14},{7,15},{8,16},{9,... | collective-permute-start | bytes 1179656 | tf_op jit(solution)/shard_map/ppermute | solution.py:77
  34.3 6.9 %collective-permute-start.8 = (bf16[16,48,256]{2,1,0:T(8,128)(2,1)S(1)}, bf16[16,48,256]{2,1,0:T(8,128)(2,1)S(1)}, u32[]{:S(2)}, u32[]{:S(2)}) collective-permute-start(bf16[16,48,256]{2,1,0:T(8,128)(2,1)S(1)} %pad_maximum_fusion.2.refs_6_), channel_id=1, source_target_pairs={{0,96},{1,97},{2,98},{3,99},{4,36},{5,37},{6,38},{7,39},{8,104},{9... | collective-permute-start | bytes 1179656 | tf_op jit(solution)/shard_map/ppermute | solution.py:77
  34.4 8.3 %collective-permute-start.9 = (bf16[16,48,256]{2,1,0:T(8,128)(2,1)S(1)}, bf16[16,48,256]{2,1,0:T(8,128)(2,1)S(1)}, u32[]{:S(2)}, u32[]{:S(2)}) collective-permute-start(bf16[16,48,256]{2,1,0:T(8,128)(2,1)S(1)} %collective-permute-done.1.refs_1_), channel_id=1, source_target_pairs={{0,3},{1,2},{2,1},{3,0},{4,5},{5,4},{6,7},{7,6},{8,11},{9,10},{10,... | collective-permute-start | bytes 1179656 | tf_op jit(solution)/shard_map/ppermute | solution.py:77
  38.5 6.9 %collective-permute-start.10 = (bf16[16,48,256]{2,1,0:T(8,128)(2,1)S(1)}, bf16[16,48,256]{2,1,0:T(8,128)(2,1)S(1)}, u32[]{:S(2)}, u32[]{:S(2)}) collective-permute-start(bf16[16,48,256]{2,1,0:T(8,128)(2,1)S(1)} %collective-permute-done.4.refs_4_), channel_id=1, source_target_pairs={{0,24},{1,25},{2,26},{3,27},{4,12},{5,13},{6,14},{7,15},{8,16},{9,... | collective-permute-start | bytes 1179656 | tf_op jit(solution)/shard_map/ppermute | solution.py:77
  38.5 8.2 %collective-permute-start.11 = (bf16[16,48,256]{2,1,0:T(8,128)(2,1)S(1)}, bf16[16,48,256]{2,1,0:T(8,128)(2,1)S(1)}, u32[]{:S(2)}, u32[]{:S(2)}) collective-permute-start(bf16[16,48,256]{2,1,0:T(8,128)(2,1)S(1)} %collective-permute-done.7.refs_7_), channel_id=1, source_target_pairs={{0,96},{1,97},{2,98},{3,99},{4,36},{5,37},{6,38},{7,39},{8,104},{9... | collective-permute-start | bytes 1179656 | tf_op jit(solution)/shard_map/ppermute | solution.py:77
  43.8 5.7 %collective-permute-start.12 = (f32[1024,128]{1,0:T(8,128)S(1)}, f32[1024,128]{1,0:T(8,128)S(1)}, u32[]{:S(2)}, u32[]{:S(2)}) collective-permute-start(f32[1024,128]{1,0:T(8,128)S(1)} %get-tuple-element.55.x_ref.own_ref), channel_id=1, source_target_pairs={{0,4},{4,0},{1,5},{5,1},{2,6},{6,2},{3,7},{7,3},{8,12},{12,8},{9,1... | collective-permute-start | bytes 1572872 | tf_op jit(solution)/shard_map/ppermute | solution.py:67
  48.0 3.2 %collective-permute-start.13 = (f32[1024,128]{1,0:T(8,128)S(1)}, f32[1024,128]{1,0:T(8,128)S(1)}, u32[]{:S(2)}, u32[]{:S(2)}) collective-permute-start(f32[1024,128]{1,0:T(8,128)S(1)} %get-tuple-element.61.grad_ref), channel_id=1, source_target_pairs={{0,4},{4,0},{1,5},{5,1},{2,6},{6,2},{3,7},{7,3},{8,12},{12,8},{9,1... | collective-permute-start | bytes 1572872 | tf_op jit(solution)/shard_map/ppermute | solution.py:67
  55.9 2.1 %collective-permute-start.14 = (f32[512,256]{1,0:T(8,128)S(1)}, f32[512,256]{1,0:T(8,128)S(1)}, u32[]{:S(2)}, u32[]{:S(2)}) collective-permute-start(f32[512,256]{1,0:T(8,128)S(1)} %get-tuple-element.66.own_ref), channel_id=1, source_target_pairs={{0,4},{4,0},{1,5},{5,1},{2,6},{6,2},{3,7},{7,3},{8,12},{12,8},{9,1... | collective-permute-start | bytes 1572872 | tf_op jit(solution)/shard_map/ppermute | solution.py:67
  57.6 2.0 %collective-permute-start.15 = (f32[512,256]{1,0:T(8,128)S(1)}, f32[512,256]{1,0:T(8,128)S(1)}, u32[]{:S(2)}, u32[]{:S(2)}) collective-permute-start(f32[512,256]{1,0:T(8,128)S(1)} %shard_map.45.own_ref), channel_id=1, source_target_pairs={{0,4},{4,0},{1,5},{5,1},{2,6},{6,2},{3,7},{7,3},{8,12},{12,8},{9,1... | collective-permute-start | bytes 1572872 | tf_op jit(solution)/shard_map/ppermute | solution.py:67
  60.8 1.2 %collective-permute-start.16 = (f32[8,128]{1,0:T(8,128)S(1)}, f32[8,128]{1,0:T(8,128)S(1)}, u32[]{:S(2)}, u32[]{:S(2)}) collective-permute-start(f32[8,128]{1,0:T(8,128)S(1)} %get-tuple-element.75.own_ref), channel_id=1, source_target_pairs={{0,4},{4,0},{1,5},{5,1},{2,6},{6,2},{3,7},{7,3},{8,12},{12,8},{9,1... | collective-permute-start | bytes 12296 | tf_op jit(solution)/shard_map/ppermute | solution.py:67
  64.8 2.2 %collective-permute-start.17 = (f32[1024,128]{1,0:T(8,128)S(1)}, f32[1024,128]{1,0:T(8,128)S(1)}, u32[]{:S(2)}, u32[]{:S(2)}) collective-permute-start(f32[1024,128]{1,0:T(8,128)S(1)} %get-tuple-element.79.grad_ref), channel_id=1, source_target_pairs={{0,4},{4,0},{1,5},{5,1},{2,6},{6,2},{3,7},{7,3},{8,12},{12,8},{9,1... | collective-permute-start | bytes 1572872 | tf_op jit(solution)/shard_map/ppermute | solution.py:67
  71.7 2.1 %collective-permute-start.18 = (f32[512,256]{1,0:T(8,128)S(1)}, f32[512,256]{1,0:T(8,128)S(1)}, u32[]{:S(2)}, u32[]{:S(2)}) collective-permute-start(f32[512,256]{1,0:T(8,128)S(1)} %get-tuple-element.83.own_ref), channel_id=1, source_target_pairs={{0,4},{4,0},{1,5},{5,1},{2,6},{6,2},{3,7},{7,3},{8,12},{12,8},{9,1... | collective-permute-start | bytes 1572872 | tf_op jit(solution)/shard_map/ppermute | solution.py:67
  73.5 2.0 %collective-permute-start.19 = (f32[512,256]{1,0:T(8,128)S(1)}, f32[512,256]{1,0:T(8,128)S(1)}, u32[]{:S(2)}, u32[]{:S(2)}) collective-permute-start(f32[512,256]{1,0:T(8,128)S(1)} %shard_map.52.own_ref), channel_id=1, source_target_pairs={{0,4},{4,0},{1,5},{5,1},{2,6},{6,2},{3,7},{7,3},{8,12},{12,8},{9,1... | collective-permute-start | bytes 1572872 | tf_op jit(solution)/shard_map/ppermute | solution.py:67
  76.7 1.2 %collective-permute-start.20 = (f32[8,128]{1,0:T(8,128)S(1)}, f32[8,128]{1,0:T(8,128)S(1)}, u32[]{:S(2)}, u32[]{:S(2)}) collective-permute-start(f32[8,128]{1,0:T(8,128)S(1)} %get-tuple-element.92.sums_ref), channel_id=1, source_target_pairs={{0,4},{4,0},{1,5},{5,1},{2,6},{6,2},{3,7},{7,3},{8,12},{12,8},{9,1... | collective-permute-start | bytes 12296 | tf_op jit(solution)/shard_map/ppermute | solution.py:67

commit v4 on v3

--- a/solution.py
+++ b/solution.py
@@ -34,7 +34,7 @@
 ROWS = (512, 768, 768)
 STARTS = (0, 512, 1280)
 CHUNK = 256
-LONG_CHUNK = 256
+LONG_CHUNK = 512
 
 
 def places():
@@ -200,8 +200,10 @@
         prob = 1.0 / (1.0 + jnp.exp(logit))
         curve_ref[part, :] = jnp.broadcast_to(like_weight * prob * (1.0 - prob), (CHUNK, HALF))
         weights.append(jnp.concatenate(two(like_weight * prob * hot), axis=1))
-    total = tn(rows_ref[start:stop, :], jnp.concatenate(weights, axis=0))
-    return total[:, :HALF] + total[:, HALF:]
+    weights = jnp.concatenate(weights, axis=0)
+    halves = (slice(0, WIDE // 2), slice(WIDE // 2, WIDE))
+    total = [tn(rows_ref[start:stop, near], weights) for near in halves]
+    return jnp.concatenate([t[:, :HALF] + t[:, HALF:] for t in total], axis=0)
 
 
 def position_kernel(_, __, hot_ref, d, rows_ref, tail_ref, x_ref, grad_ref, curve_ref):
@@ -317,10 +319,10 @@
     kernel_own = kernel_ref[mine, :]
     square = kernel_own * kernel_own
     square_ref[...] = square
-    for at in range(0, HALF * DATA, LONG_CHUNK):
-        to = pl.ds(at, LONG_CHUNK)
+    for at in range(0, HALF * DATA, CHUNK):
+        to = pl.ds(at, CHUNK)
         pieces = []
-        for start in range(at, at + LONG_CHUNK, DATA):
+        for start in range(at, at + CHUNK, DATA):
             j = owner_of(start)
             curve = curve_ref[pl.ds(start, DATA), :]
             wide = jnp.concatenate([curve, curve], axis=1)
@@ -389,8 +391,8 @@
     sums, along, rounded = read_image(near, x_ref, drift_ref, image)
     sums = [value + before_ref[at : at + 1, :] for at, value in enumerate(sums)]
     total = jnp.zeros((1, MANY), f32)
-    for at in range(0, HALF * DATA, CHUNK):
-        to = pl.ds(at, CHUNK)
+    for at in range(0, HALF * DATA, LONG_CHUNK):
+        to = pl.ds(at, LONG_CHUNK)
         projected = projected_ref[to, :] + nn(rows_ref[to, near], rounded)
         total += jnp.sum(projected * projected * factor_ref[to, :], axis=0, keepdims=True)
     fit = sums[3] / jnp.maximum(sums[4], 1e-30)

time: 78.7 us -> 78.4 us (level)
  no operation moved by 1% of the time
where the time goes in v4:
time: 78.4 us; the launch traced here: 78.2 us
  Pallas kernels  28.8 us (37%)
  blocking collectives  21.5 us (27%)
  waiting for transfers between devices  17 us (22%)
  starting transfers between devices  10.5 us (13%)
    pallas_call x19, Pallas kernels, call(): pl.pallas_call(kernel, out_shape=[pltpu.VMEM(s, t) if far else jax.ShapeD...  28.8 us
    all_to_all x1, blocking collectives, gathered(): lax.all_to_all(copies, AXES, 0, 0, axis_index_groups=cubes(), tiled=True)  21.5 us
    ppermute x12, waiting for transfers between devices, sent(): out.append(lax.ppermute(part, AXES, pairs(order[step])))  14.4 us
    ppermute x9, starting transfers between devices, swap_cores(): return lax.ppermute(x, 'c', [(0, 1), (1, 0)])  5.28 us
    ppermute x12, starting transfers between devices, sent(): out.append(lax.ppermute(part, AXES, pairs(order[step])))  5.18 us
    ppermute x9, waiting for transfers between devices, swap_cores(): return lax.ppermute(x, 'c', [(0, 1), (1, 0)])  2.68 us
  transfers between devices with their start and end apart: 21, of which 12 were waited for; matrix products, arithmetic and copies ran while one was open for 0% of the time, Pallas kernels for 16%

profile of v4, /device:TPU:1, one launch (start us, length us, event | category | flops | bytes accessed | tf_op | source)
XLA Modules:
  0.0 78.2 jit_solution(9429367752533453760)
XLA Ops:
  0.0 1.1 %shard_map.37 = bf16[8,144,256]{2,1,0:T(8,128)(2,1)S(1)} custom-call(f32[8,256]{1,0:T(8,128)} %x_far.1, bf16[8,16,256]{2,1,0:T(8,128)(2,1)} %rows_far.1, s32[8,16]{1,0:T(8,128)} %labels_far.1), custom_call_target="tpu_custom_call" | custom-call | tf_op jit(solution)/shard_map/pallas_call | solution.py:414
  1.1 21.5 %all_to_all.5 = bf16[8,144,256]{2,1,0:T(8,128)(2,1)S(1)} all-to-all(bf16[8,144,256]{2,1,0:T(8,128)(2,1)S(1)} %shard_map.37), channel_id=1, replica_groups={{0,1,8,9,32,33,40,41},{2,3,10,11,34,35,42,43},{4,7,28,31,100,103,124,12..., dimensions={0} | all-to-all | bytes 1179648 | tf_op jit(solution)/shard_map/all_to_all | solution.py:71
  22.6 0.1 collective-permute-start
  22.7 0.1 collective-permute-start.3
  22.8 0.1 collective-permute-start.6
  22.9 4.3 %collective-permute-done = bf16[8,48,256]{2,1,0:T(8,128)(2,1)S(1)} collective-permute-done((bf16[8,48,256]{2,1,0:T(8,128)(2,1)S(1)}, bf16[8,48,256]{2,1,0:T(8,128)(2,1)S(1)}, u32[]{:S(2)}, u32[]{:S(2)}) %collective-permute-start) | collective-permute-done | bytes 196640 | tf_op jit(solution)/shard_map/ppermute | solution.py:77
  27.3 0.1 collective-permute-start.2
  27.3 0.1 collective-permute-start.1
  27.4 0.0 collective-permute-done.3
  27.5 1.4 %collective-permute-start.4 = (bf16[16,48,256]{2,1,0:T(8,128)(2,1)S(1)}, bf16[16,48,256]{2,1,0:T(8,128)(2,1)S(1)}, u32[]{:S(2)}, u32[]{:S(2)}) collective-permute-start(bf16[16,48,256]{2,1,0:T(8,128)(2,1)S(1)} %pad_maximum_fusion.1.refs_3_), channel_id=1, source_target_pairs={{0,3},{1,2},{2,1},{3,0},{4,5},{5,4},{6,7},{7,6},{8,11},{9,10},{10,... | collective-permute-start | bytes 1179656 | tf_op jit(solution)/shard_map/ppermute | solution.py:77
  28.9 0.0 collective-permute-done.6
  29.0 0.3 collective-permute-start.7
  29.2 1.3 %collective-permute-start.5 = (bf16[16,48,256]{2,1,0:T(8,128)(2,1)S(1)}, bf16[16,48,256]{2,1,0:T(8,128)(2,1)S(1)}, u32[]{:S(2)}, u32[]{:S(2)}) collective-permute-start(bf16[16,48,256]{2,1,0:T(8,128)(2,1)S(1)} %pad_maximum_fusion.1.refs_3_), channel_id=1, source_target_pairs={{0,24},{1,25},{2,26},{3,27},{4,12},{5,13},{6,14},{7,15},{8,16},{9,... | collective-permute-start | bytes 1179656 | tf_op jit(solution)/shard_map/ppermute | solution.py:77
  30.5 3.7 %collective-permute-done.2.refs_2_ = bf16[16,48,256]{2,1,0:T(8,128)(2,1)S(1)} collective-permute-done((bf16[16,48,256]{2,1,0:T(8,128)(2,1)S(1)}, bf16[16,48,256]{2,1,0:T(8,128)(2,1)S(1)}, u32[]{:S(2)}, u32[]{:S(2)}) %collective-permute-start.2) | collective-permute-done | bytes 393248 | tf_op jit(solution)/shard_map/ppermute | solution.py:77
  34.3 0.0 collective-permute-start.8
  34.3 0.1 collective-permute-done.1.refs_1_
  34.4 1.4 %collective-permute-start.9 = (bf16[16,48,256]{2,1,0:T(8,128)(2,1)S(1)}, bf16[16,48,256]{2,1,0:T(8,128)(2,1)S(1)}, u32[]{:S(2)}, u32[]{:S(2)}) collective-permute-start(bf16[16,48,256]{2,1,0:T(8,128)(2,1)S(1)} %collective-permute-done.1.refs_1_), channel_id=1, source_target_pairs={{0,3},{1,2},{2,1},{3,0},{4,5},{5,4},{6,7},{7,6},{8,11},{9,10},{10,... | collective-permute-start | bytes 1179656 | tf_op jit(solution)/shard_map/ppermute | solution.py:77
  35.7 2.7 %collective-permute-done.4.refs_4_ = bf16[16,48,256]{2,1,0:T(8,128)(2,1)S(1)} collective-permute-done((bf16[16,48,256]{2,1,0:T(8,128)(2,1)S(1)}, bf16[16,48,256]{2,1,0:T(8,128)(2,1)S(1)}, u32[]{:S(2)}, u32[]{:S(2)}) %collective-permute-start.4) | collective-permute-done | bytes 393248 | tf_op jit(solution)/shard_map/ppermute | solution.py:77
  38.5 0.0 collective-permute-start.10
  38.5 0.0 collective-permute-done.7.refs_7_
  38.5 0.4 collective-permute-start.11
  38.9 1.3 %collective-permute-done.5.refs_5_ = bf16[16,48,256]{2,1,0:T(8,128)(2,1)S(1)} collective-permute-done((bf16[16,48,256]{2,1,0:T(8,128)(2,1)S(1)}, bf16[16,48,256]{2,1,0:T(8,128)(2,1)S(1)}, u32[]{:S(2)}, u32[]{:S(2)}) %collective-permute-start.5) | collective-permute-done | bytes 393248 | tf_op jit(solution)/shard_map/ppermute | solution.py:77
  40.2 1.0 %collective-permute-done.8.refs_8_ = bf16[16,48,256]{2,1,0:T(8,128)(2,1)S(1)} collective-permute-done((bf16[16,48,256]{2,1,0:T(8,128)(2,1)S(1)}, bf16[16,48,256]{2,1,0:T(8,128)(2,1)S(1)}, u32[]{:S(2)}, u32[]{:S(2)}) %collective-permute-start.8) | collective-permute-done | bytes 393248 | tf_op jit(solution)/shard_map/ppermute | solution.py:77
  41.2 0.7 shard_map.38
  41.9 0.8 collective-permute-done.9.d
  42.7 1.1 %shard_map.39 = (bf16[2048,1024]{1,0:T(8,128)(2,1)S(1)}, f32[128,1024]{1,0:T(8,128)S(1)}, f32[1024,128]{1,0:T(8,128)S(1)}, f32[1024,128]{1,0:T(8,128)S(1)}, f32[2048,128]{1,0:T(8,128)S(1)}) custom-call(bf16[2048,1024]{1,0:T(8,128)(2,1)S(1)} %get-tuple-element.49._, ...), custom_call_target="tpu_custom_call", output_to_operand_aliasing={{0}: (0, {}), {1}: (1, {})} | custom-call | tf_op jit(solution)/shard_map/pallas_call | solution.py:414
  43.8 1.2 %collective-permute-start.12 = (f32[1024,128]{1,0:T(8,128)S(1)}, f32[1024,128]{1,0:T(8,128)S(1)}, u32[]{:S(2)}, u32[]{:S(2)}) collective-permute-start(f32[1024,128]{1,0:T(8,128)S(1)} %get-tuple-element.55.x_ref.own_ref), channel_id=1, source_target_pairs={{0,4},{4,0},{1,5},{5,1},{2,6},{6,2},{3,7},{7,3},{8,12},{12,8},{9,1... | collective-permute-start | bytes 1572872 | tf_op jit(solution)/shard_map/ppermute | solution.py:67
  45.0 0.4 collective-permute-done.10.d
  45.4 1.3 %shard_map.40 = (bf16[2048,1024]{1,0:T(8,128)(2,1)S(1)}, f32[1024,128]{1,0:T(8,128)S(1)}, f32[2048,128]{1,0:T(8,128)S(1)}) custom-call(bf16[2048,1024]{1,0:T(8,128)(2,1)S(1)} %get-tuple-element.52._, f32[1024,128]{1,0:T(8,128)S(1)} %get-tuple-element.53.before_ref, ...), custom_call_target="tpu_custom_call", output_to_operand_aliasing={{0}: (0, {}), {1}: (1, {}), {2}: (2, {})} | custom-call | tf_op jit(solution)/shard_map/pallas_call | solution.py:414
  46.7 0.0 collective-permute-done.11.d
  46.7 1.3 %shard_map.41 = (bf16[2048,1024]{1,0:T(8,128)(2,1)S(1)}, f32[1024,128]{1,0:T(8,128)S(1)}, f32[2048,128]{1,0:T(8,128)S(1)}) custom-call(bf16[2048,1024]{1,0:T(8,128)(2,1)S(1)} %get-tuple-element.56._, f32[1024,128]{1,0:T(8,128)S(1)} %get-tuple-element.57.before_ref, ...), custom_call_target="tpu_custom_call", output_to_operand_aliasing={{0}: (0, {}), {1}: (1, {}), {2}: (2, {})} | custom-call | tf_op jit(solution)/shard_map/pallas_call | solution.py:414
  48.0 1.5 %collective-permute-start.13 = (f32[1024,128]{1,0:T(8,128)S(1)}, f32[1024,128]{1,0:T(8,128)S(1)}, u32[]{:S(2)}, u32[]{:S(2)}) collective-permute-start(f32[1024,128]{1,0:T(8,128)S(1)} %get-tuple-element.61.grad_ref), channel_id=1, source_target_pairs={{0,4},{4,0},{1,5},{5,1},{2,6},{6,2},{3,7},{7,3},{8,12},{12,8},{9,1... | collective-permute-start | bytes 1572872 | tf_op jit(solution)/shard_map/ppermute | solution.py:67
  49.5 0.0 collective-permute-done.12.other_ref
  49.5 1.7 %shard_map.42 = (f32[256,256]{1,0:T(8,128)S(1)}, f32[1024,256]{1,0:T(8,128)S(1)}, f32[1024,256]{1,0:T(8,128)S(1)}) custom-call(f32[1024,128]{1,0:T(8,128)S(1)} %get-tuple-element.61.grad_ref, f32[1024,128]{1,0:T(8,128)S(1)} %get-tuple-element.55.x_ref.own_ref, f32[1024,128]{1,0:T(8,128)S(1)} %collective-permute-done.12.other_ref), custom_call_target="tpu_custom_call" | custom-call | tf_op jit(solution)/shard_map/pallas_call | solution.py:414
  51.2 0.0 collective-permute-done.13.other_ref
  51.2 4.7 %shard_map.43 = (f32[1024,256]{1,0:T(8,128)S(1)}, f32[512,256]{1,0:T(8,128)S(1)}, f32[2048,256]{1,0:T(8,128)S(1)}, bf16[2,2048,256]{2,1,0:T(8,128)(2,1)S(1)}, f32[128,256]{1,0:T(8,128)S(1)}) custom-call(bf16[2048,1024]{1,0:T(8,128)(2,1)S(1)} %get-tuple-element.59.rows_ref, f32[2048,128]{1,0:T(8,128)S(1)} %get-tuple-element.60.curve_ref, ...), custom_call_target="tpu_custom_call" | custom-call | tf_op jit(solution)/shard_map/pallas_call | solution.py:414
  55.9 0.3 collective-permute-start.14
  56.2 1.4 %shard_map.45.own_ref = f32[512,256]{1,0:T(8,128)S(1)} custom-call(bf16[2048,1024]{1,0:T(8,128)(2,1)S(1)} %get-tuple-element.59.rows_ref, f32[1024,256]{1,0:T(8,128)S(1)} %get-tuple-element.62.x_ref, f32[256,256]{1,0:T(8,128)S(1)} %get-tuple-element.63.kernel_ref, f32[1024,256]{1,0:T(8,128)S(1)} %get-tuple-element.65.drift_ref, ...), custom_call_target="tpu_custom_call" | custom-call | tf_op jit(solution)/shard_map/pallas_call | solution.py:414
  57.6 0.4 collective-permute-start.15
  58.0 0.0 collective-permute-done.14.other_ref
  58.0 1.0 %shard_map.44 = (f32[512,256]{1,0:T(8,128)S(1)}, f32[2048,256]{1,0:T(8,128)S(1)}, f32[128,256]{1,0:T(8,128)S(1)}, f32[8,256]{1,0:T(8,128)S(1)}) custom-call(bf16[2048,1024]{1,0:T(8,128)(2,1)S(1)} %get-tuple-element.59.rows_ref, f32[1024,256]{1,0:T(8,128)S(1)} %get-tuple-element.62.x_ref, f32[1024,256]{1,0:T(8,128)S(1)} %get-tuple-element.65.drift_ref, ...), custom_call_target="tpu_custom_call" | custom-call | tf_op jit(solution)/shard_map/pallas_call | solution.py:414
  59.0 0.6 collective-permute-done.15.other_ref
  59.6 1.1 %shard_map.46 = (f32[512,256]{1,0:T(8,128)S(1)}, f32[8,128]{1,0:T(8,128)S(1)}) custom-call(bf16[2048,1024]{1,0:T(8,128)(2,1)S(1)} %get-tuple-element.59.rows_ref, f32[1024,256]{1,0:T(8,128)S(1)} %get-tuple-element.62.x_ref, f32[256,256]{1,0:T(8,128)S(1)} %get-tuple-element.63.kernel_ref, f32[2048,256]{1,0:T(8,128)S(1)} %get-tuple-element.68.factor_ref, ...), custom_call_target="tpu_custom_call" | custom-call | tf_op jit(solution)/shard_map/pallas_call | solution.py:414
  60.7 0.3 collective-permute-start.16
  61.0 0.9 %collective-permute-done.16.other_ref = f32[8,128]{1,0:T(8,128)S(1)} collective-permute-done((f32[8,128]{1,0:T(8,128)S(1)}, f32[8,128]{1,0:T(8,128)S(1)}, u32[]{:S(2)}, u32[]{:S(2)}) %collective-permute-start.16) | collective-permute-done | bytes 4128 | tf_op jit(solution)/shard_map/ppermute | solution.py:67
  61.9 2.8 %shard_map.48 = (f32[1024,128]{1,0:T(8,128)S(1)}, f32[2048,128]{1,0:T(8,128)S(1)}, f32[1024,256]{1,0:T(8,128)S(1)}, f32[8,128]{1,0:T(8,128)S(1)}) custom-call(bf16[2048,1024]{1,0:T(8,128)(2,1)S(1)} %get-tuple-element.59.rows_ref, bf16[2048,128]{1,0:T(8,128)(2,1)S(1)} %get-tuple-element.51.hot_ref, f32[1024,256]{1,0:T(8,128)S(1)} %get-tuple-element.62.x_ref, ...), custom_call_target="tpu_custom_call" | custom-call | tf_op jit(solution)/shard_map/pallas_call | solution.py:414
  64.6 0.6 collective-permute-start.17
  65.2 1.6 %shard_map.49 = (f32[256,256]{1,0:T(8,128)S(1)}, f32[1024,256]{1,0:T(8,128)S(1)}) custom-call(f32[1024,128]{1,0:T(8,128)S(1)} %get-tuple-element.79.grad_ref, f32[1024,256]{1,0:T(8,128)S(1)} %get-tuple-element.78.x_ref), custom_call_target="tpu_custom_call" | custom-call | tf_op jit(solution)/shard_map/pallas_call | solution.py:414
  66.9 0.0 collective-permute-done.17.other_ref
  66.9 4.7 %shard_map.50 = (f32[1024,256]{1,0:T(8,128)S(1)}, f32[512,256]{1,0:T(8,128)S(1)}, f32[2048,256]{1,0:T(8,128)S(1)}, bf16[2,2048,256]{2,1,0:T(8,128)(2,1)S(1)}, f32[128,256]{1,0:T(8,128)S(1)}) custom-call(bf16[2048,1024]{1,0:T(8,128)(2,1)S(1)} %get-tuple-element.59.rows_ref, f32[2048,128]{1,0:T(8,128)S(1)} %get-tuple-element.77.curve_ref, ...), custom_call_target="tpu_custom_call" | custom-call | tf_op jit(solution)/shard_map/pallas_call | solution.py:414
  71.6 0.3 collective-permute-start.18
  71.9 1.4 %shard_map.52.own_ref = f32[512,256]{1,0:T(8,128)S(1)} custom-call(bf16[2048,1024]{1,0:T(8,128)(2,1)S(1)} %get-tuple-element.59.rows_ref, f32[1024,256]{1,0:T(8,128)S(1)} %get-tuple-element.78.x_ref, f32[256,256]{1,0:T(8,128)S(1)} %get-tuple-element.80.kernel_ref, f32[1024,256]{1,0:T(8,128)S(1)} %get-tuple-element.82.drift_ref, ...), custom_call_target="tpu_custom_call" | custom-call | tf_op jit(solution)/shard_map/pallas_call | solution.py:414
  73.3 0.4 collective-permute-start.19
  73.7 0.0 collective-permute-done.18.other_ref
  73.7 1.0 %shard_map.51 = (f32[512,256]{1,0:T(8,128)S(1)}, f32[2048,256]{1,0:T(8,128)S(1)}, f32[128,256]{1,0:T(8,128)S(1)}, f32[8,256]{1,0:T(8,128)S(1)}) custom-call(bf16[2048,1024]{1,0:T(8,128)(2,1)S(1)} %get-tuple-element.59.rows_ref, f32[1024,256]{1,0:T(8,128)S(1)} %get-tuple-element.78.x_ref, f32[1024,256]{1,0:T(8,128)S(1)} %get-tuple-element.82.drift_ref, ...), custom_call_target="tpu_custom_call" | custom-call | tf_op jit(solution)/shard_map/pallas_call | solution.py:414
  74.7 0.6 collective-permute-done.19.other_ref
  75.3 1.1 %shard_map.53 = (f32[512,256]{1,0:T(8,128)S(1)}, f32[8,128]{1,0:T(8,128)S(1)}) custom-call(bf16[2048,1024]{1,0:T(8,128)(2,1)S(1)} %get-tuple-element.59.rows_ref, f32[1024,256]{1,0:T(8,128)S(1)} %get-tuple-element.78.x_ref, f32[256,256]{1,0:T(8,128)S(1)} %get-tuple-element.80.kernel_ref, f32[2048,256]{1,0:T(8,128)S(1)} %get-tuple-element.85.factor_ref, ...), custom_call_target="tpu_custom_call" | custom-call | tf_op jit(solution)/shard_map/pallas_call | solution.py:414
  76.4 0.3 collective-permute-start.20
  76.7 0.1 shard_map.47.before_ref
  76.8 0.1 shard_map.54.own_ref
  76.9 0.6 collective-permute-done.20.other_ref
  77.5 0.7 shard_map.55
  (4 shorter events, 0.1 us)
Async XLA Ops:
  22.6 4.6 %collective-permute-start = (bf16[8,48,256]{2,1,0:T(8,128)(2,1)S(1)}, bf16[8,48,256]{2,1,0:T(8,128)(2,1)S(1)}, u32[]{:S(2)}, u32[]{:S(2)}) collective-permute-start(bf16[8,48,256]{2,1,0:T(8,128)(2,1)S(1)} %get-tuple-element.95), channel_id=1, source_target_pairs={{0,24},{1,25},{2,26},{3,27},{4,12},{5,13},{6,14},{7,15},{8,16},{9,... | collective-permute-start | bytes 589832 | tf_op jit(solution)/shard_map/ppermute | solution.py:77
  22.7 4.7 %collective-permute-start.3 = (bf16[8,48,256]{2,1,0:T(8,128)(2,1)S(1)}, bf16[8,48,256]{2,1,0:T(8,128)(2,1)S(1)}, u32[]{:S(2)}, u32[]{:S(2)}) collective-permute-start(bf16[8,48,256]{2,1,0:T(8,128)(2,1)S(1)} %get-tuple-element.94), channel_id=1, source_target_pairs={{0,96},{1,97},{2,98},{3,99},{4,36},{5,37},{6,38},{7,39},{8,104},{9... | collective-permute-start | bytes 589832 | tf_op jit(solution)/shard_map/ppermute | solution.py:77
  22.8 6.1 %collective-permute-start.6 = (bf16[8,48,256]{2,1,0:T(8,128)(2,1)S(1)}, bf16[8,48,256]{2,1,0:T(8,128)(2,1)S(1)}, u32[]{:S(2)}, u32[]{:S(2)}) collective-permute-start(bf16[8,48,256]{2,1,0:T(8,128)(2,1)S(1)} %get-tuple-element.93), channel_id=1, source_target_pairs={{0,3},{1,2},{2,1},{3,0},{4,5},{5,4},{6,7},{7,6},{8,11},{9,10},{10,... | collective-permute-start | bytes 589832 | tf_op jit(solution)/shard_map/ppermute | solution.py:77
  27.3 7.0 %collective-permute-start.2 = (bf16[16,48,256]{2,1,0:T(8,128)(2,1)S(1)}, bf16[16,48,256]{2,1,0:T(8,128)(2,1)S(1)}, u32[]{:S(2)}, u32[]{:S(2)}) collective-permute-start(bf16[16,48,256]{2,1,0:T(8,128)(2,1)S(1)} %pad_maximum_fusion.refs_0_), channel_id=1, source_target_pairs={{0,3},{1,2},{2,1},{3,0},{4,5},{5,4},{6,7},{7,6},{8,11},{9,10},{10,... | collective-permute-start | bytes 1179656 | tf_op jit(solution)/shard_map/ppermute | solution.py:77
  27.3 7.0 %collective-permute-start.1 = (bf16[16,48,256]{2,1,0:T(8,128)(2,1)S(1)}, bf16[16,48,256]{2,1,0:T(8,128)(2,1)S(1)}, u32[]{:S(2)}, u32[]{:S(2)}) collective-permute-start(bf16[16,48,256]{2,1,0:T(8,128)(2,1)S(1)} %pad_maximum_fusion.refs_0_), channel_id=1, source_target_pairs={{0,96},{1,97},{2,98},{3,99},{4,36},{5,37},{6,38},{7,39},{8,104},{9... | collective-permute-start | bytes 1179656 | tf_op jit(solution)/shard_map/ppermute | solution.py:77
  27.5 11.0 %collective-permute-start.4 = (bf16[16,48,256]{2,1,0:T(8,128)(2,1)S(1)}, bf16[16,48,256]{2,1,0:T(8,128)(2,1)S(1)}, u32[]{:S(2)}, u32[]{:S(2)}) collective-permute-start(bf16[16,48,256]{2,1,0:T(8,128)(2,1)S(1)} %pad_maximum_fusion.1.refs_3_), channel_id=1, source_target_pairs={{0,3},{1,2},{2,1},{3,0},{4,5},{5,4},{6,7},{7,6},{8,11},{9,10},{10,... | collective-permute-start | bytes 1179656 | tf_op jit(solution)/shard_map/ppermute | solution.py:77
  29.0 9.5 %collective-permute-start.7 = (bf16[16,48,256]{2,1,0:T(8,128)(2,1)S(1)}, bf16[16,48,256]{2,1,0:T(8,128)(2,1)S(1)}, u32[]{:S(2)}, u32[]{:S(2)}) collective-permute-start(bf16[16,48,256]{2,1,0:T(8,128)(2,1)S(1)} %pad_maximum_fusion.2.refs_6_), channel_id=1, source_target_pairs={{0,24},{1,25},{2,26},{3,27},{4,12},{5,13},{6,14},{7,15},{8,16},{9,... | collective-permute-start | bytes 1179656 | tf_op jit(solution)/shard_map/ppermute | solution.py:77
  29.2 10.9 %collective-permute-start.5 = (bf16[16,48,256]{2,1,0:T(8,128)(2,1)S(1)}, bf16[16,48,256]{2,1,0:T(8,128)(2,1)S(1)}, u32[]{:S(2)}, u32[]{:S(2)}) collective-permute-start(bf16[16,48,256]{2,1,0:T(8,128)(2,1)S(1)} %pad_maximum_fusion.1.refs_3_), channel_id=1, source_target_pairs={{0,24},{1,25},{2,26},{3,27},{4,12},{5,13},{6,14},{7,15},{8,16},{9,... | collective-permute-start | bytes 1179656 | tf_op jit(solution)/shard_map/ppermute | solution.py:77
  34.3 6.9 %collective-permute-start.8 = (bf16[16,48,256]{2,1,0:T(8,128)(2,1)S(1)}, bf16[16,48,256]{2,1,0:T(8,128)(2,1)S(1)}, u32[]{:S(2)}, u32[]{:S(2)}) collective-permute-start(bf16[16,48,256]{2,1,0:T(8,128)(2,1)S(1)} %pad_maximum_fusion.2.refs_6_), channel_id=1, source_target_pairs={{0,96},{1,97},{2,98},{3,99},{4,36},{5,37},{6,38},{7,39},{8,104},{9... | collective-permute-start | bytes 1179656 | tf_op jit(solution)/shard_map/ppermute | solution.py:77
  34.4 8.3 %collective-permute-start.9 = (bf16[16,48,256]{2,1,0:T(8,128)(2,1)S(1)}, bf16[16,48,256]{2,1,0:T(8,128)(2,1)S(1)}, u32[]{:S(2)}, u32[]{:S(2)}) collective-permute-start(bf16[16,48,256]{2,1,0:T(8,128)(2,1)S(1)} %collective-permute-done.1.refs_1_), channel_id=1, source_target_pairs={{0,3},{1,2},{2,1},{3,0},{4,5},{5,4},{6,7},{7,6},{8,11},{9,10},{10,... | collective-permute-start | bytes 1179656 | tf_op jit(solution)/shard_map/ppermute | solution.py:77
  38.5 6.9 %collective-permute-start.10 = (bf16[16,48,256]{2,1,0:T(8,128)(2,1)S(1)}, bf16[16,48,256]{2,1,0:T(8,128)(2,1)S(1)}, u32[]{:S(2)}, u32[]{:S(2)}) collective-permute-start(bf16[16,48,256]{2,1,0:T(8,128)(2,1)S(1)} %collective-permute-done.4.refs_4_), channel_id=1, source_target_pairs={{0,24},{1,25},{2,26},{3,27},{4,12},{5,13},{6,14},{7,15},{8,16},{9,... | collective-permute-start | bytes 1179656 | tf_op jit(solution)/shard_map/ppermute | solution.py:77
  38.5 8.2 %collective-permute-start.11 = (bf16[16,48,256]{2,1,0:T(8,128)(2,1)S(1)}, bf16[16,48,256]{2,1,0:T(8,128)(2,1)S(1)}, u32[]{:S(2)}, u32[]{:S(2)}) collective-permute-start(bf16[16,48,256]{2,1,0:T(8,128)(2,1)S(1)} %collective-permute-done.7.refs_7_), channel_id=1, source_target_pairs={{0,96},{1,97},{2,98},{3,99},{4,36},{5,37},{6,38},{7,39},{8,104},{9... | collective-permute-start | bytes 1179656 | tf_op jit(solution)/shard_map/ppermute | solution.py:77
  43.8 5.7 %collective-permute-start.12 = (f32[1024,128]{1,0:T(8,128)S(1)}, f32[1024,128]{1,0:T(8,128)S(1)}, u32[]{:S(2)}, u32[]{:S(2)}) collective-permute-start(f32[1024,128]{1,0:T(8,128)S(1)} %get-tuple-element.55.x_ref.own_ref), channel_id=1, source_target_pairs={{0,4},{4,0},{1,5},{5,1},{2,6},{6,2},{3,7},{7,3},{8,12},{12,8},{9,1... | collective-permute-start | bytes 1572872 | tf_op jit(solution)/shard_map/ppermute | solution.py:67
  48.0 3.2 %collective-permute-start.13 = (f32[1024,128]{1,0:T(8,128)S(1)}, f32[1024,128]{1,0:T(8,128)S(1)}, u32[]{:S(2)}, u32[]{:S(2)}) collective-permute-start(f32[1024,128]{1,0:T(8,128)S(1)} %get-tuple-element.61.grad_ref), channel_id=1, source_target_pairs={{0,4},{4,0},{1,5},{5,1},{2,6},{6,2},{3,7},{7,3},{8,12},{12,8},{9,1... | collective-permute-start | bytes 1572872 | tf_op jit(solution)/shard_map/ppermute | solution.py:67
  55.9 2.1 %collective-permute-start.14 = (f32[512,256]{1,0:T(8,128)S(1)}, f32[512,256]{1,0:T(8,128)S(1)}, u32[]{:S(2)}, u32[]{:S(2)}) collective-permute-start(f32[512,256]{1,0:T(8,128)S(1)} %get-tuple-element.66.own_ref), channel_id=1, source_target_pairs={{0,4},{4,0},{1,5},{5,1},{2,6},{6,2},{3,7},{7,3},{8,12},{12,8},{9,1... | collective-permute-start | bytes 1572872 | tf_op jit(solution)/shard_map/ppermute | solution.py:67
  57.6 2.0 %collective-permute-start.15 = (f32[512,256]{1,0:T(8,128)S(1)}, f32[512,256]{1,0:T(8,128)S(1)}, u32[]{:S(2)}, u32[]{:S(2)}) collective-permute-start(f32[512,256]{1,0:T(8,128)S(1)} %shard_map.45.own_ref), channel_id=1, source_target_pairs={{0,4},{4,0},{1,5},{5,1},{2,6},{6,2},{3,7},{7,3},{8,12},{12,8},{9,1... | collective-permute-start | bytes 1572872 | tf_op jit(solution)/shard_map/ppermute | solution.py:67
  60.7 1.2 %collective-permute-start.16 = (f32[8,128]{1,0:T(8,128)S(1)}, f32[8,128]{1,0:T(8,128)S(1)}, u32[]{:S(2)}, u32[]{:S(2)}) collective-permute-start(f32[8,128]{1,0:T(8,128)S(1)} %get-tuple-element.75.own_ref), channel_id=1, source_target_pairs={{0,4},{4,0},{1,5},{5,1},{2,6},{6,2},{3,7},{7,3},{8,12},{12,8},{9,1... | collective-permute-start | bytes 12296 | tf_op jit(solution)/shard_map/ppermute | solution.py:67
  64.6 2.2 %collective-permute-start.17 = (f32[1024,128]{1,0:T(8,128)S(1)}, f32[1024,128]{1,0:T(8,128)S(1)}, u32[]{:S(2)}, u32[]{:S(2)}) collective-permute-start(f32[1024,128]{1,0:T(8,128)S(1)} %get-tuple-element.79.grad_ref), channel_id=1, source_target_pairs={{0,4},{4,0},{1,5},{5,1},{2,6},{6,2},{3,7},{7,3},{8,12},{12,8},{9,1... | collective-permute-start | bytes 1572872 | tf_op jit(solution)/shard_map/ppermute | solution.py:67
  71.6 2.1 %collective-permute-start.18 = (f32[512,256]{1,0:T(8,128)S(1)}, f32[512,256]{1,0:T(8,128)S(1)}, u32[]{:S(2)}, u32[]{:S(2)}) collective-permute-start(f32[512,256]{1,0:T(8,128)S(1)} %get-tuple-element.83.own_ref), channel_id=1, source_target_pairs={{0,4},{4,0},{1,5},{5,1},{2,6},{6,2},{3,7},{7,3},{8,12},{12,8},{9,1... | collective-permute-start | bytes 1572872 | tf_op jit(solution)/shard_map/ppermute | solution.py:67
  73.3 2.0 %collective-permute-start.19 = (f32[512,256]{1,0:T(8,128)S(1)}, f32[512,256]{1,0:T(8,128)S(1)}, u32[]{:S(2)}, u32[]{:S(2)}) collective-permute-start(f32[512,256]{1,0:T(8,128)S(1)} %shard_map.52.own_ref), channel_id=1, source_target_pairs={{0,4},{4,0},{1,5},{5,1},{2,6},{6,2},{3,7},{7,3},{8,12},{12,8},{9,1... | collective-permute-start | bytes 1572872 | tf_op jit(solution)/shard_map/ppermute | solution.py:67
  76.4 1.2 %collective-permute-start.20 = (f32[8,128]{1,0:T(8,128)S(1)}, f32[8,128]{1,0:T(8,128)S(1)}, u32[]{:S(2)}, u32[]{:S(2)}) collective-permute-start(f32[8,128]{1,0:T(8,128)S(1)} %get-tuple-element.92.sums_ref), channel_id=1, source_target_pairs={{0,4},{4,0},{1,5},{5,1},{2,6},{6,2},{3,7},{7,3},{8,12},{12,8},{9,1... | collective-permute-start | bytes 12296 | tf_op jit(solution)/shard_map/ppermute | solution.py:67

commit v5 on v4

--- a/solution.py
+++ b/solution.py
@@ -34,7 +34,7 @@
 ROWS = (512, 768, 768)
 STARTS = (0, 512, 1280)
 CHUNK = 256
-LONG_CHUNK = 512
+LONG_CHUNK = 2048
 
 
 def places():
@@ -266,9 +266,13 @@
     out_ref[1] = on_drift * own_ref[0] + on_image * own_ref[1]
 
 
-def similarity(x, grad_ref, kernel_ref, drift_ref):
+def similarity(x_ref, grad_ref, kernel_ref, drift_ref, turned_ref):
+    x = x_ref[...]
+    for k, value in enumerate(two(x_ref[:, half_of(lax.axis_index("c"))].T)):
+        turned_ref[k] = value
     high, low = two(x)
-    gram = tn(high, high) + (tn(high, low) + tn(low, high))
+    mixed = tn(high, low)
+    gram = tn(high, high) + (mixed + mixed.T)
     shape = (MANY, MANY)
     same = lax.broadcasted_iota(jnp.int32, shape, 0) == lax.broadcasted_iota(jnp.int32, shape, 1)
     diag = jnp.where(same, gram, 0.0)
@@ -280,14 +284,14 @@
     drift_ref[...] = (2.0 / scale) * total * x + stacked(two(grad_ref[...]), own)
 
 
-def start_kernel(grad_ref, own_ref, other_ref, kernel_ref, drift_ref, x_ref):
+def start_kernel(grad_ref, own_ref, other_ref, kernel_ref, drift_ref, turned_ref, x_ref):
     x = in_order(lax.axis_index("c"), own_ref[...], other_ref[...], 1)
     x_ref[...] = x
-    similarity(x, grad_ref, kernel_ref, drift_ref)
-
-
-def again_kernel(grad_ref, x_ref, kernel_ref, drift_ref):
-    similarity(x_ref[...], grad_ref, kernel_ref, drift_ref)
+    similarity(x_ref, grad_ref, kernel_ref, drift_ref, turned_ref)
+
+
+def again_kernel(grad_ref, x_ref, kernel_ref, drift_ref, turned_ref):
+    similarity(x_ref, grad_ref, kernel_ref, drift_ref, turned_ref)
 
 
 def spread(rows_ref, weighted_ref, near):
@@ -307,7 +311,7 @@
 
 
 def first_kernel(
-    rows_ref, curve_ref, x_ref, kernel_ref, own_ref, other_ref,
+    rows_ref, curve_ref, x_ref, turned_ref, kernel_ref, own_ref, other_ref,
     drift_ref, image_ref, factor_ref, weighted_ref, q_ref, square_ref,
 ):
     core = lax.axis_index("c")
@@ -333,7 +337,7 @@
         high, low = two((nn(rows, drift_two[0]) + nn(rows, drift_two[1])) * factor)
         weighted_ref[0, to, :] = high
         weighted_ref[1, to, :] = low
-    along = stacked(two(x_ref[:, mine].T), drift_two)
+    along = stacked((turned_ref[0], turned_ref[1]), drift_two)
     q = square * (jnp.sum(x * drift, axis=0, keepdims=True) - along)
     q_ref[...] = q
     near = slice(0, WIDE // 2)
@@ -349,7 +353,7 @@
     )
 
 
-def read_image(near, x_ref, drift_ref, image):
+def read_image(near, x_ref, turned_ref, drift_ref, image):
     rounded = image.astype(bf16)
     wide = rounded.astype(f32)
     pairs_ = (
@@ -361,18 +365,18 @@
         (x_ref[near, :], image),
     )
     sums = [jnp.sum(a * b, axis=0, keepdims=True) for a, b in pairs_]
-    x_own = x_ref[near, half_of(lax.axis_index("c"))]
-    return sums, stacked(two(x_own.T), two(image)), rounded
+    x_own = (turned_ref[0, :, near], turned_ref[1, :, near])
+    return sums, stacked(x_own, two(image)), rounded
 
 
 def second_kernel(
-    rows_ref, x_ref, drift_ref, own_ref, other_ref,
+    rows_ref, x_ref, turned_ref, drift_ref, own_ref, other_ref,
     image_ref, projected_ref, along_ref, sums_ref,
 ):
     near = slice(0, WIDE // 2)
     image = own_ref[...] + other_ref[...]
     image_ref[...] = image
-    sums, along, rounded = read_image(near, x_ref, drift_ref, image)
+    sums, along, rounded = read_image(near, x_ref, turned_ref, drift_ref, image)
     along_ref[...] = along
     for at, value in enumerate(sums):
         sums_ref[at : at + 1, :] = value
@@ -381,14 +385,14 @@
 
 
 def third_kernel(
-    rows_ref, x_ref, kernel_ref, factor_ref, drift_ref, projected_ref, along_ref, before_ref,
+    rows_ref, x_ref, turned_ref, kernel_ref, factor_ref, drift_ref, projected_ref, along_ref, before_ref,
     own_ref, other_ref,
     image_ref, sums_ref,
 ):
     near = slice(WIDE // 2, WIDE)
     image = own_ref[...] + other_ref[...]
     image_ref[...] = image
-    sums, along, rounded = read_image(near, x_ref, drift_ref, image)
+    sums, along, rounded = read_image(near, x_ref, turned_ref, drift_ref, image)
     sums = [value + before_ref[at : at + 1, :] for at, value in enumerate(sums)]
     total = jnp.zeros((1, MANY), f32)
     for at in range(0, HALF * DATA, LONG_CHUNK):
@@ -446,6 +450,7 @@
     turn = [pltpu.VMEM((HALF, SLICE), f32)]
     rows_of = ((count, WIDE), bf16)
     tail_of = ((HALF, WIDE), f32)
+    turned_of = ((2, HALF, WIDE), bf16)
     curve_of = ((count, HALF), f32)
     rows, tail, hot = call(
         early_kernel,
@@ -466,8 +471,8 @@
             rows, grad, curve, hot, x_own, pieces[color][3],
             aliases={0: 0, 1: 1, 2: 2},
         )
-    kernel, partial_drift, x = call(
-        start_kernel, [square, long, long], grad, x_own, x_other
+    kernel, partial_drift, turned, x = call(
+        start_kernel, [square, long, turned_of, long], grad, x_own, x_other
     )
     own = []
     for newton_step in range(NEWTON):
@@ -478,11 +483,13 @@
             )
         grad_other = swap_cores(grad)
         if newton_step > 0:
-            kernel, partial_drift = call(again_kernel, [square, long], grad, x)
+            kernel, partial_drift, turned = call(
+                again_kernel, [square, long, turned_of], grad, x
+            )
         drift, own_a, factor, weighted, q = call(
             first_kernel,
             [long, wing, tall, ((2, count, MANY), bf16), low],
-            rows, curve, x, kernel, partial_drift, grad_other,
+            rows, curve, x, turned, kernel, partial_drift, grad_other,
             scratch=[pltpu.VMEM((HALF, MANY), f32)],
         )
         other_a = swap_cores(own_a)
@@ -490,11 +497,11 @@
         other_b = swap_cores(own_b)
         image_a, projected, along, partial_sums = call(
             second_kernel, [wing, tall, low, ((8, MANY), f32)],
-            rows, x, drift, own_a, other_a,
+            rows, x, turned, drift, own_a, other_a,
         )
         image_b, sums = call(
             third_kernel, [wing, ((8, HALF), f32)],
-            rows, x, kernel, factor, drift, projected, along, partial_sums, own_b, other_b,
+            rows, x, turned, kernel, factor, drift, projected, along, partial_sums, own_b, other_b,
         )
         image = (image_a, image_b)
         sums_other = swap_cores(sums)

time: 78.4 us -> 78.2 us (level)
  waiting for transfers between devices: 17 us -> 18.4 us
  Pallas kernels: 28.8 us -> 27.5 us
    pallas_call x19, Pallas kernels: 28.8 us -> 27.5 us  [call(): pl.pallas_call(kernel, out_shape=[pltpu.VMEM(s, t) if far else jax.ShapeD...]
    ppermute x9, waiting for transfers between devices: 2.68 us -> 3.98 us  [swap_cores(): return lax.ppermute(x, 'c', [(0, 1), (1, 0)])]
  transfers between devices with their start and end apart: 21 -> 21, of which waited for: 12 -> 14; matrix products, arithmetic and copies ran while one was open for 0% -> 0% of each run, Pallas kernels for 16% -> 15%
where the time goes in v5:
time: 78.2 us; the launch traced here: 78 us
  Pallas kernels  27.5 us (35%)
  blocking collectives  21.5 us (27%)
  waiting for transfers between devices  18.4 us (24%)
  starting transfers between devices  10.2 us (13%)
    pallas_call x19, Pallas kernels, call(): pl.pallas_call(kernel, out_shape=[pltpu.VMEM(s, t) if far else jax.ShapeD...  27.5 us
    all_to_all x1, blocking collectives, gathered(): lax.all_to_all(copies, AXES, 0, 0, axis_index_groups=cubes(), tiled=True)  21.5 us
    ppermute x12, waiting for transfers between devices, sent(): out.append(lax.ppermute(part, AXES, pairs(order[step])))  14.4 us
    ppermute x12, starting transfers between devices, sent(): out.append(lax.ppermute(part, AXES, pairs(order[step])))  5.18 us
    ppermute x9, starting transfers between devices, swap_cores(): return lax.ppermute(x, 'c', [(0, 1), (1, 0)])  5.05 us
    ppermute x9, waiting for transfers between devices, swap_cores(): return lax.ppermute(x, 'c', [(0, 1), (1, 0)])  3.98 us
  transfers between devices with their start and end apart: 21, of which 14 were waited for; matrix products, arithmetic and copies ran while one was open for 0% of the time, Pallas kernels for 15%

profile of v5, /device:TPU:1, one launch (start us, length us, event | category | flops | bytes accessed | tf_op | source)
XLA Modules:
  0.0 78.0 jit_solution(3715320093456075184)
XLA Ops:
  0.0 1.1 %shard_map.37 = bf16[8,144,256]{2,1,0:T(8,128)(2,1)S(1)} custom-call(f32[8,256]{1,0:T(8,128)} %x_far.1, bf16[8,16,256]{2,1,0:T(8,128)(2,1)} %rows_far.1, s32[8,16]{1,0:T(8,128)} %labels_far.1), custom_call_target="tpu_custom_call" | custom-call | tf_op jit(solution)/shard_map/pallas_call | solution.py:418
  1.1 21.5 %all_to_all.5 = bf16[8,144,256]{2,1,0:T(8,128)(2,1)S(1)} all-to-all(bf16[8,144,256]{2,1,0:T(8,128)(2,1)S(1)} %shard_map.37), channel_id=1, replica_groups={{0,1,8,9,32,33,40,41},{2,3,10,11,34,35,42,43},{4,7,28,31,100,103,124,12..., dimensions={0} | all-to-all | bytes 1179648 | tf_op jit(solution)/shard_map/all_to_all | solution.py:71
  22.6 0.1 collective-permute-start
  22.7 0.1 collective-permute-start.3
  22.8 0.1 collective-permute-start.6
  22.9 4.3 %collective-permute-done = bf16[8,48,256]{2,1,0:T(8,128)(2,1)S(1)} collective-permute-done((bf16[8,48,256]{2,1,0:T(8,128)(2,1)S(1)}, bf16[8,48,256]{2,1,0:T(8,128)(2,1)S(1)}, u32[]{:S(2)}, u32[]{:S(2)}) %collective-permute-start) | collective-permute-done | bytes 196640 | tf_op jit(solution)/shard_map/ppermute | solution.py:77
  27.3 0.1 collective-permute-start.2
  27.4 0.1 collective-permute-start.1
  27.4 0.0 collective-permute-done.3
  27.5 1.4 %collective-permute-start.4 = (bf16[16,48,256]{2,1,0:T(8,128)(2,1)S(1)}, bf16[16,48,256]{2,1,0:T(8,128)(2,1)S(1)}, u32[]{:S(2)}, u32[]{:S(2)}) collective-permute-start(bf16[16,48,256]{2,1,0:T(8,128)(2,1)S(1)} %pad_maximum_fusion.1.refs_3_), channel_id=1, source_target_pairs={{0,3},{1,2},{2,1},{3,0},{4,5},{5,4},{6,7},{7,6},{8,11},{9,10},{10,... | collective-permute-start | bytes 1179656 | tf_op jit(solution)/shard_map/ppermute | solution.py:77
  28.9 0.0 collective-permute-done.6
  29.0 0.3 collective-permute-start.7
  29.2 1.3 %collective-permute-start.5 = (bf16[16,48,256]{2,1,0:T(8,128)(2,1)S(1)}, bf16[16,48,256]{2,1,0:T(8,128)(2,1)S(1)}, u32[]{:S(2)}, u32[]{:S(2)}) collective-permute-start(bf16[16,48,256]{2,1,0:T(8,128)(2,1)S(1)} %pad_maximum_fusion.1.refs_3_), channel_id=1, source_target_pairs={{0,24},{1,25},{2,26},{3,27},{4,12},{5,13},{6,14},{7,15},{8,16},{9,... | collective-permute-start | bytes 1179656 | tf_op jit(solution)/shard_map/ppermute | solution.py:77
  30.5 3.7 %collective-permute-done.2.refs_2_ = bf16[16,48,256]{2,1,0:T(8,128)(2,1)S(1)} collective-permute-done((bf16[16,48,256]{2,1,0:T(8,128)(2,1)S(1)}, bf16[16,48,256]{2,1,0:T(8,128)(2,1)S(1)}, u32[]{:S(2)}, u32[]{:S(2)}) %collective-permute-start.2) | collective-permute-done | bytes 393248 | tf_op jit(solution)/shard_map/ppermute | solution.py:77
  34.3 0.0 collective-permute-start.8
  34.3 0.1 collective-permute-done.1.refs_1_
  34.4 1.4 %collective-permute-start.9 = (bf16[16,48,256]{2,1,0:T(8,128)(2,1)S(1)}, bf16[16,48,256]{2,1,0:T(8,128)(2,1)S(1)}, u32[]{:S(2)}, u32[]{:S(2)}) collective-permute-start(bf16[16,48,256]{2,1,0:T(8,128)(2,1)S(1)} %collective-permute-done.1.refs_1_), channel_id=1, source_target_pairs={{0,3},{1,2},{2,1},{3,0},{4,5},{5,4},{6,7},{7,6},{8,11},{9,10},{10,... | collective-permute-start | bytes 1179656 | tf_op jit(solution)/shard_map/ppermute | solution.py:77
  35.7 2.7 %collective-permute-done.4.refs_4_ = bf16[16,48,256]{2,1,0:T(8,128)(2,1)S(1)} collective-permute-done((bf16[16,48,256]{2,1,0:T(8,128)(2,1)S(1)}, bf16[16,48,256]{2,1,0:T(8,128)(2,1)S(1)}, u32[]{:S(2)}, u32[]{:S(2)}) %collective-permute-start.4) | collective-permute-done | bytes 393248 | tf_op jit(solution)/shard_map/ppermute | solution.py:77
  38.5 0.0 collective-permute-start.10
  38.5 0.0 collective-permute-done.7.refs_7_
  38.5 0.4 collective-permute-start.11
  38.9 1.3 %collective-permute-done.5.refs_5_ = bf16[16,48,256]{2,1,0:T(8,128)(2,1)S(1)} collective-permute-done((bf16[16,48,256]{2,1,0:T(8,128)(2,1)S(1)}, bf16[16,48,256]{2,1,0:T(8,128)(2,1)S(1)}, u32[]{:S(2)}, u32[]{:S(2)}) %collective-permute-start.5) | collective-permute-done | bytes 393248 | tf_op jit(solution)/shard_map/ppermute | solution.py:77
  40.2 1.0 %collective-permute-done.8.refs_8_ = bf16[16,48,256]{2,1,0:T(8,128)(2,1)S(1)} collective-permute-done((bf16[16,48,256]{2,1,0:T(8,128)(2,1)S(1)}, bf16[16,48,256]{2,1,0:T(8,128)(2,1)S(1)}, u32[]{:S(2)}, u32[]{:S(2)}) %collective-permute-start.8) | collective-permute-done | bytes 393248 | tf_op jit(solution)/shard_map/ppermute | solution.py:77
  41.2 0.7 shard_map.38
  41.9 0.8 %collective-permute-done.9.d = bf16[16,48,256]{2,1,0:T(8,128)(2,1)S(1)} collective-permute-done((bf16[16,48,256]{2,1,0:T(8,128)(2,1)S(1)}, bf16[16,48,256]{2,1,0:T(8,128)(2,1)S(1)}, u32[]{:S(2)}, u32[]{:S(2)}) %collective-permute-start.9) | collective-permute-done | bytes 393248 | tf_op jit(solution)/shard_map/ppermute | solution.py:77
  42.7 1.1 %shard_map.39 = (bf16[2048,1024]{1,0:T(8,128)(2,1)S(1)}, f32[128,1024]{1,0:T(8,128)S(1)}, f32[1024,128]{1,0:T(8,128)S(1)}, f32[1024,128]{1,0:T(8,128)S(1)}, f32[2048,128]{1,0:T(8,128)S(1)}) custom-call(bf16[2048,1024]{1,0:T(8,128)(2,1)S(1)} %get-tuple-element.51._, ...), custom_call_target="tpu_custom_call", output_to_operand_aliasing={{0}: (0, {}), {1}: (1, {})} | custom-call | tf_op jit(solution)/shard_map/pallas_call | solution.py:418
  43.8 1.2 %collective-permute-start.12 = (f32[1024,128]{1,0:T(8,128)S(1)}, f32[1024,128]{1,0:T(8,128)S(1)}, u32[]{:S(2)}, u32[]{:S(2)}) collective-permute-start(f32[1024,128]{1,0:T(8,128)S(1)} %get-tuple-element.57.x_ref.own_ref), channel_id=1, source_target_pairs={{0,4},{4,0},{1,5},{5,1},{2,6},{6,2},{3,7},{7,3},{8,12},{12,8},{9,1... | collective-permute-start | bytes 1572872 | tf_op jit(solution)/shard_map/ppermute | solution.py:67
  45.0 0.4 collective-permute-done.10.d
  45.4 1.3 %shard_map.40 = (bf16[2048,1024]{1,0:T(8,128)(2,1)S(1)}, f32[1024,128]{1,0:T(8,128)S(1)}, f32[2048,128]{1,0:T(8,128)S(1)}) custom-call(bf16[2048,1024]{1,0:T(8,128)(2,1)S(1)} %get-tuple-element.54._, f32[1024,128]{1,0:T(8,128)S(1)} %get-tuple-element.55.before_ref, ...), custom_call_target="tpu_custom_call", output_to_operand_aliasing={{0}: (0, {}), {1}: (1, {}), {2}: (2, {})} | custom-call | tf_op jit(solution)/shard_map/pallas_call | solution.py:418
  46.7 0.0 collective-permute-done.11.d
  46.7 1.3 %shard_map.41 = (bf16[2048,1024]{1,0:T(8,128)(2,1)S(1)}, f32[1024,128]{1,0:T(8,128)S(1)}, f32[2048,128]{1,0:T(8,128)S(1)}) custom-call(bf16[2048,1024]{1,0:T(8,128)(2,1)S(1)} %get-tuple-element.58._, f32[1024,128]{1,0:T(8,128)S(1)} %get-tuple-element.59.before_ref, ...), custom_call_target="tpu_custom_call", output_to_operand_aliasing={{0}: (0, {}), {1}: (1, {}), {2}: (2, {})} | custom-call | tf_op jit(solution)/shard_map/pallas_call | solution.py:418
  48.0 1.5 %collective-permute-start.13 = (f32[1024,128]{1,0:T(8,128)S(1)}, f32[1024,128]{1,0:T(8,128)S(1)}, u32[]{:S(2)}, u32[]{:S(2)}) collective-permute-start(f32[1024,128]{1,0:T(8,128)S(1)} %get-tuple-element.63.grad_ref), channel_id=1, source_target_pairs={{0,4},{4,0},{1,5},{5,1},{2,6},{6,2},{3,7},{7,3},{8,12},{12,8},{9,1... | collective-permute-start | bytes 1572872 | tf_op jit(solution)/shard_map/ppermute | solution.py:67
  49.5 0.0 collective-permute-done.12.other_ref
  49.5 1.2 %shard_map.42 = (f32[256,256]{1,0:T(8,128)S(1)}, f32[1024,256]{1,0:T(8,128)S(1)}, bf16[2,128,1024]{2,1,0:T(8,128)(2,1)S(1)}, f32[1024,256]{1,0:T(8,128)S(1)}) custom-call(f32[1024,128]{1,0:T(8,128)S(1)} %get-tuple-element.63.grad_ref, f32[1024,128]{1,0:T(8,128)S(1)} %get-tuple-element.57.x_ref.own_ref, f32[1024,128]{1,0:T(8,128)S(1)} %collective-permute-done.12.other_ref), custom_call_target="tpu_custom_call" | custom-call | tf_op jit(solution)/shard_map/pallas_call | solution.py:418
  50.7 0.4 collective-permute-done.13.other_ref
  51.1 4.6 %shard_map.43 = (f32[1024,256]{1,0:T(8,128)S(1)}, f32[512,256]{1,0:T(8,128)S(1)}, f32[2048,256]{1,0:T(8,128)S(1)}, bf16[2,2048,256]{2,1,0:T(8,128)(2,1)S(1)}, f32[128,256]{1,0:T(8,128)S(1)}) custom-call(bf16[2048,1024]{1,0:T(8,128)(2,1)S(1)} %get-tuple-element.61.rows_ref, f32[2048,128]{1,0:T(8,128)S(1)} %get-tuple-element.62.curve_ref, ...), custom_call_target="tpu_custom_call" | custom-call | tf_op jit(solution)/shard_map/pallas_call | solution.py:418
  55.7 0.4 collective-permute-start.14
  56.1 1.4 %shard_map.45.own_ref = f32[512,256]{1,0:T(8,128)S(1)} custom-call(bf16[2048,1024]{1,0:T(8,128)(2,1)S(1)} %get-tuple-element.61.rows_ref, f32[1024,256]{1,0:T(8,128)S(1)} %get-tuple-element.64.x_ref, f32[256,256]{1,0:T(8,128)S(1)} %get-tuple-element.66.kernel_ref, f32[1024,256]{1,0:T(8,128)S(1)} %get-tuple-element.68.drift_ref, ...), custom_call_target="tpu_custom_call" | custom-call | tf_op jit(solution)/shard_map/pallas_call | solution.py:418
  57.5 0.2 collective-permute-start.15
  57.7 0.0 collective-permute-done.14.other_ref
  57.7 0.9 %shard_map.44 = (f32[512,256]{1,0:T(8,128)S(1)}, f32[2048,256]{1,0:T(8,128)S(1)}, f32[128,256]{1,0:T(8,128)S(1)}, f32[8,256]{1,0:T(8,128)S(1)}) custom-call(bf16[2048,1024]{1,0:T(8,128)(2,1)S(1)} %get-tuple-element.61.rows_ref, f32[1024,256]{1,0:T(8,128)S(1)} %get-tuple-element.64.x_ref, bf16[2,128,1024]{2,1,0:T(8,128)(2,1)S(1)} %get-tuple-element.65.turned_ref, ...), custom_call_target="tpu_custom_call" | custom-call | tf_op jit(solution)/shard_map/pallas_call | solution.py:418
  58.7 0.8 %collective-permute-done.15.other_ref = f32[512,256]{1,0:T(8,128)S(1)} collective-permute-done((f32[512,256]{1,0:T(8,128)S(1)}, f32[512,256]{1,0:T(8,128)S(1)}, u32[]{:S(2)}, u32[]{:S(2)}) %collective-permute-start.15) | collective-permute-done | bytes 524320 | tf_op jit(solution)/shard_map/ppermute | solution.py:67
  59.5 1.1 %shard_map.46 = (f32[512,256]{1,0:T(8,128)S(1)}, f32[8,128]{1,0:T(8,128)S(1)}) custom-call(bf16[2048,1024]{1,0:T(8,128)(2,1)S(1)} %get-tuple-element.61.rows_ref, f32[1024,256]{1,0:T(8,128)S(1)} %get-tuple-element.64.x_ref, bf16[2,128,1024]{2,1,0:T(8,128)(2,1)S(1)} %get-tuple-element.65.turned_ref, f32[256,256]{1,0:T(8,128)S(1)} %get-tuple-element.66.kernel_ref, ...), custom_call_target="tpu_custom_call" | custom-call | tf_op jit(solution)/shard_map/pallas_call | solution.py:418
  60.6 0.2 collective-permute-start.16
  60.7 1.0 %collective-permute-done.16.other_ref = f32[8,128]{1,0:T(8,128)S(1)} collective-permute-done((f32[8,128]{1,0:T(8,128)S(1)}, f32[8,128]{1,0:T(8,128)S(1)}, u32[]{:S(2)}, u32[]{:S(2)}) %collective-permute-start.16) | collective-permute-done | bytes 4128 | tf_op jit(solution)/shard_map/ppermute | solution.py:67
  61.8 2.8 %shard_map.48 = (f32[1024,128]{1,0:T(8,128)S(1)}, f32[2048,128]{1,0:T(8,128)S(1)}, f32[1024,256]{1,0:T(8,128)S(1)}, f32[8,128]{1,0:T(8,128)S(1)}) custom-call(bf16[2048,1024]{1,0:T(8,128)(2,1)S(1)} %get-tuple-element.61.rows_ref, bf16[2048,128]{1,0:T(8,128)(2,1)S(1)} %get-tuple-element.53.hot_ref, f32[1024,256]{1,0:T(8,128)S(1)} %get-tuple-element.64.x_ref, ...), custom_call_target="tpu_custom_call" | custom-call | tf_op jit(solution)/shard_map/pallas_call | solution.py:418
  64.5 0.4 collective-permute-start.17
  65.0 1.1 %shard_map.49 = (f32[256,256]{1,0:T(8,128)S(1)}, f32[1024,256]{1,0:T(8,128)S(1)}, bf16[2,128,1024]{2,1,0:T(8,128)(2,1)S(1)}) custom-call(f32[1024,128]{1,0:T(8,128)S(1)} %get-tuple-element.82.grad_ref, f32[1024,256]{1,0:T(8,128)S(1)} %get-tuple-element.81.x_ref), custom_call_target="tpu_custom_call" | custom-call | tf_op jit(solution)/shard_map/pallas_call | solution.py:418
  66.1 0.6 collective-permute-done.17.other_ref
  66.7 4.6 %shard_map.50 = (f32[1024,256]{1,0:T(8,128)S(1)}, f32[512,256]{1,0:T(8,128)S(1)}, f32[2048,256]{1,0:T(8,128)S(1)}, bf16[2,2048,256]{2,1,0:T(8,128)(2,1)S(1)}, f32[128,256]{1,0:T(8,128)S(1)}) custom-call(bf16[2048,1024]{1,0:T(8,128)(2,1)S(1)} %get-tuple-element.61.rows_ref, f32[2048,128]{1,0:T(8,128)S(1)} %get-tuple-element.80.curve_ref, ...), custom_call_target="tpu_custom_call" | custom-call | tf_op jit(solution)/shard_map/pallas_call | solution.py:418
  71.3 0.2 collective-permute-start.18
  71.5 1.4 %shard_map.52.own_ref = f32[512,256]{1,0:T(8,128)S(1)} custom-call(bf16[2048,1024]{1,0:T(8,128)(2,1)S(1)} %get-tuple-element.61.rows_ref, f32[1024,256]{1,0:T(8,128)S(1)} %get-tuple-element.81.x_ref, f32[256,256]{1,0:T(8,128)S(1)} %get-tuple-element.84.kernel_ref, f32[1024,256]{1,0:T(8,128)S(1)} %get-tuple-element.86.drift_ref, ...), custom_call_target="tpu_custom_call" | custom-call | tf_op jit(solution)/shard_map/pallas_call | solution.py:418
  73.0 0.5 collective-permute-start.19
  73.4 0.0 collective-permute-done.18.other_ref
  73.4 0.9 %shard_map.51 = (f32[512,256]{1,0:T(8,128)S(1)}, f32[2048,256]{1,0:T(8,128)S(1)}, f32[128,256]{1,0:T(8,128)S(1)}, f32[8,256]{1,0:T(8,128)S(1)}) custom-call(bf16[2048,1024]{1,0:T(8,128)(2,1)S(1)} %get-tuple-element.61.rows_ref, f32[1024,256]{1,0:T(8,128)S(1)} %get-tuple-element.81.x_ref, bf16[2,128,1024]{2,1,0:T(8,128)(2,1)S(1)} %get-tuple-element.83.turned_ref, ...), custom_call_target="tpu_custom_call" | custom-call | tf_op jit(solution)/shard_map/pallas_call | solution.py:418
  74.4 0.6 collective-permute-done.19.other_ref
  75.0 1.1 %shard_map.53 = (f32[512,256]{1,0:T(8,128)S(1)}, f32[8,128]{1,0:T(8,128)S(1)}) custom-call(bf16[2048,1024]{1,0:T(8,128)(2,1)S(1)} %get-tuple-element.61.rows_ref, f32[1024,256]{1,0:T(8,128)S(1)} %get-tuple-element.81.x_ref, bf16[2,128,1024]{2,1,0:T(8,128)(2,1)S(1)} %get-tuple-element.83.turned_ref, f32[256,256]{1,0:T(8,128)S(1)} %get-tuple-element.84.kernel_ref, ...), custom_call_target="tpu_custom_call" | custom-call | tf_op jit(solution)/shard_map/pallas_call | solution.py:418
  76.1 0.4 collective-permute-start.20
  76.5 0.1 shard_map.47.before_ref
  76.6 0.1 shard_map.54.own_ref
  76.8 0.5 collective-permute-done.20.other_ref
  77.3 0.7 shard_map.55
  (4 shorter events, 0.1 us)
Async XLA Ops:
  22.6 4.6 %collective-permute-start = (bf16[8,48,256]{2,1,0:T(8,128)(2,1)S(1)}, bf16[8,48,256]{2,1,0:T(8,128)(2,1)S(1)}, u32[]{:S(2)}, u32[]{:S(2)}) collective-permute-start(bf16[8,48,256]{2,1,0:T(8,128)(2,1)S(1)} %get-tuple-element.99), channel_id=1, source_target_pairs={{0,24},{1,25},{2,26},{3,27},{4,12},{5,13},{6,14},{7,15},{8,16},{9,... | collective-permute-start | bytes 589832 | tf_op jit(solution)/shard_map/ppermute | solution.py:77
  22.7 4.7 %collective-permute-start.3 = (bf16[8,48,256]{2,1,0:T(8,128)(2,1)S(1)}, bf16[8,48,256]{2,1,0:T(8,128)(2,1)S(1)}, u32[]{:S(2)}, u32[]{:S(2)}) collective-permute-start(bf16[8,48,256]{2,1,0:T(8,128)(2,1)S(1)} %get-tuple-element.98), channel_id=1, source_target_pairs={{0,96},{1,97},{2,98},{3,99},{4,36},{5,37},{6,38},{7,39},{8,104},{9... | collective-permute-start | bytes 589832 | tf_op jit(solution)/shard_map/ppermute | solution.py:77
  22.8 6.1 %collective-permute-start.6 = (bf16[8,48,256]{2,1,0:T(8,128)(2,1)S(1)}, bf16[8,48,256]{2,1,0:T(8,128)(2,1)S(1)}, u32[]{:S(2)}, u32[]{:S(2)}) collective-permute-start(bf16[8,48,256]{2,1,0:T(8,128)(2,1)S(1)} %get-tuple-element.97), channel_id=1, source_target_pairs={{0,3},{1,2},{2,1},{3,0},{4,5},{5,4},{6,7},{7,6},{8,11},{9,10},{10,... | collective-permute-start | bytes 589832 | tf_op jit(solution)/shard_map/ppermute | solution.py:77
  27.3 7.0 %collective-permute-start.2 = (bf16[16,48,256]{2,1,0:T(8,128)(2,1)S(1)}, bf16[16,48,256]{2,1,0:T(8,128)(2,1)S(1)}, u32[]{:S(2)}, u32[]{:S(2)}) collective-permute-start(bf16[16,48,256]{2,1,0:T(8,128)(2,1)S(1)} %pad_maximum_fusion.refs_0_), channel_id=1, source_target_pairs={{0,3},{1,2},{2,1},{3,0},{4,5},{5,4},{6,7},{7,6},{8,11},{9,10},{10,... | collective-permute-start | bytes 1179656 | tf_op jit(solution)/shard_map/ppermute | solution.py:77
  27.4 7.0 %collective-permute-start.1 = (bf16[16,48,256]{2,1,0:T(8,128)(2,1)S(1)}, bf16[16,48,256]{2,1,0:T(8,128)(2,1)S(1)}, u32[]{:S(2)}, u32[]{:S(2)}) collective-permute-start(bf16[16,48,256]{2,1,0:T(8,128)(2,1)S(1)} %pad_maximum_fusion.refs_0_), channel_id=1, source_target_pairs={{0,96},{1,97},{2,98},{3,99},{4,36},{5,37},{6,38},{7,39},{8,104},{9... | collective-permute-start | bytes 1179656 | tf_op jit(solution)/shard_map/ppermute | solution.py:77
  27.5 11.0 %collective-permute-start.4 = (bf16[16,48,256]{2,1,0:T(8,128)(2,1)S(1)}, bf16[16,48,256]{2,1,0:T(8,128)(2,1)S(1)}, u32[]{:S(2)}, u32[]{:S(2)}) collective-permute-start(bf16[16,48,256]{2,1,0:T(8,128)(2,1)S(1)} %pad_maximum_fusion.1.refs_3_), channel_id=1, source_target_pairs={{0,3},{1,2},{2,1},{3,0},{4,5},{5,4},{6,7},{7,6},{8,11},{9,10},{10,... | collective-permute-start | bytes 1179656 | tf_op jit(solution)/shard_map/ppermute | solution.py:77
  29.0 9.5 %collective-permute-start.7 = (bf16[16,48,256]{2,1,0:T(8,128)(2,1)S(1)}, bf16[16,48,256]{2,1,0:T(8,128)(2,1)S(1)}, u32[]{:S(2)}, u32[]{:S(2)}) collective-permute-start(bf16[16,48,256]{2,1,0:T(8,128)(2,1)S(1)} %pad_maximum_fusion.2.refs_6_), channel_id=1, source_target_pairs={{0,24},{1,25},{2,26},{3,27},{4,12},{5,13},{6,14},{7,15},{8,16},{9,... | collective-permute-start | bytes 1179656 | tf_op jit(solution)/shard_map/ppermute | solution.py:77
  29.2 10.9 %collective-permute-start.5 = (bf16[16,48,256]{2,1,0:T(8,128)(2,1)S(1)}, bf16[16,48,256]{2,1,0:T(8,128)(2,1)S(1)}, u32[]{:S(2)}, u32[]{:S(2)}) collective-permute-start(bf16[16,48,256]{2,1,0:T(8,128)(2,1)S(1)} %pad_maximum_fusion.1.refs_3_), channel_id=1, source_target_pairs={{0,24},{1,25},{2,26},{3,27},{4,12},{5,13},{6,14},{7,15},{8,16},{9,... | collective-permute-start | bytes 1179656 | tf_op jit(solution)/shard_map/ppermute | solution.py:77
  34.3 6.9 %collective-permute-start.8 = (bf16[16,48,256]{2,1,0:T(8,128)(2,1)S(1)}, bf16[16,48,256]{2,1,0:T(8,128)(2,1)S(1)}, u32[]{:S(2)}, u32[]{:S(2)}) collective-permute-start(bf16[16,48,256]{2,1,0:T(8,128)(2,1)S(1)} %pad_maximum_fusion.2.refs_6_), channel_id=1, source_target_pairs={{0,96},{1,97},{2,98},{3,99},{4,36},{5,37},{6,38},{7,39},{8,104},{9... | collective-permute-start | bytes 1179656 | tf_op jit(solution)/shard_map/ppermute | solution.py:77
  34.4 8.3 %collective-permute-start.9 = (bf16[16,48,256]{2,1,0:T(8,128)(2,1)S(1)}, bf16[16,48,256]{2,1,0:T(8,128)(2,1)S(1)}, u32[]{:S(2)}, u32[]{:S(2)}) collective-permute-start(bf16[16,48,256]{2,1,0:T(8,128)(2,1)S(1)} %collective-permute-done.1.refs_1_), channel_id=1, source_target_pairs={{0,3},{1,2},{2,1},{3,0},{4,5},{5,4},{6,7},{7,6},{8,11},{9,10},{10,... | collective-permute-start | bytes 1179656 | tf_op jit(solution)/shard_map/ppermute | solution.py:77
  38.5 6.9 %collective-permute-start.10 = (bf16[16,48,256]{2,1,0:T(8,128)(2,1)S(1)}, bf16[16,48,256]{2,1,0:T(8,128)(2,1)S(1)}, u32[]{:S(2)}, u32[]{:S(2)}) collective-permute-start(bf16[16,48,256]{2,1,0:T(8,128)(2,1)S(1)} %collective-permute-done.4.refs_4_), channel_id=1, source_target_pairs={{0,24},{1,25},{2,26},{3,27},{4,12},{5,13},{6,14},{7,15},{8,16},{9,... | collective-permute-start | bytes 1179656 | tf_op jit(solution)/shard_map/ppermute | solution.py:77
  38.5 8.2 %collective-permute-start.11 = (bf16[16,48,256]{2,1,0:T(8,128)(2,1)S(1)}, bf16[16,48,256]{2,1,0:T(8,128)(2,1)S(1)}, u32[]{:S(2)}, u32[]{:S(2)}) collective-permute-start(bf16[16,48,256]{2,1,0:T(8,128)(2,1)S(1)} %collective-permute-done.7.refs_7_), channel_id=1, source_target_pairs={{0,96},{1,97},{2,98},{3,99},{4,36},{5,37},{6,38},{7,39},{8,104},{9... | collective-permute-start | bytes 1179656 | tf_op jit(solution)/shard_map/ppermute | solution.py:77
  43.8 5.7 %collective-permute-start.12 = (f32[1024,128]{1,0:T(8,128)S(1)}, f32[1024,128]{1,0:T(8,128)S(1)}, u32[]{:S(2)}, u32[]{:S(2)}) collective-permute-start(f32[1024,128]{1,0:T(8,128)S(1)} %get-tuple-element.57.x_ref.own_ref), channel_id=1, source_target_pairs={{0,4},{4,0},{1,5},{5,1},{2,6},{6,2},{3,7},{7,3},{8,12},{12,8},{9,1... | collective-permute-start | bytes 1572872 | tf_op jit(solution)/shard_map/ppermute | solution.py:67
  48.0 3.0 %collective-permute-start.13 = (f32[1024,128]{1,0:T(8,128)S(1)}, f32[1024,128]{1,0:T(8,128)S(1)}, u32[]{:S(2)}, u32[]{:S(2)}) collective-permute-start(f32[1024,128]{1,0:T(8,128)S(1)} %get-tuple-element.63.grad_ref), channel_id=1, source_target_pairs={{0,4},{4,0},{1,5},{5,1},{2,6},{6,2},{3,7},{7,3},{8,12},{12,8},{9,1... | collective-permute-start | bytes 1572872 | tf_op jit(solution)/shard_map/ppermute | solution.py:67
  55.7 2.1 %collective-permute-start.14 = (f32[512,256]{1,0:T(8,128)S(1)}, f32[512,256]{1,0:T(8,128)S(1)}, u32[]{:S(2)}, u32[]{:S(2)}) collective-permute-start(f32[512,256]{1,0:T(8,128)S(1)} %get-tuple-element.69.own_ref), channel_id=1, source_target_pairs={{0,4},{4,0},{1,5},{5,1},{2,6},{6,2},{3,7},{7,3},{8,12},{12,8},{9,1... | collective-permute-start | bytes 1572872 | tf_op jit(solution)/shard_map/ppermute | solution.py:67
  57.5 2.0 %collective-permute-start.15 = (f32[512,256]{1,0:T(8,128)S(1)}, f32[512,256]{1,0:T(8,128)S(1)}, u32[]{:S(2)}, u32[]{:S(2)}) collective-permute-start(f32[512,256]{1,0:T(8,128)S(1)} %shard_map.45.own_ref), channel_id=1, source_target_pairs={{0,4},{4,0},{1,5},{5,1},{2,6},{6,2},{3,7},{7,3},{8,12},{12,8},{9,1... | collective-permute-start | bytes 1572872 | tf_op jit(solution)/shard_map/ppermute | solution.py:67
  60.6 1.2 %collective-permute-start.16 = (f32[8,128]{1,0:T(8,128)S(1)}, f32[8,128]{1,0:T(8,128)S(1)}, u32[]{:S(2)}, u32[]{:S(2)}) collective-permute-start(f32[8,128]{1,0:T(8,128)S(1)} %get-tuple-element.78.own_ref), channel_id=1, source_target_pairs={{0,4},{4,0},{1,5},{5,1},{2,6},{6,2},{3,7},{7,3},{8,12},{12,8},{9,1... | collective-permute-start | bytes 12296 | tf_op jit(solution)/shard_map/ppermute | solution.py:67
  64.5 2.2 %collective-permute-start.17 = (f32[1024,128]{1,0:T(8,128)S(1)}, f32[1024,128]{1,0:T(8,128)S(1)}, u32[]{:S(2)}, u32[]{:S(2)}) collective-permute-start(f32[1024,128]{1,0:T(8,128)S(1)} %get-tuple-element.82.grad_ref), channel_id=1, source_target_pairs={{0,4},{4,0},{1,5},{5,1},{2,6},{6,2},{3,7},{7,3},{8,12},{12,8},{9,1... | collective-permute-start | bytes 1572872 | tf_op jit(solution)/shard_map/ppermute | solution.py:67
  71.3 2.1 %collective-permute-start.18 = (f32[512,256]{1,0:T(8,128)S(1)}, f32[512,256]{1,0:T(8,128)S(1)}, u32[]{:S(2)}, u32[]{:S(2)}) collective-permute-start(f32[512,256]{1,0:T(8,128)S(1)} %get-tuple-element.87.own_ref), channel_id=1, source_target_pairs={{0,4},{4,0},{1,5},{5,1},{2,6},{6,2},{3,7},{7,3},{8,12},{12,8},{9,1... | collective-permute-start | bytes 1572872 | tf_op jit(solution)/shard_map/ppermute | solution.py:67
  73.0 2.0 %collective-permute-start.19 = (f32[512,256]{1,0:T(8,128)S(1)}, f32[512,256]{1,0:T(8,128)S(1)}, u32[]{:S(2)}, u32[]{:S(2)}) collective-permute-start(f32[512,256]{1,0:T(8,128)S(1)} %shard_map.52.own_ref), channel_id=1, source_target_pairs={{0,4},{4,0},{1,5},{5,1},{2,6},{6,2},{3,7},{7,3},{8,12},{12,8},{9,1... | collective-permute-start | bytes 1572872 | tf_op jit(solution)/shard_map/ppermute | solution.py:67
  76.1 1.2 %collective-permute-start.20 = (f32[8,128]{1,0:T(8,128)S(1)}, f32[8,128]{1,0:T(8,128)S(1)}, u32[]{:S(2)}, u32[]{:S(2)}) collective-permute-start(f32[8,128]{1,0:T(8,128)S(1)} %get-tuple-element.96.sums_ref), channel_id=1, source_target_pairs={{0,4},{4,0},{1,5},{5,1},{2,6},{6,2},{3,7},{7,3},{8,12},{12,8},{9,1... | collective-permute-start | bytes 12296 | tf_op jit(solution)/shard_map/ppermute | solution.py:67
